TPU v7x, 32 devices: a whole 2x2x4 slice. The times are simulated.
32 devices in a mesh: tok: 8 (over z, x), feat: 4 (over y, core).
Axes of the slice: x: 2, y: 2, z: 4, core: 2. Of those that a mesh axis runs over, the one named last changes fastest.
Arguments:
- queries: bfloat16 [1024, 4096], P('tok', 'feat'), may hold values from -12 to 12
- keys: bfloat16 [1024, 1024], P('tok', 'feat'), may hold values from -12 to 12
- values: bfloat16 [1024, 1024], P('tok', 'feat'), may hold values from -6 to 6
- out_weight: bfloat16 [4096, 4096], P('feat', 'tok'), may hold values from -0.09375 to 0.09375
- doc_lengths: int32 [6], replicated, may hold values from 1 to 640, 1024 in all
Outputs:
- mixed: bfloat16 [1024, 4096], P('tok', 'feat')
Inputs may be any that keep to these rules, and one draw needn't show every extreme that they name: `doc_lengths`: the lengths sum to 1024, and the largest is exactly 640.
All inputs are finite; a program needn't handle non-finite values.
Results may differ from a plain program's by a relative error of at most 0.012.
The roundings to bfloat16 on the way count: a program that leaves them out, or rounds other values in their place, can miss the bound.
Values may be sent and summed in bfloat16 or wider, within the bound.
No kernel may reach another device: no remote copies, remote signals or barrier semaphores. Data moves between devices by JAX's collectives and lax.ppermute only.
A program may use at most 64 MiB of HBM per device.

v0:
```python
import jax
import jax.numpy as jnp
from jax import lax
from jax.sharding import PartitionSpec as P

HD = 128


ROPE_BASE = 500000.0
NEG_FILL = -1e30


def locate(token_index, doc_lengths):
    doc_ends = jnp.cumsum(doc_lengths)
    starts = doc_ends - doc_lengths
    doc_ids = jnp.sum((token_index[:, None] >= doc_ends[None, :]).astype(jnp.int32), axis=1)
    number = jnp.arange(doc_lengths.shape[0], dtype=jnp.int32)
    first_token = jnp.sum(
        jnp.where(doc_ids[:, None] == number[None, :], starts[None, :], 0), axis=1
    )
    return (doc_ids, token_index - first_token)


def rotary(tensor, positions):
    half_size = tensor.shape[-1] // 2
    frequency = ROPE_BASE ** (-(jnp.arange(half_size, dtype=jnp.float32) * 2.0 / tensor.shape[-1]))
    angles = positions.astype(jnp.float32)[:, None] * frequency[None, :]
    cosine = jnp.cos(angles)[:, None, :]
    sine_part = jnp.sin(angles)[:, None, :]
    first_half = tensor[..., :half_size]
    second_half = tensor[..., half_size:]
    return jnp.concatenate(
        [
            first_half * cosine - second_half * sine_part,
            second_half * cosine + first_half * sine_part,
        ],
        axis=-1,
    )


def pick_block(extent):
    for candidate in (512, 256, 128):
        return candidate
    return extent


def shards(queries, keys, values, out_weight, doc_lengths):
    my_index = lax.axis_index("tok")
    local_rows = queries.shape[0]
    local_heads = queries.shape[1] // HD
    kv_local = keys.shape[1] // HD
    group_size = local_heads // kv_local
    scale_factor = HD ** (-0.5)
    own_index = my_index * local_rows + jnp.arange(local_rows, dtype=jnp.int32)
    own_docs, own_positions = locate(own_index, doc_lengths)
    rotated_q = rotary(
        queries.astype(jnp.float32).reshape(local_rows, local_heads, HD), own_positions
    ).astype(jnp.bfloat16)
    rotated_k = rotary(
        keys.astype(jnp.float32).reshape(local_rows, kv_local, HD), own_positions
    ).astype(jnp.bfloat16)
    rotated_k = rotated_k.reshape(local_rows, kv_local * HD)

    def fresh(query_rows):
        running_max = jnp.full((kv_local, group_size, query_rows), NEG_FILL, jnp.float32)
        totals = jnp.zeros((kv_local, group_size, query_rows), jnp.float32)
        weighted = jnp.zeros((kv_local, group_size, query_rows, HD), jnp.float32)
        return (running_max, totals, weighted)

    def absorb(carry_state, query_block, query_index, key_piece, value_piece, offset):
        query_docs, query_positions = locate(query_index, doc_lengths)
        doc_begin = query_index[0] - query_positions[0]
        last_index = query_index[-1]
        extent = key_piece.shape[0]
        needed = (offset + extent > doc_begin) & (offset <= last_index)
        block_rows = pick_block(extent)

        def sweep_keys(state_in):

            def one_block(block_number, state_now):
                running_max, totals, weighted = state_now
                first_key = block_number * block_rows
                key_tile = lax.dynamic_slice_in_dim(key_piece, first_key, block_rows, 0).reshape(
                    block_rows, kv_local, HD
                )
                value_tile = lax.dynamic_slice_in_dim(
                    value_piece, first_key, block_rows, 0
                ).reshape(block_rows, kv_local, HD)
                key_index = first_key + jnp.arange(block_rows, dtype=jnp.int32)
                key_docs, key_positions = locate(key_index, doc_lengths)
                scores = (
                    jnp.einsum(
                        "qgjd,kgd->gjqk", query_block, key_tile, preferred_element_type=jnp.float32
                    )
                    * scale_factor
                )
                visible = (query_docs[:, None] == key_docs[None, :]) & (
                    key_index[None, :] <= query_index[:, None]
                )
                scores = jnp.where(visible, scores, NEG_FILL)
                new_max = jnp.maximum(running_max, jnp.max(scores, axis=-1))
                factor = jnp.exp(running_max - new_max)
                weights = jnp.where(visible, jnp.exp(scores - new_max[..., None]), 0.0)
                totals = totals * factor + jnp.sum(weights, axis=-1)
                update = jnp.einsum(
                    "gjqk,kgd->gjqd",
                    weights.astype(jnp.bfloat16),
                    value_tile,
                    preferred_element_type=jnp.float32,
                )
                weighted = weighted * factor[..., None] + update
                return (new_max, totals, weighted)

            return lax.fori_loop(0, extent // block_rows, one_block, state_in)

        return lax.cond(needed, sweep_keys, lambda state_in: state_in, carry_state)

    def finish(carry_state):
        running_max, totals, weighted = carry_state
        output = weighted / totals[..., None]
        query_rows = output.shape[2]
        return (
            output.transpose(2, 0, 1, 3).reshape(query_rows, local_heads * HD).astype(jnp.bfloat16)
        )

    groups = [(rotated_q, own_index)]
    query_sets = [
        (member[0].reshape(member[0].shape[0], kv_local, group_size, HD), member[1])
        for member in groups
    ]

    def fold_keys(states, pieces, offset):
        return tuple(
            (
                absorb(state_now, member[0], member[1], pieces[0], pieces[1], offset)
                for state_now, member in zip(states, query_sets)
            )
        )

    initial = tuple((fresh(member[0].shape[0]) for member in query_sets))
    states = fold_keys(
        initial,
        (
            lax.all_gather(rotated_k, "tok", axis=0, tiled=True),
            lax.all_gather(values, "tok", axis=0, tiled=True),
        ),
        jnp.int32(0),
    )
    results = [finish(state_now) for state_now in states]
    attended = results[0]
    partial_terms = jnp.dot(
        attended,
        lax.all_gather(out_weight, "tok", axis=1, tiled=True),
        preferred_element_type=jnp.float32,
    )
    return lax.psum_scatter(
        partial_terms.astype(jnp.bfloat16), "feat", scatter_dimension=1, tiled=True
    )


def solution(mesh):
    in_specs = (P("tok", "feat"), P("tok", "feat"), P("tok", "feat"), P("feat", "tok"), P())
    out_specs = P("tok", "feat")
    return jax.shard_map(shards, mesh=mesh, in_specs=in_specs, out_specs=out_specs, check_vma=False)
```

profile of v0, /device:TPU:1, one launch (start us, length us, event | category | flops | bytes accessed | tf_op | source)
XLA Modules:
  0.0 189.5 jit_solution(9263879160086370022)
XLA Ops:
  6.5 0.7 all-gather.2.cloned.1.call-update
  7.3 0.8 reduce-window.9
  8.2 0.7 bitcast_subtract_fusion
  9.0 0.2 multiply_cosine_fusion
  9.4 1.0 convert_bitcast_fusion
  10.8 0.6 fusion.16
  12.6 0.2 fusion.15
  12.8 0.2 subtract_convert_fusion
  13.2 29.0 %all_gather.9 = bf16[1024,256]{0,1:T(8,128)(2,1)S(1)} all-gather(bf16[128,256]{0,1:T(8,128)(2,1)S(1)} %bitcast.68), channel_id=1, replica_groups=mesh['tok'=8,'feat'=4] {'tok'}, dimensions={0}, use_global_device_ids=true | all-gather | bytes 589824 | tf_op jit(solution)/shard_map/all_gather | solution.py:144
  42.2 31.9 %all_gather.10 = bf16[1024,256]{0,1:T(8,128)(2,1)} all-gather(bf16[128,256]{0,1:T(8,128)(2,1)S(1)} %copy.40), channel_id=1, replica_groups=mesh['tok'=8,'feat'=4] {'tok'}, dimensions={0}, use_global_device_ids=true | all-gather | bytes 589824 | tf_op jit(solution)/shard_map/all_gather | solution.py:145
  74.2 12.6 %conditional.1 = (f32[2,4,128]{2,1,0:T(4,128)}, f32[2,4,128,128]{2,3,1,0:T(8,128)}) conditional(s32[]{:T(128)} %bitcast.3, () %tuple.34, (s32[6]{0:T(128)S(1)}, s32[128]{0:T(128)S(1)}, s32[128]{0:T(128)S(1)}, bf16[1024,256]{0,1:T(8,128)(2,1)S(1)}, bf16[128,2,4,128]{3,0,2,1:T(8,128)(2,1)S(1)}, /*index=5*/bf16[1024,256]{0,1:T(8,128)(2,1)}) %tuple.74), branch_computations={%region_3.4_spmd, %region_4.11_spmd} | conditional | flops 275855392 | bytes 14757331 | solution.py:116
  74.2 0.2 broadcast_in_dim.105
  74.4 10.4 %while.19 = (s32[]{:T(128)}, f32[2,4,128]{2,1,0:T(4,128)S(1)}, f32[2,4,128]{2,1,0:T(4,128)}, f32[2,4,128,128]{3,2,1,0:T(8,128)}, s32[128]{0:T(128)S(1)}, /*index...) while((s32[]{:T(128)}, f32[2,4,128]{2,1,0:T(4,128)S(1)}, ...), condition=%wide.region_10.10_spmd.clone, body=%wide.region_6.9_spmd.clone.sunk | while | flops 275855360 | bytes 13708567 | solution.py:114
  74.4 1.0 constant_dynamic-slice_fusion.3
  75.5 0.2 compare_and_fusion.2
  75.7 0.5 fusion.33
  76.2 0.5 fusion.34
  76.8 0.6 fusion.35
  77.4 0.9 convolution_add_fusion.2
  78.3 0.9 copy-done.1
  79.2 1.0 constant_dynamic-slice_fusion.3
  80.3 0.2 compare_and_fusion.2
  80.5 0.5 fusion.33
  81.1 0.5 fusion.34
  81.6 1.3 fusion.35
  82.9 0.9 convolution_add_fusion.2
  83.9 0.9 copy-done.1
  84.7 2.1 %copy.50 = f32[2,4,128,128]{2,3,1,0:T(8,128)} copy(f32[2,4,128,128]{3,2,1,0:T(8,128)} %get-tuple-element.256) | data formatting | bytes 1048576 | tf_op jit(solution)/shard_map/cond | solution.py:116
  86.8 1.1 divide_convert_fusion
  87.9 65.3 %all-gather.2.cloned.1.call-done = bf16[1024,4096]{1,0:T(8,128)(2,1)} async-done(((bf16[1024,512]{1,0:T(8,128)(2,1)}), bf16[1024,4096]{1,0:T(8,128)(2,1)}) %all-gather.2.cloned.1.call-update) | async-done | bytes 8388624 | tf_op jit(solution)/shard_map/all_gather | solution.py:153
  153.2 5.7 %convolution_convert_fusion = bf16[128,4096]{1,0:T(8,128)(2,1)} fusion(bf16[128,1024]{0,1:T(8,128)(2,1)S(1)} %bitcast.64, bf16[1024,4096]{1,0:T(8,128)(2,1)} %all-gather.2.cloned.1.call-done), kind=kOutput, calls=%fused_computation.23 | convolution fusion | flops 1074266112 | bytes 9699328 | tf_op jit(solution)/shard_map/dot_general | solution.py:151
  158.9 23.7 %reduce-scatter.2.cloned.1.call-done = bf16[128,1024]{1,0:T(8,128)(2,1)} async-done(((bf16[128,4096]{1,0:T(8,128)(2,1)}), bf16[128,1024]{1,0:T(8,128)(2,1)}) %reduce-scatter.2.cloned.1.call-update) | async-done | bytes 262160 | tf_op jit(solution)/shard_map/reduce_scatter | solution.py:156
  (39 shorter events, 1.1 us)
Async XLA Ops:
  6.5 4.0 %copy-start.2 = (bf16[128,256]{1,0:T(8,128)(2,1)S(1)}, bf16[128,256]{1,0:T(8,128)(2,1)}, u32[]{:S(2)}) copy-start(bf16[128,256]{1,0:T(8,128)(2,1)} %param.10) | copy-start | bytes 196612
  6.5 4.1 %copy-start.3 = (bf16[128,256]{1,0:T(8,128)(2,1)S(1)}, bf16[128,256]{1,0:T(8,128)(2,1)}, u32[]{:S(2)}) copy-start(bf16[128,256]{1,0:T(8,128)(2,1)} %param.11) | copy-start | bytes 196612
  6.5 146.6 %all-gather.2.cloned.1.call-start = ((), (), s32[]{:S(2)}) async-start(), calls=%async_computation.1 | async-start | bytes 9437184 | tf_op jit(solution)/shard_map/all_gather | solution.py:153
  7.3 175.4 %reduce-scatter.2.cloned.1.call-start = ((), (), s32[]{:S(2)}) async-start(), calls=%async_computation.2 | async-start | bytes 1310720 | tf_op jit(solution)/shard_map/reduce_scatter | solution.py:156
  12.8 61.4 %copy-start.4 = (s32[6]{0:T(128)S(1)}, s32[6]{0:T(128)}, u32[]{:S(2)}) copy-start(s32[6]{0:T(128)} %param.13) | copy-start | bytes 76
  76.2 1.2 copy-start
  78.3 0.9 copy-start.1
  81.1 1.9 copy-start
  83.9 0.9 copy-start.1
Sparse Core Ops, SparseCore 0:
  9.4 143.7 all-gather.1
  159.1 23.5 reduce-scatter.1
where the time goes:
time: 191 us; the launch traced here: 190 us
  waiting for transfers between devices  89.7 us (47%)
  blocking collectives  61 us (32%)
  between operations  14.8 us (8%)
  matrix products  8.69 us (5%)
  other arithmetic  8.12 us (4%)
  local copies, waits for them, and re-layouts  7.07 us (4%)
    all_gather x1, waiting for transfers between devices, shards(): lax.all_gather(out_weight, 'tok', axis=1, tiled=True)  65.3 us
    all_gather x1, blocking collectives, shards(): lax.all_gather(values, 'tok', axis=0, tiled=True)  31.9 us
    all_gather x1, blocking collectives, shards(): lax.all_gather(rotated_k, 'tok', axis=0, tiled=True)  29 us
    reduce_scatter x1, waiting for transfers between devices, shards(): lax.psum_scatter(partial_terms.astype(jnp.bfloat16), 'feat', scatter_dime...  23.7 us
    dot_general x1, matrix products, shards(): jnp.dot(attended, lax.all_gather(out_weight, 'tok', axis=1, tiled=True),...  5.73 us
  transfers between devices with their start and end apart: 2, of which 2 were waited for; matrix products, arithmetic and copies ran while one was open for 9% of the time, Pallas kernels for 0%

commit v1 on v0

v1 whole, which is shorter than its diff:
```python
import math
from functools import partial

import jax
import jax.numpy as jnp
from jax import lax
from jax.experimental import pallas as pl
from jax.experimental.pallas import tpu as pltpu
from jax.sharding import PartitionSpec as P

HD = 128
ROPE_BASE = 500000.0
NEG_FILL = -1e30
LONGEST = (5, 8)
FAR_BLOCKS = 7


def locate(token_index, doc_lengths):
    doc_ends = jnp.cumsum(doc_lengths)
    starts = doc_ends - doc_lengths
    doc_ids = jnp.sum((token_index[:, None] >= doc_ends[None, :]).astype(jnp.int32), axis=1)
    number = jnp.arange(doc_lengths.shape[0], dtype=jnp.int32)
    first_token = jnp.sum(
        jnp.where(doc_ids[:, None] == number[None, :], starts[None, :], 0), axis=1
    )
    return (doc_ids, token_index - first_token)


def tables(positions):
    half = HD // 2
    frequency = ROPE_BASE ** (-(jnp.arange(half, dtype=jnp.float32) * 2.0 / HD))
    angles = positions.astype(jnp.float32)[:, None] * frequency[None, :]
    cosine, sine = jnp.cos(angles), jnp.sin(angles)
    return (
        jnp.concatenate([cosine, cosine], axis=-1),
        jnp.concatenate([-sine, sine], axis=-1),
    )


def turn(block, cosine, sine):
    block = block.astype(jnp.float32)
    return (block * cosine + pltpu.roll(block, HD // 2, 1) * sine).astype(jnp.bfloat16)


def attention_kernel(first_ref, q_ref, k_ref, v_ref, *refs, reach, group):
    far = refs[:reach]
    cos_ref, sin_ref, start_ref, out_ref = refs[reach:]
    rows = q_ref.shape[0]
    kv_heads = k_ref.shape[1] // HD
    first = first_ref[0]
    scale = HD**-0.5 * math.log2(math.e)
    starts = start_ref[...]
    lane = lax.broadcasted_iota(jnp.int32, (rows, rows), 1)
    sub = lax.broadcasted_iota(jnp.int32, (rows, rows), 0)
    own_cos, own_sin = (r[reach * rows : (reach + 1) * rows, :] for r in (cos_ref, sin_ref))
    seen = []
    for d in range(reach, 0, -1):
        seen.append(first - d * rows + lane >= starts)
    seen.append((first + lane >= starts) & (lane <= sub))
    for g in range(kv_heads):
        at = slice(g * HD, (g + 1) * HD)
        keys, vals = [], []
        for d in range(reach, 0, -1):
            part = slice((reach - d) * rows, (reach - d + 1) * rows)
            keys.append(turn(far[d - 1][:, at], cos_ref[part, :], sin_ref[part, :]))
            vals.append(far[d - 1][:, kv_heads * HD + g * HD : kv_heads * HD + (g + 1) * HD])
        keys.append(turn(k_ref[:, at], own_cos, own_sin))
        vals.append(v_ref[:, at])
        keys = jnp.concatenate(keys, axis=0)
        vals = jnp.concatenate(vals, axis=0)
        for h in range(g * group, (g + 1) * group):
            query = turn(q_ref[:, h * HD : (h + 1) * HD], own_cos, own_sin)
            scores = lax.dot_general(
                query, keys, (((1,), (1,)), ((), ())), preferred_element_type=jnp.float32
            )
            masked = [
                jnp.where(seen[n], scores[:, n * rows : (n + 1) * rows] * scale, NEG_FILL)
                for n in range(reach + 1)
            ]
            top = masked[0]
            for m in masked[1:]:
                top = jnp.maximum(top, m)
            top = jnp.max(top, axis=1, keepdims=True)
            weights = [jnp.exp2(m - top) for m in masked]
            total = weights[0]
            for w in weights[1:]:
                total = total + w
            total = jnp.sum(total, axis=1, keepdims=True)
            rounded = jnp.concatenate([w.astype(jnp.bfloat16) for w in weights], axis=1)
            update = jnp.dot(rounded, vals, preferred_element_type=jnp.float32)
            out_ref[:, h * HD : (h + 1) * HD] = (update / total).astype(jnp.bfloat16)


def attend_near(queries, keys, values, doc_lengths, reach, n_tok):
    rows = queries.shape[0]
    me = lax.axis_index("tok")
    both = jnp.concatenate([keys, values], axis=1)
    far = []
    for d in range(1, reach + 1):
        far.append(lax.ppermute(both, "tok", [(i, i + d) for i in range(n_tok - d)]))
    first = me * rows
    window = first - reach * rows + jnp.arange((reach + 1) * rows, dtype=jnp.int32)
    _, positions = locate(window, doc_lengths)
    cosine, sine = tables(positions)
    starts = (window - positions)[reach * rows :].reshape(rows, 1)
    vmem = pl.BlockSpec(memory_space=pltpu.VMEM)
    attended = pl.pallas_call(
        partial(
            attention_kernel, reach=reach, group=queries.shape[1] // keys.shape[1]
        ),
        out_shape=jax.ShapeDtypeStruct(queries.shape, jnp.bfloat16),
        in_specs=[pl.BlockSpec(memory_space=pltpu.SMEM)] + [vmem] * (6 + reach),
        out_specs=vmem,
        name="attention",
    )(first.reshape(1), queries, keys, values, *far, cosine, sine, starts)
    return attended, far[-1]


def rotary(tensor, positions):
    half_size = tensor.shape[-1] // 2
    frequency = ROPE_BASE ** (-(jnp.arange(half_size, dtype=jnp.float32) * 2.0 / tensor.shape[-1]))
    angles = positions.astype(jnp.float32)[:, None] * frequency[None, :]
    cosine = jnp.cos(angles)[:, None, :]
    sine_part = jnp.sin(angles)[:, None, :]
    a = tensor[..., :half_size]
    b = tensor[..., half_size:]
    return jnp.concatenate([a * cosine - b * sine_part, b * cosine + a * sine_part], axis=-1)


def attend_far(queries, keys, values, doc_lengths):
    rows = queries.shape[0]
    heads, kv_heads = queries.shape[1] // HD, keys.shape[1] // HD
    own = lax.axis_index("tok") * rows + jnp.arange(rows, dtype=jnp.int32)
    docs, positions = locate(own, doc_lengths)
    rotated_q = rotary(queries.astype(jnp.float32).reshape(rows, heads, HD), positions)
    rotated_q = rotated_q.astype(jnp.bfloat16).reshape(rows, kv_heads, heads // kv_heads, HD)
    rotated_k = rotary(keys.astype(jnp.float32).reshape(rows, kv_heads, HD), positions)
    rotated_k = rotated_k.astype(jnp.bfloat16).reshape(rows, kv_heads * HD)
    all_k = lax.all_gather(rotated_k, "tok", axis=0, tiled=True)
    all_v = lax.all_gather(values, "tok", axis=0, tiled=True)
    step = 4 * rows

    def one_block(number, state):
        running, totals, weighted = state
        begin = number * step
        key = lax.dynamic_slice_in_dim(all_k, begin, step, 0).reshape(step, kv_heads, HD)
        value = lax.dynamic_slice_in_dim(all_v, begin, step, 0).reshape(step, kv_heads, HD)
        index = begin + jnp.arange(step, dtype=jnp.int32)
        key_docs, _ = locate(index, doc_lengths)
        scores = HD**-0.5 * jnp.einsum(
            "qgjd,kgd->gjqk", rotated_q, key, preferred_element_type=jnp.float32
        )
        visible = (docs[:, None] == key_docs[None, :]) & (index[None, :] <= own[:, None])
        scores = jnp.where(visible, scores, NEG_FILL)
        top = jnp.maximum(running, jnp.max(scores, axis=-1))
        factor = jnp.exp(running - top)
        weights = jnp.where(visible, jnp.exp(scores - top[..., None]), 0.0)
        totals = totals * factor + jnp.sum(weights, axis=-1)
        update = jnp.einsum(
            "gjqk,kgd->gjqd",
            weights.astype(jnp.bfloat16),
            value,
            preferred_element_type=jnp.float32,
        )
        return (top, totals, weighted * factor[..., None] + update)

    shape = (kv_heads, heads // kv_heads, rows)
    state = (
        jnp.full(shape, NEG_FILL, jnp.float32),
        jnp.zeros(shape, jnp.float32),
        jnp.zeros(shape + (HD,), jnp.float32),
    )
    _, totals, weighted = lax.fori_loop(0, all_k.shape[0] // step, one_block, state)
    output = (weighted / totals[..., None]).transpose(2, 0, 1, 3)
    return output.reshape(rows, heads * HD).astype(jnp.bfloat16), all_v[:rows]


def project_kernel(place_ref, *refs, count, sides):
    blocks, weights, (keep_ref, send_ref) = refs[:count], refs[count:-2], refs[-2:]
    width = weights[0].shape[1]
    for r in range(count):
        pieces = [
            jnp.dot(blocks[r][...], w[...], preferred_element_type=jnp.float32).astype(jnp.bfloat16)
            for w in weights
        ]
        slot = r ^ place_ref[1]
        turn_now = slot & 1
        for n, piece in enumerate(pieces):
            begin = pl.multiple_of((place_ref[0] ^ n) * width if sides > 1 else 0, HD)

            @pl.when(slot < count // 2)
            def _():
                keep_ref[turn_now, :, pl.ds(begin, width)] = piece

            @pl.when(slot >= count // 2)
            def _():
                send_ref[turn_now, :, pl.ds(begin, width)] = piece


def solution(mesh):
    n_tok, n_feat = mesh.shape["tok"], mesh.shape["feat"]
    inner = n_tok // n_feat

    def everyone(move):
        pairs = []
        for z in range(n_feat):
            for x in range(inner):
                for j in range(n_feat):
                    to_z, to_x, to_j = move(z, x, j)
                    pairs.append(
                        (
                            (z * inner + x) * n_feat + j,
                            (to_z * inner + to_x) * n_feat + to_j,
                        )
                    )
        return pairs

    def permute(array, move):
        return lax.ppermute(array, ("tok", "feat"), everyone(move))

    def shards(queries, keys, values, out_weight, doc_lengths):
        rows = queries.shape[0]
        me, feat = lax.axis_index("tok"), lax.axis_index("feat")
        z, x = me // inner, me % inner
        longest = n_tok * rows * LONGEST[0] // LONGEST[1]
        reach = min(n_tok - 1, -(-(longest - 1) // rows))
        if reach <= FAR_BLOCKS:
            attended, seen = attend_near(queries, keys, values, doc_lengths, reach, n_tok)
        else:
            attended, seen = attend_far(queries, keys, values, doc_lengths)
        out_weight, _ = lax.optimization_barrier((out_weight, seen))
        if inner == 2:
            weights = [out_weight, permute(out_weight, lambda z, x, j: (z, 1 - x, j))]
        else:
            groups = [[z * inner + x for x in range(inner)] for z in range(n_feat)]
            weights = [
                lax.all_gather(
                    out_weight, "tok", axis=1, tiled=True, axis_index_groups=groups
                )
            ]
        blocks = [attended] + [
            permute(attended, lambda z, x, j, r=r: (z ^ r, x, j)) for r in range(1, n_feat)
        ]
        low, high = feat & 1, feat >> 1
        mask = low * 2 + high
        place = jnp.stack([x, mask]).astype(jnp.int32)
        vmem = pl.BlockSpec(memory_space=pltpu.VMEM)
        half = jax.ShapeDtypeStruct(
            (n_feat // 2, rows, sum(w.shape[1] for w in weights)), jnp.bfloat16
        )
        keep, send = pl.pallas_call(
            partial(project_kernel, count=n_feat, sides=len(weights)),
            out_shape=(half, half),
            in_specs=[pl.BlockSpec(memory_space=pltpu.SMEM)] + [vmem] * (n_feat + len(weights)),
            out_specs=(vmem, vmem),
            name="project",
        )(place, *blocks, *weights)
        other = permute(send, lambda z, x, j: (z, x, j ^ 1))
        both = keep.astype(jnp.float32) + other.astype(jnp.float32)
        both = both.astype(jnp.bfloat16)
        home = [
            permute(
                both[k],
                lambda z, x, j, k=k: (z ^ ((j & 1) * 2 + ((j >> 1) ^ k)), x, z),
            )
            for k in range(2)
        ]
        return (home[0].astype(jnp.float32) + home[1].astype(jnp.float32)).astype(jnp.bfloat16)

    in_specs = (P("tok", "feat"), P("tok", "feat"), P("tok", "feat"), P("feat", "tok"), P())
    return jax.shard_map(
        shards, mesh=mesh, in_specs=in_specs, out_specs=P("tok", "feat"), check_vma=False
    )
```

time: 191 us -> 83.3 us (0.44)
  waiting for transfers between devices: 89.7 us -> 26.6 us
  blocking collectives: 61 us -> 0 us
  starting transfers between devices: 0.04 us -> 36 us
  between operations: 14.8 us -> 0.21 us
  Pallas kernels: 0 us -> 9.73 us
  matrix products: 8.69 us -> 0 us
  other arithmetic: 8.12 us -> 5.58 us
  local copies, waits for them, and re-layouts: 7.07 us -> 4.76 us
    all_gather x1 -> x0, waiting for transfers between devices: 65.3 us -> none  [shards(): lax.all_gather(out_weight, 'tok', axis=1, tiled=True)]
    all_gather x2 -> x0, blocking collectives: 61 us -> none  [the longest x1 31.9 us: shards(): lax.all_gather(values, 'tok', axis=0, tiled=True)]
    ppermute x0 -> x12, starting transfers between devices: none -> 36 us  [the longest x7 21.5 us: permute(): return lax.ppermute(array, ('tok', 'feat'), everyone(move))]
    ppermute x0 -> x12, waiting for transfers between devices: none -> 26.6 us  [the longest x7 26.6 us: permute(): return lax.ppermute(array, ('tok', 'feat'), everyone(move))]
    reduce_scatter x1 -> x0, waiting for transfers between devices: 23.7 us -> none  [shards(): lax.psum_scatter(partial_terms.astype(jnp.bfloat16), 'feat', scatter_dime...]
    pallas_call x0 -> x2, Pallas kernels: none -> 9.73 us  [the longest x1 4.98 us: attend_near(): pl.pallas_call(partial(attention_kernel, reach=reach, group=queries.shape...]
    dot_general x5 -> x0, matrix products: 8.69 us -> none  [the longest x1 5.73 us: shards(): jnp.dot(attended, lax.all_gather(out_weight, 'tok', axis=1, tiled=True),...]
    unnamed x8 -> x23, local copies, waits for them, and re-layouts: 0.22 us -> 3.97 us
  transfers between devices with their start and end apart: 2 -> 12, of which waited for: 2 -> 6; matrix products, arithmetic and copies ran while one was open for 9% -> 5% of each run, Pallas kernels for 0% -> 6%
where the time goes in v1:
time: 83.3 us; the launch traced here: 83 us
  starting transfers between devices  36 us (43%)
  waiting for transfers between devices  26.6 us (32%)
  Pallas kernels  9.73 us (12%)
  other arithmetic  5.58 us (7%)
  local copies, waits for them, and re-layouts  4.76 us (6%)
    ppermute x7, waiting for transfers between devices, permute(): return lax.ppermute(array, ('tok', 'feat'), everyone(move))  26.6 us
    ppermute x7, starting transfers between devices, permute(): return lax.ppermute(array, ('tok', 'feat'), everyone(move))  21.5 us
    ppermute x5, starting transfers between devices, attend_near(): lax.ppermute(both, 'tok', [(i, i + d) for i in range(n_tok - d)])  14.6 us
    pallas_call x1, Pallas kernels, attend_near(): pl.pallas_call(partial(attention_kernel, reach=reach, group=queries.shape...  4.98 us
    pallas_call x1, Pallas kernels, shards(): pl.pallas_call(partial(project_kernel, count=n_feat, sides=len(weights)),...  4.75 us
    unnamed x23, local copies, waits for them, and re-layouts  3.97 us
  transfers between devices with their start and end apart: 12, of which 6 were waited for; matrix products, arithmetic and copies ran while one was open for 5% of the time, Pallas kernels for 6%

profile of v1, /device:TPU:1, one launch (start us, length us, event | category | flops | bytes accessed | tf_op | source)
XLA Modules:
  0.0 83.0 jit_solution(3764484929805904686)
XLA Ops:
  0.0 0.9 %constant_dynamic-update-slice_fusion.1 = bf16[128,512]{1,0:T(8,128)(2,1)S(1)} fusion(bf16[128,256]{1,0:T(8,128)(2,1)} %k_ref.1), kind=kLoop, calls=%fused_computation.13 | loop fusion | bytes 131072
  0.9 6.0 %collective-permute-start.4 = (bf16[128,512]{1,0:T(8,128)(2,1)S(1)}, bf16[128,512]{1,0:T(8,128)(2,1)S(1)}, u32[]{:S(2)}, u32[]{:S(2)}) collective-permute-start(bf16[128,512]{1,0:T(8,128)(2,1)S(1)} %constant_dynamic-update-slice_fusion), channel_id=1, source_target_pairs={{0,20},{4,24},{8,28},{1,21},{5,25},{9,29},{2,22},{6,26},{10,30},{3... | collective-permute-start | bytes 393224 | tf_op jit(solution)/shard_map/ppermute | solution.py:100
  6.9 3.2 %collective-permute-start = (bf16[128,512]{1,0:T(8,128)(2,1)S(1)}, bf16[128,512]{1,0:T(8,128)(2,1)S(1)}, u32[]{:S(2)}, u32[]{:S(2)}) collective-permute-start(bf16[128,512]{1,0:T(8,128)(2,1)S(1)} %constant_dynamic-update-slice_fusion), channel_id=1, source_target_pairs={{0,4},{4,8},{8,12},{12,16},{16,20},{20,24},{24,28},{1,5},{5,9},{9,... | collective-permute-start | bytes 393224 | tf_op jit(solution)/shard_map/ppermute | solution.py:100
  10.1 1.9 %collective-permute-start.1 = (bf16[128,512]{1,0:T(8,128)(2,1)S(1)}, bf16[128,512]{1,0:T(8,128)(2,1)S(1)}, u32[]{:S(2)}, u32[]{:S(2)}) collective-permute-start(bf16[128,512]{1,0:T(8,128)(2,1)S(1)} %constant_dynamic-update-slice_fusion), channel_id=1, source_target_pairs={{0,8},{4,12},{8,16},{12,20},{16,24},{20,28},{1,9},{5,13},{9,17},{1... | collective-permute-start | bytes 393224 | tf_op jit(solution)/shard_map/ppermute | solution.py:100
  12.0 1.5 %collective-permute-start.2 = (bf16[128,512]{1,0:T(8,128)(2,1)S(1)}, bf16[128,512]{1,0:T(8,128)(2,1)S(1)}, u32[]{:S(2)}, u32[]{:S(2)}) collective-permute-start(bf16[128,512]{1,0:T(8,128)(2,1)S(1)} %constant_dynamic-update-slice_fusion), channel_id=1, source_target_pairs={{0,12},{4,16},{8,20},{12,24},{16,28},{1,13},{5,17},{9,21},{13,25},... | collective-permute-start | bytes 393224 | tf_op jit(solution)/shard_map/ppermute | solution.py:100
  13.5 1.9 %collective-permute-start.3 = (bf16[128,512]{1,0:T(8,128)(2,1)S(1)}, bf16[128,512]{1,0:T(8,128)(2,1)S(1)}, u32[]{:S(2)}, u32[]{:S(2)}) collective-permute-start(bf16[128,512]{1,0:T(8,128)(2,1)S(1)} %constant_dynamic-update-slice_fusion), channel_id=1, source_target_pairs={{0,16},{4,20},{8,24},{12,28},{1,17},{5,21},{9,25},{13,29},{2,18},{... | collective-permute-start | bytes 393224 | tf_op jit(solution)/shard_map/ppermute | solution.py:100
  15.5 0.6 copy-done.10
  16.2 0.2 reduce-window.8
  16.4 0.1 convert_reduce_fusion
  16.6 0.6 collective-permute-start.8
  17.2 0.7 copy.7.refs_7_
  17.9 1.5 %fusion = (f32[768,64]{1,0:T(8,128)S(1)}, f32[768,64]{1,0:T(8,128)S(1)}, f32[768,64]{1,0:T(8,128)S(1)}) fusion(f32[64]{0:T(128)S(1)} %negate_power_fusion, f32[768]{0:T(1024)S(1)} %subtract_convert_fusion), kind=kLoop, calls=%fused_computation.8 | loop fusion | flops 98304 | bytes 593152 | tf_op jit(solution)/shard_map/neg | solution.py:36
  19.4 1.2 %pad_maximum_fusion = (f32[768,128]{1,0:T(8,128)}, f32[768,128]{1,0:T(8,128)}) fusion(f32[768,64]{1,0:T(8,128)S(1)} %get-tuple-element.15, f32[768,64]{1,0:T(8,128)S(1)} %get-tuple-element.14, f32[768,64]{1,0:T(8,128)S(1)} %get-tuple-element.13), kind=kLoop, calls=%fused_computation.4 | loop fusion | flops 196608 | bytes 1376256 | tf_op jit(solution)/shard_map/concatenate | solution.py:35
  20.6 0.6 copy-done.6
  21.4 5.0 %attention.1.refs_0_ = bf16[128,1024]{1,0:T(8,128)(2,1)} custom-call(s32[1]{0:T(128)} %bitcast.2.first_ref, bf16[128,1024]{1,0:T(8,128)(2,1)} %q_ref.1, bf16[128,256]{1,0:T(8,128)(2,1)} %k_ref.1, bf16[128,256]{1,0:T(8,128)(2,1)} %v_ref.1, bf16[128,512]{1,0:T(8,128)(2,1)} %copy-done.6, bf16[128,512]{1,0:T(8,128)(2,1)} %copy-done.7, ...), custom_call_target="tpu_custom_call" | custom-call | tf_op jit(solution)/shard_map/attention/pallas_call | solution.py:107
  26.4 4.6 %collective-permute-start.5 = (bf16[128,1024]{1,0:T(8,128)(2,1)}, bf16[128,1024]{1,0:T(8,128)(2,1)S(1)}, u32[]{:S(2)}, u32[]{:S(2)}) collective-permute-start(bf16[128,1024]{1,0:T(8,128)(2,1)} %attention.1.refs_0_), channel_id=1, source_target_pairs={{0,8},{1,9},{2,10},{3,11},{4,12},{5,13},{6,14},{7,15},{8,0},{9,1},... | collective-permute-start | bytes 786440 | tf_op jit(solution)/shard_map/ppermute | solution.py:219
  30.9 3.1 %collective-permute-start.6 = (bf16[128,1024]{1,0:T(8,128)(2,1)}, bf16[128,1024]{1,0:T(8,128)(2,1)S(1)}, u32[]{:S(2)}, u32[]{:S(2)}) collective-permute-start(bf16[128,1024]{1,0:T(8,128)(2,1)} %attention.1.refs_0_), channel_id=1, source_target_pairs={{0,16},{1,17},{2,18},{3,19},{4,20},{5,21},{6,22},{7,23},{8,24},{9,... | collective-permute-start | bytes 786440 | tf_op jit(solution)/shard_map/ppermute | solution.py:219
  34.0 0.6 pad_add_fusion.place_ref
  34.6 7.1 %collective-permute-done.5.refs_1_ = bf16[128,1024]{1,0:T(8,128)(2,1)S(1)} collective-permute-done((bf16[128,1024]{1,0:T(8,128)(2,1)}, bf16[128,1024]{1,0:T(8,128)(2,1)S(1)}, u32[]{:S(2)}, u32[]{:S(2)}) %collective-permute-start.5) | collective-permute-done | bytes 262176 | tf_op jit(solution)/shard_map/ppermute | solution.py:219
  41.7 0.4 collective-permute-done.6.refs_2_
  42.1 8.4 %collective-permute-done.7.refs_3_ = bf16[128,1024]{1,0:T(8,128)(2,1)S(1)} collective-permute-done((bf16[128,1024]{1,0:T(8,128)(2,1)}, bf16[128,1024]{1,0:T(8,128)(2,1)S(1)}, u32[]{:S(2)}, u32[]{:S(2)}) %collective-permute-start.7) | collective-permute-done | bytes 262176 | tf_op jit(solution)/shard_map/ppermute | solution.py:219
  50.5 0.7 copy-done.4
  51.2 1.0 %copy-done = bf16[1024,512]{1,0:T(8,128)(2,1)} copy-done((bf16[1024,512]{1,0:T(8,128)(2,1)}, bf16[1024,512]{1,0:T(8,128)(2,1)S(1)}, u32[]{:S(2)}) %copy-start) | copy-done | bytes 1048600
  52.2 4.8 %project.1 = (bf16[2,128,1024]{2,1,0:T(8,128)(2,1)}, bf16[2,128,1024]{2,1,0:T(8,128)(2,1)}) custom-call(s32[2]{0:T(128)} %pad_add_fusion.place_ref, bf16[128,1024]{1,0:T(8,128)(2,1)} %attention.1.refs_0_, bf16[128,1024]{1,0:T(8,128)(2,1)} %copy-done.2, bf16[128,1024]{1,0:T(8,128)(2,1)} %copy-done.3, bf16[128,1024]{1,0:T(8,128)(2,1)} %copy-done.4, ...), custom_call_target="tpu_custom_call" | custom-call | tf_op jit(solution)/shard_map/project/pallas_call | solution.py:251
  57.0 4.2 %collective-permute-start.9 = (bf16[2,128,1024]{2,1,0:T(8,128)(2,1)}, bf16[2,128,1024]{2,1,0:T(8,128)(2,1)S(1)}, u32[]{:S(2)}, u32[]{:S(2)}) collective-permute-start(bf16[2,128,1024]{2,1,0:T(8,128)(2,1)} %get-tuple-element.10), channel_id=1, source_target_pairs={{0,1},{1,0},{2,3},{3,2},{4,5},{5,4},{6,7},{7,6},{8,9},{9,8},{10,11... | collective-permute-start | bytes 1572872 | tf_op jit(solution)/shard_map/ppermute | solution.py:219
  61.2 1.7 %collective-permute-done.9 = bf16[2,128,1024]{2,1,0:T(8,128)(2,1)S(1)} collective-permute-done((bf16[2,128,1024]{2,1,0:T(8,128)(2,1)}, bf16[2,128,1024]{2,1,0:T(8,128)(2,1)S(1)}, u32[]{:S(2)}, u32[]{:S(2)}) %collective-permute-start.9) | collective-permute-done | bytes 524320 | tf_op jit(solution)/shard_map/ppermute | solution.py:219
  62.9 1.2 %add_convert_fusion = bf16[2,128,1024]{2,1,0:T(8,128)(2,1)S(1)} fusion(bf16[2,128,1024]{2,1,0:T(8,128)(2,1)S(1)} %collective-permute-done.9, bf16[2,128,1024]{2,1,0:T(8,128)(2,1)} %get-tuple-element.9), kind=kLoop, calls=%fused_computation | loop fusion | flops 1048576 | bytes 1572864 | tf_op jit(solution)/shard_map/convert_element_type | solution.py:260
  64.2 7.0 %collective-permute-start.10 = (bf16[128,1024]{1,0:T(8,128)(2,1)S(1)}, bf16[128,1024]{1,0:T(8,128)(2,1)S(1)}, u32[]{:S(2)}, u32[]{:S(2)}) collective-permute-start(bf16[128,1024]{1,0:T(8,128)(2,1)S(1)} %get-tuple-element.11), channel_id=1, source_target_pairs={{0,0},{1,16},{2,8},{3,24},{4,4},{5,20},{6,12},{7,28},{8,9},{9,25},... | collective-permute-start | bytes 786440 | tf_op jit(solution)/shard_map/ppermute | solution.py:219
  71.3 1.9 %collective-permute-start.11 = (bf16[128,1024]{1,0:T(8,128)(2,1)S(1)}, bf16[128,1024]{1,0:T(8,128)(2,1)S(1)}, u32[]{:S(2)}, u32[]{:S(2)}) collective-permute-start(bf16[128,1024]{1,0:T(8,128)(2,1)S(1)} %get-tuple-element.12), channel_id=1, source_target_pairs={{0,8},{1,24},{2,0},{3,16},{4,12},{5,28},{6,4},{7,20},{8,1},{9,17},... | collective-permute-start | bytes 786440 | tf_op jit(solution)/shard_map/ppermute | solution.py:219
  73.2 3.8 %collective-permute-done.10 = bf16[128,1024]{1,0:T(8,128)(2,1)S(1)} collective-permute-done((bf16[128,1024]{1,0:T(8,128)(2,1)S(1)}, bf16[128,1024]{1,0:T(8,128)(2,1)S(1)}, u32[]{:S(2)}, u32[]{:S(2)}) %collective-permute-start.10) | collective-permute-done | bytes 262176 | tf_op jit(solution)/shard_map/ppermute | solution.py:219
  77.0 5.2 %collective-permute-done.11 = bf16[128,1024]{1,0:T(8,128)(2,1)S(1)} collective-permute-done((bf16[128,1024]{1,0:T(8,128)(2,1)S(1)}, bf16[128,1024]{1,0:T(8,128)(2,1)S(1)}, u32[]{:S(2)}, u32[]{:S(2)}) %collective-permute-start.11) | collective-permute-done | bytes 262176 | tf_op jit(solution)/shard_map/ppermute | solution.py:219
  82.2 0.8 add_convert_fusion.1
  (33 shorter events, 0.3 us)
Async XLA Ops:
  0.0 0.9 %copy-start.1 = (bf16[128,256]{1,0:T(8,128)(2,1)S(1)}, bf16[128,256]{1,0:T(8,128)(2,1)}, u32[]{:S(2)}) copy-start(bf16[128,256]{1,0:T(8,128)(2,1)} %v_ref.1) | copy-start | bytes 196612
  0.9 15.6 %collective-permute-start.4 = (bf16[128,512]{1,0:T(8,128)(2,1)S(1)}, bf16[128,512]{1,0:T(8,128)(2,1)S(1)}, u32[]{:S(2)}, u32[]{:S(2)}) collective-permute-start(bf16[128,512]{1,0:T(8,128)(2,1)S(1)} %constant_dynamic-update-slice_fusion), channel_id=1, source_target_pairs={{0,20},{4,24},{8,28},{1,21},{5,25},{9,29},{2,22},{6,26},{10,30},{3... | collective-permute-start | bytes 393224 | tf_op jit(solution)/shard_map/ppermute | solution.py:100
  6.9 13.7 %collective-permute-start = (bf16[128,512]{1,0:T(8,128)(2,1)S(1)}, bf16[128,512]{1,0:T(8,128)(2,1)S(1)}, u32[]{:S(2)}, u32[]{:S(2)}) collective-permute-start(bf16[128,512]{1,0:T(8,128)(2,1)S(1)} %constant_dynamic-update-slice_fusion), channel_id=1, source_target_pairs={{0,4},{4,8},{8,12},{12,16},{16,20},{20,24},{24,28},{1,5},{5,9},{9,... | collective-permute-start | bytes 393224 | tf_op jit(solution)/shard_map/ppermute | solution.py:100
  10.1 10.5 %collective-permute-start.1 = (bf16[128,512]{1,0:T(8,128)(2,1)S(1)}, bf16[128,512]{1,0:T(8,128)(2,1)S(1)}, u32[]{:S(2)}, u32[]{:S(2)}) collective-permute-start(bf16[128,512]{1,0:T(8,128)(2,1)S(1)} %constant_dynamic-update-slice_fusion), channel_id=1, source_target_pairs={{0,8},{4,12},{8,16},{12,20},{16,24},{20,28},{1,9},{5,13},{9,17},{1... | collective-permute-start | bytes 393224 | tf_op jit(solution)/shard_map/ppermute | solution.py:100
  12.0 8.6 %collective-permute-start.2 = (bf16[128,512]{1,0:T(8,128)(2,1)S(1)}, bf16[128,512]{1,0:T(8,128)(2,1)S(1)}, u32[]{:S(2)}, u32[]{:S(2)}) collective-permute-start(bf16[128,512]{1,0:T(8,128)(2,1)S(1)} %constant_dynamic-update-slice_fusion), channel_id=1, source_target_pairs={{0,12},{4,16},{8,20},{12,24},{16,28},{1,13},{5,17},{9,21},{13,25},... | collective-permute-start | bytes 393224 | tf_op jit(solution)/shard_map/ppermute | solution.py:100
  13.5 7.1 %collective-permute-start.3 = (bf16[128,512]{1,0:T(8,128)(2,1)S(1)}, bf16[128,512]{1,0:T(8,128)(2,1)S(1)}, u32[]{:S(2)}, u32[]{:S(2)}) collective-permute-start(bf16[128,512]{1,0:T(8,128)(2,1)S(1)} %constant_dynamic-update-slice_fusion), channel_id=1, source_target_pairs={{0,16},{4,20},{8,24},{12,28},{1,17},{5,21},{9,25},{13,29},{2,18},{... | collective-permute-start | bytes 393224 | tf_op jit(solution)/shard_map/ppermute | solution.py:100
  15.5 0.7 copy-start.10
  16.5 2.9 %copy-start.5 = (bf16[128,512]{1,0:T(8,128)(2,1)}, bf16[128,512]{1,0:T(8,128)(2,1)S(1)}, u32[]{:S(2)}) copy-start(bf16[128,512]{1,0:T(8,128)(2,1)S(1)} %collective-permute-done.4.refs_4_) | copy-start | bytes 393220
  16.6 34.0 %collective-permute-start.8 = (bf16[1024,512]{1,0:T(8,128)(2,1)}, bf16[1024,512]{1,0:T(8,128)(2,1)S(1)}, u32[]{:S(2)}, u32[]{:S(2)}) collective-permute-start(bf16[1024,512]{1,0:T(8,128)(2,1)} %refs_4_), channel_id=1, source_target_pairs={{0,4},{1,5},{2,6},{3,7},{4,0},{5,1},{6,2},{7,3},{8,12},{9,13},{10,... | collective-permute-start | bytes 3145736 | tf_op jit(solution)/shard_map/ppermute | solution.py:219
  20.6 0.7 copy-start.6
  20.6 0.7 copy-start.7
  20.6 0.7 copy-start.8
  20.6 0.7 copy-start.9
  26.4 15.3 %collective-permute-start.5 = (bf16[128,1024]{1,0:T(8,128)(2,1)}, bf16[128,1024]{1,0:T(8,128)(2,1)S(1)}, u32[]{:S(2)}, u32[]{:S(2)}) collective-permute-start(bf16[128,1024]{1,0:T(8,128)(2,1)} %attention.1.refs_0_), channel_id=1, source_target_pairs={{0,8},{1,9},{2,10},{3,11},{4,12},{5,13},{6,14},{7,15},{8,0},{9,1},... | collective-permute-start | bytes 786440 | tf_op jit(solution)/shard_map/ppermute | solution.py:219
  30.9 11.2 %collective-permute-start.6 = (bf16[128,1024]{1,0:T(8,128)(2,1)}, bf16[128,1024]{1,0:T(8,128)(2,1)S(1)}, u32[]{:S(2)}, u32[]{:S(2)}) collective-permute-start(bf16[128,1024]{1,0:T(8,128)(2,1)} %attention.1.refs_0_), channel_id=1, source_target_pairs={{0,16},{1,17},{2,18},{3,19},{4,20},{5,21},{6,22},{7,23},{8,24},{9,... | collective-permute-start | bytes 786440 | tf_op jit(solution)/shard_map/ppermute | solution.py:219
  34.0 16.5 %collective-permute-start.7 = (bf16[128,1024]{1,0:T(8,128)(2,1)}, bf16[128,1024]{1,0:T(8,128)(2,1)S(1)}, u32[]{:S(2)}, u32[]{:S(2)}) collective-permute-start(bf16[128,1024]{1,0:T(8,128)(2,1)} %attention.1.refs_0_), channel_id=1, source_target_pairs={{0,24},{1,25},{2,26},{3,27},{4,28},{5,29},{6,30},{7,31},{8,16},{9,... | collective-permute-start | bytes 786440 | tf_op jit(solution)/shard_map/ppermute | solution.py:219
  41.7 8.8 %copy-start.2 = (bf16[128,1024]{1,0:T(8,128)(2,1)}, bf16[128,1024]{1,0:T(8,128)(2,1)S(1)}, u32[]{:S(2)}) copy-start(bf16[128,1024]{1,0:T(8,128)(2,1)S(1)} %collective-permute-done.5.refs_1_) | copy-start | bytes 786436
  42.1 8.4 %copy-start.3 = (bf16[128,1024]{1,0:T(8,128)(2,1)}, bf16[128,1024]{1,0:T(8,128)(2,1)S(1)}, u32[]{:S(2)}) copy-start(bf16[128,1024]{1,0:T(8,128)(2,1)S(1)} %collective-permute-done.6.refs_2_) | copy-start | bytes 786436
  50.5 0.7 copy-start.4
  51.2 1.0 %copy-start = (bf16[1024,512]{1,0:T(8,128)(2,1)}, bf16[1024,512]{1,0:T(8,128)(2,1)S(1)}, u32[]{:S(2)}) copy-start(bf16[1024,512]{1,0:T(8,128)(2,1)S(1)} %collective-permute-done.8.refs_5_) | copy-start | bytes 3145732
  57.0 5.9 %collective-permute-start.9 = (bf16[2,128,1024]{2,1,0:T(8,128)(2,1)}, bf16[2,128,1024]{2,1,0:T(8,128)(2,1)S(1)}, u32[]{:S(2)}, u32[]{:S(2)}) collective-permute-start(bf16[2,128,1024]{2,1,0:T(8,128)(2,1)} %get-tuple-element.10), channel_id=1, source_target_pairs={{0,1},{1,0},{2,3},{3,2},{4,5},{5,4},{6,7},{7,6},{8,9},{9,8},{10,11... | collective-permute-start | bytes 1572872 | tf_op jit(solution)/shard_map/ppermute | solution.py:219
  64.2 12.8 %collective-permute-start.10 = (bf16[128,1024]{1,0:T(8,128)(2,1)S(1)}, bf16[128,1024]{1,0:T(8,128)(2,1)S(1)}, u32[]{:S(2)}, u32[]{:S(2)}) collective-permute-start(bf16[128,1024]{1,0:T(8,128)(2,1)S(1)} %get-tuple-element.11), channel_id=1, source_target_pairs={{0,0},{1,16},{2,8},{3,24},{4,4},{5,20},{6,12},{7,28},{8,9},{9,25},... | collective-permute-start | bytes 786440 | tf_op jit(solution)/shard_map/ppermute | solution.py:219
  71.3 10.9 %collective-permute-start.11 = (bf16[128,1024]{1,0:T(8,128)(2,1)S(1)}, bf16[128,1024]{1,0:T(8,128)(2,1)S(1)}, u32[]{:S(2)}, u32[]{:S(2)}) collective-permute-start(bf16[128,1024]{1,0:T(8,128)(2,1)S(1)} %get-tuple-element.12), channel_id=1, source_target_pairs={{0,8},{1,24},{2,0},{3,16},{4,12},{5,28},{6,4},{7,20},{8,1},{9,17},... | collective-permute-start | bytes 786440 | tf_op jit(solution)/shard_map/ppermute | solution.py:219

commit v2 on v1

v2 whole, which is shorter than its diff:
```python
import math
from functools import partial

import jax
import jax.numpy as jnp
from jax import lax
from jax.experimental import pallas as pl
from jax.experimental.pallas import tpu as pltpu
from jax.sharding import PartitionSpec as P


HD = 128
ROPE_BASE = 500000.0
NEG_FILL = -1e30
LONGEST = (5, 8)
KERNEL_BYTES = 16 << 20
FAR_BLOCKS = 7


def locate(token_index, doc_lengths):
    doc_ends = jnp.cumsum(doc_lengths)
    starts = doc_ends - doc_lengths
    doc_ids = jnp.sum((token_index[:, None] >= doc_ends[None, :]).astype(jnp.int32), axis=1)
    number = jnp.arange(doc_lengths.shape[0], dtype=jnp.int32)
    first_token = jnp.sum(
        jnp.where(doc_ids[:, None] == number[None, :], starts[None, :], 0), axis=1
    )
    return (doc_ids, token_index - first_token)


def on_chip(*arrays):
    return [pltpu.with_memory_space_constraint(a, pltpu.VMEM) for a in arrays]


def sine_cosine(angle):
    turns = jnp.round(angle * (2.0 / math.pi))
    rest = ((angle - turns * 1.5703125) - turns * 4.837512969970703125e-4) - turns * 7.54978995489188216e-8
    square = rest * rest
    sine = (-1.9515295891e-4 * square + 8.3321608736e-3) * square - 1.6666654611e-1
    sine = sine * square * rest + rest
    cosine = (2.443315711809948e-5 * square - 1.388731625493765e-3) * square
    cosine = (cosine + 4.166664568298827e-2) * square * square - 0.5 * square + 1.0
    quarter = turns.astype(jnp.int32)
    swapped = (quarter & 1) == 1
    flip_sine = (quarter & 2) == 2
    flip_cosine = ((quarter + 1) & 2) == 2
    out_sine = jnp.where(swapped, cosine, sine)
    out_cosine = jnp.where(swapped, sine, cosine)
    return (
        jnp.where(flip_sine, -out_sine, out_sine),
        jnp.where(flip_cosine, -out_cosine, out_cosine),
    )


def doc_start(index, lengths_ref):
    start, end = jnp.zeros_like(index), jnp.int32(0)
    for n in range(lengths_ref.shape[0]):
        start = jnp.where(index >= end, end, start)
        end = end + lengths_ref[n]
    return start


def turn(block, cosine, sine):
    block = block.astype(jnp.float32)
    return (block * cosine + pltpu.roll(block, HD // 2, 1) * sine).astype(jnp.bfloat16)


def attention_kernel(first_ref, lengths_ref, freq_ref, q_ref, k_ref, v_ref, *refs, reach, group):
    far, (out_ref, copy_ref, score_ref, weight_ref) = refs[:reach], refs[reach:]
    rows = q_ref.shape[0]
    kv_heads = k_ref.shape[1] // HD
    count = reach + 1
    first = first_ref[0]
    scale = HD**-0.5 * math.log2(math.e)
    lane = lax.broadcasted_iota(jnp.int32, (rows, HD), 1)
    sub = lax.broadcasted_iota(jnp.int32, (rows, HD), 0)
    freq = freq_ref[...]
    cosines, sines = [], []
    for n in range(count):
        index = first - (reach - n) * rows + sub
        start = doc_start(index, lengths_ref)
        sine, cosine = sine_cosine((index - start).astype(jnp.float32) * freq)
        cosines.append(cosine)
        sines.append(jnp.where(lane < HD // 2, -sine, sine))
    key_lane = lax.broadcasted_iota(jnp.int32, (rows, rows), 1)
    key_sub = lax.broadcasted_iota(jnp.int32, (rows, rows), 0)
    starts = doc_start(first + key_sub, lengths_ref)
    seen = [first - (reach - n) * rows + key_lane >= starts for n in range(count)]
    seen[reach] = seen[reach] & (key_lane <= key_sub)
    for g in range(kv_heads):
        at = slice(g * HD, (g + 1) * HD)
        at_v = slice((kv_heads + g) * HD, (kv_heads + g + 1) * HD)
        keys = [turn(far[reach - n - 1][:, at], cosines[n], sines[n]) for n in range(reach)]
        keys = jnp.concatenate(keys + [turn(k_ref[:, at], cosines[reach], sines[reach])], axis=0)
        vals = jnp.concatenate(
            [far[reach - n - 1][:, at_v] for n in range(reach)] + [v_ref[:, at]], axis=0
        )
        query = jnp.concatenate(
            [
                turn(q_ref[:, h * HD : (h + 1) * HD], cosines[reach], sines[reach])
                for h in range(g * group, (g + 1) * group)
            ],
            axis=0,
        )
        score_ref[...] = lax.dot_general(
            query, keys, (((1,), (1,)), ((), ())), preferred_element_type=jnp.float32
        )
        totals = []
        for h in range(group):
            band = slice(h * rows, (h + 1) * rows)
            masked = [
                jnp.where(seen[n], score_ref[band, n * rows : (n + 1) * rows] * scale, NEG_FILL)
                for n in range(count)
            ]
            top = masked[0]
            for m in masked[1:]:
                top = jnp.maximum(top, m)
            top = jnp.max(top, axis=1, keepdims=True)
            total = None
            for n in range(count):
                w = jnp.exp2(masked[n] - top)
                total = w if total is None else total + w
                weight_ref[band, n * rows : (n + 1) * rows] = w.astype(jnp.bfloat16)
            totals.append(jnp.sum(total, axis=1, keepdims=True))
        update = jnp.dot(weight_ref[...], vals, preferred_element_type=jnp.float32)
        for h in range(group):
            piece = update[h * rows : (h + 1) * rows, :] / totals[h]
            head = g * group + h
            out_ref[:, head * HD : (head + 1) * HD] = piece.astype(jnp.bfloat16)
            copy_ref[:, head * HD : (head + 1) * HD] = piece.astype(jnp.bfloat16)


def attend_near(queries, keys, values, doc_lengths, reach, n_tok):
    rows = queries.shape[0]
    group = queries.shape[1] // keys.shape[1]
    both = jnp.concatenate([keys, values], axis=1)
    far = []
    for d in range(1, reach + 1):
        far.append(lax.ppermute(both, "tok", [(i, i + d) for i in range(n_tok - d)]))
    first = (lax.axis_index("tok") * rows).astype(jnp.int32).reshape(1)
    half = jnp.arange(HD, dtype=jnp.float32) % (HD // 2)
    freq = (ROPE_BASE ** (-(half * 2.0 / HD))).reshape(1, HD)
    vmem = pl.BlockSpec(memory_space=pltpu.VMEM)
    smem = pl.BlockSpec(memory_space=pltpu.SMEM)
    span = (reach + 1) * rows
    attended = pl.pallas_call(
        partial(attention_kernel, reach=reach, group=group),
        out_shape=(pltpu.VMEM(queries.shape, jnp.bfloat16),) * 2,
        in_specs=[smem, smem] + [vmem] * (4 + reach),
        out_specs=(vmem, vmem),
        scratch_shapes=[
            pltpu.VMEM((group * rows, span), jnp.float32),
            pltpu.VMEM((group * rows, span), jnp.bfloat16),
        ],
        compiler_params=pltpu.CompilerParams(vmem_limit_bytes=KERNEL_BYTES),
        name="attention",
    )(first, doc_lengths, freq, *on_chip(queries, keys, values, *far))
    return *attended, far


def rotary(tensor, positions):
    half_size = tensor.shape[-1] // 2
    frequency = ROPE_BASE ** (-(jnp.arange(half_size, dtype=jnp.float32) * 2.0 / tensor.shape[-1]))
    angles = positions.astype(jnp.float32)[:, None] * frequency[None, :]
    cosine = jnp.cos(angles)[:, None, :]
    sine_part = jnp.sin(angles)[:, None, :]
    a = tensor[..., :half_size]
    b = tensor[..., half_size:]
    return jnp.concatenate([a * cosine - b * sine_part, b * cosine + a * sine_part], axis=-1)


def attend_far(queries, keys, values, doc_lengths):
    rows = queries.shape[0]
    heads, kv_heads = queries.shape[1] // HD, keys.shape[1] // HD
    own = lax.axis_index("tok") * rows + jnp.arange(rows, dtype=jnp.int32)
    docs, positions = locate(own, doc_lengths)
    rotated_q = rotary(queries.astype(jnp.float32).reshape(rows, heads, HD), positions)
    rotated_q = rotated_q.astype(jnp.bfloat16).reshape(rows, kv_heads, heads // kv_heads, HD)
    rotated_k = rotary(keys.astype(jnp.float32).reshape(rows, kv_heads, HD), positions)
    rotated_k = rotated_k.astype(jnp.bfloat16).reshape(rows, kv_heads * HD)
    all_k = lax.all_gather(rotated_k, "tok", axis=0, tiled=True)
    all_v = lax.all_gather(values, "tok", axis=0, tiled=True)
    step = 4 * rows

    def one_block(number, state):
        running, totals, weighted = state
        begin = number * step
        key = lax.dynamic_slice_in_dim(all_k, begin, step, 0).reshape(step, kv_heads, HD)
        value = lax.dynamic_slice_in_dim(all_v, begin, step, 0).reshape(step, kv_heads, HD)
        index = begin + jnp.arange(step, dtype=jnp.int32)
        key_docs, _ = locate(index, doc_lengths)
        scores = HD**-0.5 * jnp.einsum(
            "qgjd,kgd->gjqk", rotated_q, key, preferred_element_type=jnp.float32
        )
        visible = (docs[:, None] == key_docs[None, :]) & (index[None, :] <= own[:, None])
        scores = jnp.where(visible, scores, NEG_FILL)
        top = jnp.maximum(running, jnp.max(scores, axis=-1))
        factor = jnp.exp(running - top)
        weights = jnp.where(visible, jnp.exp(scores - top[..., None]), 0.0)
        totals = totals * factor + jnp.sum(weights, axis=-1)
        update = jnp.einsum(
            "gjqk,kgd->gjqd",
            weights.astype(jnp.bfloat16),
            value,
            preferred_element_type=jnp.float32,
        )
        return (top, totals, weighted * factor[..., None] + update)

    shape = (kv_heads, heads // kv_heads, rows)
    state = (
        jnp.full(shape, NEG_FILL, jnp.float32),
        jnp.zeros(shape, jnp.float32),
        jnp.zeros(shape + (HD,), jnp.float32),
    )
    _, totals, weighted = lax.fori_loop(0, all_k.shape[0] // step, one_block, state)
    output = (weighted / totals[..., None]).transpose(2, 0, 1, 3)
    output = output.reshape(rows, heads * HD).astype(jnp.bfloat16)
    return output, output, all_v[0]


def columns(left, weights, flip):
    pieces = []
    for w in weights:
        piece = jnp.dot(left, w[...], preferred_element_type=jnp.float32)
        pieces.append(piece.astype(jnp.bfloat16))
    if len(pieces) == 1:
        return pieces[0]
    straight = jnp.concatenate(pieces, axis=1)
    return jnp.where(flip == 0, straight, jnp.concatenate(pieces[::-1], axis=1))


def near_kernel(place_ref, own_ref, mate_ref, *refs, sides):
    weights, (first_ref, second_ref) = refs[:sides], refs[sides : sides + 2]
    rows = own_ref.shape[0]
    left = jnp.concatenate([own_ref[...], mate_ref[...]], axis=0)
    result = columns(left, weights, place_ref[0])
    own, mate = result[:rows], result[rows:]
    first_ref[...] = jnp.where(place_ref[1] == 0, own, mate)
    second_ref[...] = jnp.where(place_ref[1] == 0, mate, own)


def away_kernel(place_ref, near_ref, far_ref, *refs, sides):
    weights, (keep_ref, send_ref) = refs[:sides], refs[sides : sides + 2]
    result = columns(far_ref[...], weights, place_ref[0])
    keep_ref[...] = jnp.where(place_ref[2] == 0, near_ref[...], result)
    send_ref[...] = jnp.where(place_ref[2] == 0, result, near_ref[...])


def project(kernel, place, left, weights):
    rows, width = left[0].shape[0], sum(w.shape[1] for w in weights)
    vmem = pl.BlockSpec(memory_space=pltpu.VMEM)
    outs = [pltpu.VMEM((rows, width), jnp.bfloat16)] * 2
    outs += [pltpu.VMEM(w.shape, w.dtype) for w in weights]
    begin = 1 + len(left)
    first, second, *weights = pl.pallas_call(
        partial(kernel, sides=len(weights)),
        out_shape=tuple(outs),
        in_specs=[pl.BlockSpec(memory_space=pltpu.SMEM)] + [vmem] * (len(left) + len(weights)),
        out_specs=(vmem,) * len(outs),
        input_output_aliases={begin + n: 2 + n for n in range(len(weights))},
        compiler_params=pltpu.CompilerParams(vmem_limit_bytes=KERNEL_BYTES),
    )(place, *on_chip(*left, *weights))
    return first, second, weights


def solution(mesh):
    n_tok, n_feat = mesh.shape["tok"], mesh.shape["feat"]
    inner = n_tok // n_feat

    def everyone(move):
        pairs = []
        for z in range(n_feat):
            for x in range(inner):
                for j in range(n_feat):
                    to_z, to_x, to_j = move(z, x, j)
                    pairs.append(
                        (
                            (z * inner + x) * n_feat + j,
                            (to_z * inner + to_x) * n_feat + to_j,
                        )
                    )
        return pairs

    def permute(array, move):
        return lax.ppermute(array, ("tok", "feat"), everyone(move))

    def shards(queries, keys, values, out_weight, doc_lengths):
        rows = queries.shape[0]
        me, feat = lax.axis_index("tok"), lax.axis_index("feat")
        x = me % inner
        longest = n_tok * rows * LONGEST[0] // LONGEST[1]
        reach = min(n_tok - 1, -(-(longest - 1) // rows))
        if reach <= FAR_BLOCKS:
            attended, own, seen = attend_near(queries, keys, values, doc_lengths, reach, n_tok)
        else:
            attended, own, seen = attend_far(queries, keys, values, doc_lengths)
        out_weight, _ = lax.optimization_barrier((out_weight, seen))
        if inner == 2:
            weights = [out_weight, permute(out_weight, lambda z, x, j: (z, 1 - x, j))]
        else:
            groups = [[z * inner + x for x in range(inner)] for z in range(n_feat)]
            weights = [
                lax.all_gather(
                    out_weight, "tok", axis=1, tiled=True, axis_index_groups=groups
                )
            ]
        mate = permute(attended, lambda z, x, j: (z ^ 1, x, j))
        away = []
        for k in range(2):
            away.append(
                permute(attended, lambda z, x, j: (z ^ (2 | ((j >> 1) ^ k)), x, j))
            )
        place = jnp.stack([x, feat >> 1, feat & 1]).astype(jnp.int32)
        *near, weights = project(near_kernel, place, [own, mate], weights)
        home = []
        for k in range(2):
            keep, send, weights = project(away_kernel, place, [near[k], away[k]], weights)
            other = permute(send, lambda z, x, j: (z, x, j ^ 1))
            both = (keep.astype(jnp.float32) + other.astype(jnp.float32)).astype(jnp.bfloat16)
            home.append(permute(both, lambda z, x, j: (z ^ ((j & 1) * 2 + ((j >> 1) ^ k)), x, z)))
        return (home[0].astype(jnp.float32) + home[1].astype(jnp.float32)).astype(jnp.bfloat16)

    in_specs = (P("tok", "feat"), P("tok", "feat"), P("tok", "feat"), P("feat", "tok"), P())
    return jax.shard_map(
        shards, mesh=mesh, in_specs=in_specs, out_specs=P("tok", "feat"), check_vma=False
    )
```

time: 83.3 us -> 79.4 us (0.953)
  starting transfers between devices: 36 us -> 49.5 us
  waiting for transfers between devices: 26.6 us -> 19.3 us
  other arithmetic: 5.58 us -> 1 us
  local copies, waits for them, and re-layouts: 4.76 us -> 1.93 us
  Pallas kernels: 9.73 us -> 7.18 us
    ppermute x7 -> x8, starting transfers between devices: 21.5 us -> 34.8 us  [permute(): return lax.ppermute(array, ('tok', 'feat'), everyone(move))]
    ppermute x7 -> x8, waiting for transfers between devices: 26.6 us -> 17.4 us  [permute(): return lax.ppermute(array, ('tok', 'feat'), everyone(move))]
    unnamed x23 -> x9, local copies, waits for them, and re-layouts: 3.97 us -> 0.66 us
    pallas_call x2 -> x4, Pallas kernels: 9.73 us -> 7.18 us  [the longest x1 3.87 us: attend_near(): pl.pallas_call(partial(attention_kernel, reach=reach, group=group), out_s...]
    ppermute x5, waiting for transfers between devices: 0.01 us -> 1.96 us  [attend_near(): lax.ppermute(both, 'tok', [(i, i + d) for i in range(n_tok - d)])]
    neg x1 -> x0, other arithmetic: 1.45 us -> none  [tables(): -sine]
    optimization_barrier x0 -> x1, local copies, waits for them, and re-layouts: none -> 1.26 us  [shards(): out_weight, _ = lax.optimization_barrier((out_weight, seen))]
    concatenate x1 -> x0, other arithmetic: 1.17 us -> none  [tables(): jnp.concatenate([cosine, cosine], axis=-1)]
  transfers between devices with their start and end apart: 12 -> 13, of which waited for: 6 -> 4; matrix products, arithmetic and copies ran while one was open for 5% -> 0% of each run, Pallas kernels for 6% -> 9%
where the time goes in v2:
time: 79.4 us; the launch traced here: 79.2 us
  starting transfers between devices  49.5 us (62%)
  waiting for transfers between devices  19.3 us (24%)
  Pallas kernels  7.18 us (9%)
  local copies, waits for them, and re-layouts  1.93 us (2%)
  other arithmetic  1 us (1%)
    ppermute x8, starting transfers between devices, permute(): return lax.ppermute(array, ('tok', 'feat'), everyone(move))  34.8 us
    ppermute x8, waiting for transfers between devices, permute(): return lax.ppermute(array, ('tok', 'feat'), everyone(move))  17.4 us
    ppermute x5, starting transfers between devices, attend_near(): lax.ppermute(both, 'tok', [(i, i + d) for i in range(n_tok - d)])  14.7 us
    pallas_call x1, Pallas kernels, attend_near(): pl.pallas_call(partial(attention_kernel, reach=reach, group=group), out_s...  3.87 us
    pallas_call x3, Pallas kernels, project(): pl.pallas_call(partial(kernel, sides=len(weights)), out_shape=tuple(outs)...  3.3 us
    ppermute x5, waiting for transfers between devices, attend_near(): lax.ppermute(both, 'tok', [(i, i + d) for i in range(n_tok - d)])  1.96 us
  transfers between devices with their start and end apart: 13, of which 4 were waited for; matrix products, arithmetic and copies ran while one was open for 0% of the time, Pallas kernels for 9%

profile of v2, /device:TPU:1, one launch (start us, length us, event | category | flops | bytes accessed | tf_op | source)
XLA Modules:
  0.0 79.2 jit_solution(11088833440660953968)
XLA Ops:
  0.0 1.3 %copy.20.refs_0_ = bf16[1024,512]{1,0:T(8,128)(2,1)S(1)} copy(bf16[1024,512]{1,0:T(8,128)(2,1)} %param.8) | data formatting | bytes 2097152 | tf_op jit(solution)/shard_map/optimization_barrier | solution.py:297
  1.3 6.1 %collective-permute-start.4 = (bf16[128,512]{1,0:T(8,128)(2,1)S(1)}, bf16[128,512]{1,0:T(8,128)(2,1)S(1)}, u32[]{:S(2)}, u32[]{:S(2)}) collective-permute-start(bf16[128,512]{1,0:T(8,128)(2,1)S(1)} %constant_dynamic-update-slice_fusion), channel_id=1, source_target_pairs={{0,20},{4,24},{8,28},{1,21},{5,25},{9,29},{2,22},{6,26},{10,30},{3... | collective-permute-start | bytes 393224 | tf_op jit(solution)/shard_map/ppermute | solution.py:139
  7.4 1.3 %collective-permute-start.3 = (bf16[128,512]{1,0:T(8,128)(2,1)S(1)}, bf16[128,512]{1,0:T(8,128)(2,1)S(1)}, u32[]{:S(2)}, u32[]{:S(2)}) collective-permute-start(bf16[128,512]{1,0:T(8,128)(2,1)S(1)} %constant_dynamic-update-slice_fusion), channel_id=1, source_target_pairs={{0,16},{4,20},{8,24},{12,28},{1,17},{5,21},{9,25},{13,29},{2,18},{... | collective-permute-start | bytes 393224 | tf_op jit(solution)/shard_map/ppermute | solution.py:139
  8.7 3.2 %collective-permute-start.2 = (bf16[128,512]{1,0:T(8,128)(2,1)S(1)}, bf16[128,512]{1,0:T(8,128)(2,1)S(1)}, u32[]{:S(2)}, u32[]{:S(2)}) collective-permute-start(bf16[128,512]{1,0:T(8,128)(2,1)S(1)} %constant_dynamic-update-slice_fusion), channel_id=1, source_target_pairs={{0,12},{4,16},{8,20},{12,24},{16,28},{1,13},{5,17},{9,21},{13,25},... | collective-permute-start | bytes 393224 | tf_op jit(solution)/shard_map/ppermute | solution.py:139
  11.9 1.3 %collective-permute-start.1 = (bf16[128,512]{1,0:T(8,128)(2,1)S(1)}, bf16[128,512]{1,0:T(8,128)(2,1)S(1)}, u32[]{:S(2)}, u32[]{:S(2)}) collective-permute-start(bf16[128,512]{1,0:T(8,128)(2,1)S(1)} %constant_dynamic-update-slice_fusion), channel_id=1, source_target_pairs={{0,8},{4,12},{8,16},{12,20},{16,24},{20,28},{1,9},{5,13},{9,17},{1... | collective-permute-start | bytes 393224 | tf_op jit(solution)/shard_map/ppermute | solution.py:139
  13.2 2.8 %collective-permute-start = (bf16[128,512]{1,0:T(8,128)(2,1)S(1)}, bf16[128,512]{1,0:T(8,128)(2,1)S(1)}, u32[]{:S(2)}, u32[]{:S(2)}) collective-permute-start(bf16[128,512]{1,0:T(8,128)(2,1)S(1)} %constant_dynamic-update-slice_fusion), channel_id=1, source_target_pairs={{0,4},{4,8},{8,12},{12,16},{16,20},{20,24},{24,28},{1,5},{5,9},{9,... | collective-permute-start | bytes 393224 | tf_op jit(solution)/shard_map/ppermute | solution.py:139
  16.1 0.0 collective-permute-done.4.refs_4_
  16.1 0.0 collective-permute-done.2.refs_2_
  16.1 1.9 %collective-permute-done.1.refs_1_ = bf16[128,512]{1,0:T(8,128)(2,1)S(1)} collective-permute-done((bf16[128,512]{1,0:T(8,128)(2,1)S(1)}, bf16[128,512]{1,0:T(8,128)(2,1)S(1)}, u32[]{:S(2)}, u32[]{:S(2)}) %collective-permute-start.1) | collective-permute-done | bytes 131104 | tf_op jit(solution)/shard_map/ppermute | solution.py:139
  18.0 4.1 %collective-permute-start.6 = (bf16[1024,512]{1,0:T(8,128)(2,1)S(1)}, bf16[1024,512]{1,0:T(8,128)(2,1)S(1)}, u32[]{:S(2)}, u32[]{:S(2)}) collective-permute-start(bf16[1024,512]{1,0:T(8,128)(2,1)S(1)} %copy.20.refs_0_), channel_id=1, source_target_pairs={{0,4},{1,5},{2,6},{3,7},{4,0},{5,1},{6,2},{7,3},{8,12},{9,13},{10,... | collective-permute-start | bytes 3145736 | tf_op jit(solution)/shard_map/ppermute | solution.py:285
  22.2 0.6 copy-done.3
  22.8 3.9 %attention.1 = (bf16[128,1024]{1,0:T(8,128)(2,1)}, bf16[128,1024]{1,0:T(8,128)(2,1)S(1)}) custom-call(s32[1]{0:T(128)} %bitcast.3.first_ref, s32[6]{0:T(128)S(1)} %copy-done.3, f32[1,128]{1,0:T(1,128)S(1)} %fusion.2.freq_ref, bf16[128,1024]{1,0:T(8,128)(2,1)S(1)} %copy-done, bf16[128,256]{1,0:T(8,128)(2,1)S(1)} %copy-done.1, bf16[128,256]{1,0:T(8,128)(2,1)S(1)} %copy-done.2, ...), custom_call_target="tpu_custom_call" | custom-call | tf_op jit(solution)/shard_map/attention/pallas_call | solution.py:146
  26.7 7.8 %collective-permute-start.5 = (bf16[128,1024]{1,0:T(8,128)(2,1)}, bf16[128,1024]{1,0:T(8,128)(2,1)S(1)}, u32[]{:S(2)}, u32[]{:S(2)}) collective-permute-start(bf16[128,1024]{1,0:T(8,128)(2,1)} %get-tuple-element.19), channel_id=1, source_target_pairs={{0,8},{1,9},{2,10},{3,11},{4,12},{5,13},{6,14},{7,15},{8,0},{9,1},... | collective-permute-start | bytes 786440 | tf_op jit(solution)/shard_map/ppermute | solution.py:285
  34.5 1.6 %collective-permute-start.7 = (bf16[128,1024]{1,0:T(8,128)(2,1)}, bf16[128,1024]{1,0:T(8,128)(2,1)S(1)}, u32[]{:S(2)}, u32[]{:S(2)}) collective-permute-start(bf16[128,1024]{1,0:T(8,128)(2,1)} %get-tuple-element.19), channel_id=1, source_target_pairs={{0,16},{1,17},{2,26},{3,27},{4,20},{5,21},{6,30},{7,31},{8,24},{9,... | collective-permute-start | bytes 786440 | tf_op jit(solution)/shard_map/ppermute | solution.py:285
  36.1 1.2 %collective-permute-start.10 = (bf16[128,1024]{1,0:T(8,128)(2,1)}, bf16[128,1024]{1,0:T(8,128)(2,1)S(1)}, u32[]{:S(2)}, u32[]{:S(2)}) collective-permute-start(bf16[128,1024]{1,0:T(8,128)(2,1)} %get-tuple-element.19), channel_id=1, source_target_pairs={{0,24},{1,25},{2,18},{3,19},{4,28},{5,29},{6,22},{7,23},{8,16},{9,... | collective-permute-start | bytes 786440 | tf_op jit(solution)/shard_map/ppermute | solution.py:285
  37.3 0.1 pad_add_fusion.place_ref
  37.4 8.4 %collective-permute-done.5.mate_ref = bf16[128,1024]{1,0:T(8,128)(2,1)S(1)} collective-permute-done((bf16[128,1024]{1,0:T(8,128)(2,1)}, bf16[128,1024]{1,0:T(8,128)(2,1)S(1)}, u32[]{:S(2)}, u32[]{:S(2)}) %collective-permute-start.5) | collective-permute-done | bytes 262176 | tf_op jit(solution)/shard_map/ppermute | solution.py:285
  45.8 0.0 collective-permute-done.6.refs_1_
  45.8 1.3 %shard_map.55 = (bf16[128,1024]{1,0:T(8,128)(2,1)S(1)}, bf16[128,1024]{1,0:T(8,128)(2,1)S(1)}, bf16[1024,512]{1,0:T(8,128)(2,1)S(1)}, bf16[1024,512]{1,0:T(8,128)(2,1)S(1)}) custom-call(s32[3]{0:T(128)S(1)} %pad_add_fusion.place_ref, bf16[128,1024]{1,0:T(8,128)(2,1)S(1)} %get-tuple-element.18.own_ref, ...), custom_call_target="tpu_custom_call", output_to_operand_aliasing={{2}: (3, {}), {3}: (4, {})} | custom-call | tf_op jit(solution)/shard_map/pallas_call | solution.py:255
  47.0 0.0 collective-permute-done.7.far_ref
  47.1 1.0 %shard_map.56 = (bf16[128,1024]{1,0:T(8,128)(2,1)S(1)}, bf16[128,1024]{1,0:T(8,128)(2,1)S(1)}, bf16[1024,512]{1,0:T(8,128)(2,1)S(1)}, bf16[1024,512]{1,0:T(8,128)(2,1)S(1)}) custom-call(s32[3]{0:T(128)S(1)} %pad_add_fusion.place_ref, bf16[128,1024]{1,0:T(8,128)(2,1)S(1)} %get-tuple-element.21.near_ref, ...), custom_call_target="tpu_custom_call", output_to_operand_aliasing={{2}: (3, {}), {3}: (4, {})} | custom-call | tf_op jit(solution)/shard_map/pallas_call | solution.py:255
  48.1 10.1 %collective-permute-start.8 = (bf16[128,1024]{1,0:T(8,128)(2,1)S(1)}, bf16[128,1024]{1,0:T(8,128)(2,1)S(1)}, u32[]{:S(2)}, u32[]{:S(2)}) collective-permute-start(bf16[128,1024]{1,0:T(8,128)(2,1)S(1)} %get-tuple-element.25), channel_id=1, source_target_pairs={{0,1},{1,0},{2,3},{3,2},{4,5},{5,4},{6,7},{7,6},{8,9},{9,8},{10,11... | collective-permute-start | bytes 786440 | tf_op jit(solution)/shard_map/ppermute | solution.py:285
  58.2 1.0 %shard_map.57 = (bf16[128,1024]{1,0:T(8,128)(2,1)S(1)}, bf16[128,1024]{1,0:T(8,128)(2,1)S(1)}, bf16[1024,512]{1,0:T(8,128)(2,1)S(1)}, bf16[1024,512]{1,0:T(8,128)(2,1)S(1)}) custom-call(s32[3]{0:T(128)S(1)} %pad_add_fusion.place_ref, bf16[128,1024]{1,0:T(8,128)(2,1)S(1)} %get-tuple-element.26.near_ref, ...), custom_call_target="tpu_custom_call", output_to_operand_aliasing={{2}: (3, {}), {3}: (4, {})} | custom-call | tf_op jit(solution)/shard_map/pallas_call | solution.py:255
  59.2 0.1 collective-permute-start.11
  59.3 0.0 collective-permute-done.8
  59.3 0.1 add_convert_fusion.2
  59.4 6.7 %collective-permute-start.9 = (bf16[128,1024]{1,0:T(8,128)(2,1)S(1)}, bf16[128,1024]{1,0:T(8,128)(2,1)S(1)}, u32[]{:S(2)}, u32[]{:S(2)}) collective-permute-start(bf16[128,1024]{1,0:T(8,128)(2,1)S(1)} %add_convert_fusion.2), channel_id=1, source_target_pairs={{0,0},{1,16},{2,8},{3,24},{4,4},{5,20},{6,12},{7,28},{8,9},{9,25},... | collective-permute-start | bytes 786440 | tf_op jit(solution)/shard_map/ppermute | solution.py:285
  66.2 0.1 add_convert_fusion.1
  66.2 3.2 %collective-permute-start.12 = (bf16[128,1024]{1,0:T(8,128)(2,1)S(1)}, bf16[128,1024]{1,0:T(8,128)(2,1)S(1)}, u32[]{:S(2)}, u32[]{:S(2)}) collective-permute-start(bf16[128,1024]{1,0:T(8,128)(2,1)S(1)} %add_convert_fusion.1), channel_id=1, source_target_pairs={{0,8},{1,24},{2,0},{3,16},{4,12},{5,28},{6,4},{7,20},{8,1},{9,17},... | collective-permute-start | bytes 786440 | tf_op jit(solution)/shard_map/ppermute | solution.py:285
  69.4 1.5 %collective-permute-done.9 = bf16[128,1024]{1,0:T(8,128)(2,1)S(1)} collective-permute-done((bf16[128,1024]{1,0:T(8,128)(2,1)S(1)}, bf16[128,1024]{1,0:T(8,128)(2,1)S(1)}, u32[]{:S(2)}, u32[]{:S(2)}) %collective-permute-start.9) | collective-permute-done | bytes 262176 | tf_op jit(solution)/shard_map/ppermute | solution.py:285
  70.9 7.5 %collective-permute-done.12 = bf16[128,1024]{1,0:T(8,128)(2,1)S(1)} collective-permute-done((bf16[128,1024]{1,0:T(8,128)(2,1)S(1)}, bf16[128,1024]{1,0:T(8,128)(2,1)S(1)}, u32[]{:S(2)}, u32[]{:S(2)}) %collective-permute-start.12) | collective-permute-done | bytes 262176 | tf_op jit(solution)/shard_map/ppermute | solution.py:285
  78.4 0.8 add_convert_fusion
  (14 shorter events, 0.1 us)
Async XLA Ops:
  0.0 1.3 %copy-start.1 = (bf16[128,256]{1,0:T(8,128)(2,1)S(1)}, bf16[128,256]{1,0:T(8,128)(2,1)}, u32[]{:S(2)}) copy-start(bf16[128,256]{1,0:T(8,128)(2,1)} %k_ref.1) | copy-start | bytes 196612
  0.0 1.3 %copy-start.2 = (bf16[128,256]{1,0:T(8,128)(2,1)S(1)}, bf16[128,256]{1,0:T(8,128)(2,1)}, u32[]{:S(2)}) copy-start(bf16[128,256]{1,0:T(8,128)(2,1)} %v_ref.1) | copy-start | bytes 196612
  1.3 20.9 %copy-start = (bf16[128,1024]{1,0:T(8,128)(2,1)S(1)}, bf16[128,1024]{1,0:T(8,128)(2,1)}, u32[]{:S(2)}) copy-start(bf16[128,1024]{1,0:T(8,128)(2,1)} %q_ref.1) | copy-start | bytes 786436
  1.3 14.8 %collective-permute-start.4 = (bf16[128,512]{1,0:T(8,128)(2,1)S(1)}, bf16[128,512]{1,0:T(8,128)(2,1)S(1)}, u32[]{:S(2)}, u32[]{:S(2)}) collective-permute-start(bf16[128,512]{1,0:T(8,128)(2,1)S(1)} %constant_dynamic-update-slice_fusion), channel_id=1, source_target_pairs={{0,20},{4,24},{8,28},{1,21},{5,25},{9,29},{2,22},{6,26},{10,30},{3... | collective-permute-start | bytes 393224 | tf_op jit(solution)/shard_map/ppermute | solution.py:139
  7.4 8.7 %collective-permute-start.3 = (bf16[128,512]{1,0:T(8,128)(2,1)S(1)}, bf16[128,512]{1,0:T(8,128)(2,1)S(1)}, u32[]{:S(2)}, u32[]{:S(2)}) collective-permute-start(bf16[128,512]{1,0:T(8,128)(2,1)S(1)} %constant_dynamic-update-slice_fusion), channel_id=1, source_target_pairs={{0,16},{4,20},{8,24},{12,28},{1,17},{5,21},{9,25},{13,29},{2,18},{... | collective-permute-start | bytes 393224 | tf_op jit(solution)/shard_map/ppermute | solution.py:139
  8.7 7.4 %collective-permute-start.2 = (bf16[128,512]{1,0:T(8,128)(2,1)S(1)}, bf16[128,512]{1,0:T(8,128)(2,1)S(1)}, u32[]{:S(2)}, u32[]{:S(2)}) collective-permute-start(bf16[128,512]{1,0:T(8,128)(2,1)S(1)} %constant_dynamic-update-slice_fusion), channel_id=1, source_target_pairs={{0,12},{4,16},{8,20},{12,24},{16,28},{1,13},{5,17},{9,21},{13,25},... | collective-permute-start | bytes 393224 | tf_op jit(solution)/shard_map/ppermute | solution.py:139
  11.9 6.1 %collective-permute-start.1 = (bf16[128,512]{1,0:T(8,128)(2,1)S(1)}, bf16[128,512]{1,0:T(8,128)(2,1)S(1)}, u32[]{:S(2)}, u32[]{:S(2)}) collective-permute-start(bf16[128,512]{1,0:T(8,128)(2,1)S(1)} %constant_dynamic-update-slice_fusion), channel_id=1, source_target_pairs={{0,8},{4,12},{8,16},{12,20},{16,24},{20,28},{1,9},{5,13},{9,17},{1... | collective-permute-start | bytes 393224 | tf_op jit(solution)/shard_map/ppermute | solution.py:139
  13.2 4.8 %collective-permute-start = (bf16[128,512]{1,0:T(8,128)(2,1)S(1)}, bf16[128,512]{1,0:T(8,128)(2,1)S(1)}, u32[]{:S(2)}, u32[]{:S(2)}) collective-permute-start(bf16[128,512]{1,0:T(8,128)(2,1)S(1)} %constant_dynamic-update-slice_fusion), channel_id=1, source_target_pairs={{0,4},{4,8},{8,12},{12,16},{16,20},{20,24},{24,28},{1,5},{5,9},{9,... | collective-permute-start | bytes 393224 | tf_op jit(solution)/shard_map/ppermute | solution.py:139
  18.0 27.7 %collective-permute-start.6 = (bf16[1024,512]{1,0:T(8,128)(2,1)S(1)}, bf16[1024,512]{1,0:T(8,128)(2,1)S(1)}, u32[]{:S(2)}, u32[]{:S(2)}) collective-permute-start(bf16[1024,512]{1,0:T(8,128)(2,1)S(1)} %copy.20.refs_0_), channel_id=1, source_target_pairs={{0,4},{1,5},{2,6},{3,7},{4,0},{5,1},{6,2},{7,3},{8,12},{9,13},{10,... | collective-permute-start | bytes 3145736 | tf_op jit(solution)/shard_map/ppermute | solution.py:285
  22.1 0.7 copy-start.3
  26.7 19.1 %collective-permute-start.5 = (bf16[128,1024]{1,0:T(8,128)(2,1)}, bf16[128,1024]{1,0:T(8,128)(2,1)S(1)}, u32[]{:S(2)}, u32[]{:S(2)}) collective-permute-start(bf16[128,1024]{1,0:T(8,128)(2,1)} %get-tuple-element.19), channel_id=1, source_target_pairs={{0,8},{1,9},{2,10},{3,11},{4,12},{5,13},{6,14},{7,15},{8,0},{9,1},... | collective-permute-start | bytes 786440 | tf_op jit(solution)/shard_map/ppermute | solution.py:285
  34.5 12.5 %collective-permute-start.7 = (bf16[128,1024]{1,0:T(8,128)(2,1)}, bf16[128,1024]{1,0:T(8,128)(2,1)S(1)}, u32[]{:S(2)}, u32[]{:S(2)}) collective-permute-start(bf16[128,1024]{1,0:T(8,128)(2,1)} %get-tuple-element.19), channel_id=1, source_target_pairs={{0,16},{1,17},{2,26},{3,27},{4,20},{5,21},{6,30},{7,31},{8,24},{9,... | collective-permute-start | bytes 786440 | tf_op jit(solution)/shard_map/ppermute | solution.py:285
  36.1 22.0 %collective-permute-start.10 = (bf16[128,1024]{1,0:T(8,128)(2,1)}, bf16[128,1024]{1,0:T(8,128)(2,1)S(1)}, u32[]{:S(2)}, u32[]{:S(2)}) collective-permute-start(bf16[128,1024]{1,0:T(8,128)(2,1)} %get-tuple-element.19), channel_id=1, source_target_pairs={{0,24},{1,25},{2,18},{3,19},{4,28},{5,29},{6,22},{7,23},{8,16},{9,... | collective-permute-start | bytes 786440 | tf_op jit(solution)/shard_map/ppermute | solution.py:285
  48.1 11.3 %collective-permute-start.8 = (bf16[128,1024]{1,0:T(8,128)(2,1)S(1)}, bf16[128,1024]{1,0:T(8,128)(2,1)S(1)}, u32[]{:S(2)}, u32[]{:S(2)}) collective-permute-start(bf16[128,1024]{1,0:T(8,128)(2,1)S(1)} %get-tuple-element.25), channel_id=1, source_target_pairs={{0,1},{1,0},{2,3},{3,2},{4,5},{5,4},{6,7},{7,6},{8,9},{9,8},{10,11... | collective-permute-start | bytes 786440 | tf_op jit(solution)/shard_map/ppermute | solution.py:285
  59.2 6.9 %collective-permute-start.11 = (bf16[128,1024]{1,0:T(8,128)(2,1)S(1)}, bf16[128,1024]{1,0:T(8,128)(2,1)S(1)}, u32[]{:S(2)}, u32[]{:S(2)}) collective-permute-start(bf16[128,1024]{1,0:T(8,128)(2,1)S(1)} %get-tuple-element.30), channel_id=1, source_target_pairs={{0,1},{1,0},{2,3},{3,2},{4,5},{5,4},{6,7},{7,6},{8,9},{9,8},{10,11... | collective-permute-start | bytes 786440 | tf_op jit(solution)/shard_map/ppermute | solution.py:285
  59.4 11.5 %collective-permute-start.9 = (bf16[128,1024]{1,0:T(8,128)(2,1)S(1)}, bf16[128,1024]{1,0:T(8,128)(2,1)S(1)}, u32[]{:S(2)}, u32[]{:S(2)}) collective-permute-start(bf16[128,1024]{1,0:T(8,128)(2,1)S(1)} %add_convert_fusion.2), channel_id=1, source_target_pairs={{0,0},{1,16},{2,8},{3,24},{4,4},{5,20},{6,12},{7,28},{8,9},{9,25},... | collective-permute-start | bytes 786440 | tf_op jit(solution)/shard_map/ppermute | solution.py:285
  66.2 12.2 %collective-permute-start.12 = (bf16[128,1024]{1,0:T(8,128)(2,1)S(1)}, bf16[128,1024]{1,0:T(8,128)(2,1)S(1)}, u32[]{:S(2)}, u32[]{:S(2)}) collective-permute-start(bf16[128,1024]{1,0:T(8,128)(2,1)S(1)} %add_convert_fusion.1), channel_id=1, source_target_pairs={{0,8},{1,24},{2,0},{3,16},{4,12},{5,28},{6,4},{7,20},{8,1},{9,17},... | collective-permute-start | bytes 786440 | tf_op jit(solution)/shard_map/ppermute | solution.py:285

commit v3 on v2

--- a/solution.py
+++ b/solution.py
@@ -3,6 +3,7 @@
 
 import jax
 import jax.numpy as jnp
+import numpy as np
 from jax import lax
 from jax.experimental import pallas as pl
 from jax.experimental.pallas import tpu as pltpu
@@ -65,23 +66,35 @@
     return (block * cosine + pltpu.roll(block, HD // 2, 1) * sine).astype(jnp.bfloat16)
 
 
-def attention_kernel(first_ref, lengths_ref, freq_ref, q_ref, k_ref, v_ref, *refs, reach, group):
-    far, (out_ref, copy_ref, score_ref, weight_ref) = refs[:reach], refs[reach:]
-    rows = q_ref.shape[0]
-    kv_heads = k_ref.shape[1] // HD
-    count = reach + 1
-    first = first_ref[0]
-    scale = HD**-0.5 * math.log2(math.e)
+def prepare_kernel(lengths_ref, freq_ref, q_ref, k_ref, *refs, reach):
+    cos_ref, sin_ref, query_ref, key_ref = refs
+    rows = k_ref.shape[0]
+    first = lax.axis_index("tok") * rows
     lane = lax.broadcasted_iota(jnp.int32, (rows, HD), 1)
     sub = lax.broadcasted_iota(jnp.int32, (rows, HD), 0)
     freq = freq_ref[...]
-    cosines, sines = [], []
-    for n in range(count):
+    for n in range(reach + 1):
         index = first - (reach - n) * rows + sub
         start = doc_start(index, lengths_ref)
         sine, cosine = sine_cosine((index - start).astype(jnp.float32) * freq)
-        cosines.append(cosine)
-        sines.append(jnp.where(lane < HD // 2, -sine, sine))
+        sine = jnp.where(lane < HD // 2, -sine, sine)
+        if n < reach:
+            cos_ref[n * rows : (n + 1) * rows, :] = cosine
+            sin_ref[n * rows : (n + 1) * rows, :] = sine
+    for source, target in ((q_ref, query_ref), (k_ref, key_ref)):
+        for h in range(source.shape[1] // HD):
+            at = slice(h * HD, (h + 1) * HD)
+            target[:, at] = turn(source[:, at], cosine, sine)
+
+
+def attention_kernel(lengths_ref, cos_ref, sin_ref, q_ref, k_ref, v_ref, *refs, reach):
+    far, (out_ref, score_ref, weight_ref) = refs[:reach], refs[reach:]
+    rows = k_ref.shape[0]
+    kv_heads = k_ref.shape[1] // HD
+    group = q_ref.shape[1] // k_ref.shape[1]
+    count = reach + 1
+    first = lax.axis_index("tok") * rows
+    scale = HD**-0.5 * math.log2(math.e)
     key_lane = lax.broadcasted_iota(jnp.int32, (rows, rows), 1)
     key_sub = lax.broadcasted_iota(jnp.int32, (rows, rows), 0)
     starts = doc_start(first + key_sub, lengths_ref)
@@ -90,26 +103,25 @@
     for g in range(kv_heads):
         at = slice(g * HD, (g + 1) * HD)
         at_v = slice((kv_heads + g) * HD, (kv_heads + g + 1) * HD)
-        keys = [turn(far[reach - n - 1][:, at], cosines[n], sines[n]) for n in range(reach)]
-        keys = jnp.concatenate(keys + [turn(k_ref[:, at], cosines[reach], sines[reach])], axis=0)
+        keys = []
+        for n in range(reach):
+            part = slice(n * rows, (n + 1) * rows)
+            keys.append(turn(far[reach - n - 1][:, at], cos_ref[part, :], sin_ref[part, :]))
+        keys = jnp.concatenate(keys + [k_ref[:, at]], axis=0)
         vals = jnp.concatenate(
             [far[reach - n - 1][:, at_v] for n in range(reach)] + [v_ref[:, at]], axis=0
         )
         query = jnp.concatenate(
-            [
-                turn(q_ref[:, h * HD : (h + 1) * HD], cosines[reach], sines[reach])
-                for h in range(g * group, (g + 1) * group)
-            ],
-            axis=0,
-        )
-        score_ref[...] = lax.dot_general(
+            [q_ref[:, h * HD : (h + 1) * HD] for h in range(g * group, (g + 1) * group)], axis=0
+        )
+        score_ref[g] = lax.dot_general(
             query, keys, (((1,), (1,)), ((), ())), preferred_element_type=jnp.float32
         )
         totals = []
         for h in range(group):
             band = slice(h * rows, (h + 1) * rows)
             masked = [
-                jnp.where(seen[n], score_ref[band, n * rows : (n + 1) * rows] * scale, NEG_FILL)
+                jnp.where(seen[n], score_ref[g, band, n * rows : (n + 1) * rows] * scale, NEG_FILL)
                 for n in range(count)
             ]
             top = masked[0]
@@ -120,42 +132,55 @@
             for n in range(count):
                 w = jnp.exp2(masked[n] - top)
                 total = w if total is None else total + w
-                weight_ref[band, n * rows : (n + 1) * rows] = w.astype(jnp.bfloat16)
+                weight_ref[g, band, n * rows : (n + 1) * rows] = w.astype(jnp.bfloat16)
             totals.append(jnp.sum(total, axis=1, keepdims=True))
-        update = jnp.dot(weight_ref[...], vals, preferred_element_type=jnp.float32)
+        update = jnp.dot(weight_ref[g], vals, preferred_element_type=jnp.float32)
         for h in range(group):
             piece = update[h * rows : (h + 1) * rows, :] / totals[h]
             head = g * group + h
             out_ref[:, head * HD : (head + 1) * HD] = piece.astype(jnp.bfloat16)
-            copy_ref[:, head * HD : (head + 1) * HD] = piece.astype(jnp.bfloat16)
 
 
 def attend_near(queries, keys, values, doc_lengths, reach, n_tok):
     rows = queries.shape[0]
+    kv_heads = keys.shape[1] // HD
     group = queries.shape[1] // keys.shape[1]
     both = jnp.concatenate([keys, values], axis=1)
     far = []
     for d in range(1, reach + 1):
         far.append(lax.ppermute(both, "tok", [(i, i + d) for i in range(n_tok - d)]))
-    first = (lax.axis_index("tok") * rows).astype(jnp.int32).reshape(1)
-    half = jnp.arange(HD, dtype=jnp.float32) % (HD // 2)
-    freq = (ROPE_BASE ** (-(half * 2.0 / HD))).reshape(1, HD)
+    half = np.arange(HD, dtype=np.float32) % (HD // 2)
+    freq = jnp.asarray((ROPE_BASE ** (-(half * 2.0 / HD))).astype(np.float32).reshape(1, HD))
     vmem = pl.BlockSpec(memory_space=pltpu.VMEM)
     smem = pl.BlockSpec(memory_space=pltpu.SMEM)
     span = (reach + 1) * rows
-    attended = pl.pallas_call(
-        partial(attention_kernel, reach=reach, group=group),
-        out_shape=(pltpu.VMEM(queries.shape, jnp.bfloat16),) * 2,
-        in_specs=[smem, smem] + [vmem] * (4 + reach),
-        out_specs=(vmem, vmem),
+    whole = pltpu.VMEM(queries.shape, jnp.bfloat16)
+    settings = pltpu.CompilerParams(vmem_limit_bytes=KERNEL_BYTES)
+    cosine, sine, query, key = pl.pallas_call(
+        partial(prepare_kernel, reach=reach),
+        out_shape=(
+            pltpu.VMEM((reach * rows, HD), jnp.float32),
+            pltpu.VMEM((reach * rows, HD), jnp.float32),
+            whole,
+            pltpu.VMEM(keys.shape, jnp.bfloat16),
+        ),
+        in_specs=[smem] + [vmem] * 3,
+        out_specs=(vmem,) * 4,
+        compiler_params=settings,
+        name="prepare",
+    )(doc_lengths, freq, *on_chip(queries, keys))
+    return pl.pallas_call(
+        partial(attention_kernel, reach=reach),
+        out_shape=whole,
+        in_specs=[smem] + [vmem] * (5 + reach),
+        out_specs=vmem,
         scratch_shapes=[
-            pltpu.VMEM((group * rows, span), jnp.float32),
-            pltpu.VMEM((group * rows, span), jnp.bfloat16),
+            pltpu.VMEM((kv_heads, group * rows, span), jnp.float32),
+            pltpu.VMEM((kv_heads, group * rows, span), jnp.bfloat16),
         ],
-        compiler_params=pltpu.CompilerParams(vmem_limit_bytes=KERNEL_BYTES),
+        compiler_params=settings,
         name="attention",
-    )(first, doc_lengths, freq, *on_chip(queries, keys, values, *far))
-    return *attended, far
+    )(doc_lengths, *on_chip(cosine, sine, query, key, values, *far))
 
 
 def rotary(tensor, positions):
@@ -214,53 +239,35 @@
     )
     _, totals, weighted = lax.fori_loop(0, all_k.shape[0] // step, one_block, state)
     output = (weighted / totals[..., None]).transpose(2, 0, 1, 3)
-    output = output.reshape(rows, heads * HD).astype(jnp.bfloat16)
-    return output, output, all_v[0]
-
-
-def columns(left, weights, flip):
+    return output.reshape(rows, heads * HD).astype(jnp.bfloat16)
+
+
+def project_kernel(own_ref, mate_ref, *refs, inner):
+    half = (len(refs) - 1) // 2
+    out_ref = refs[-1]
     pieces = []
-    for w in weights:
-        piece = jnp.dot(left, w[...], preferred_element_type=jnp.float32)
-        pieces.append(piece.astype(jnp.bfloat16))
-    if len(pieces) == 1:
-        return pieces[0]
+    for own_w, mate_w in zip(refs[:half], refs[half:-1]):
+        own = jnp.dot(own_ref[...], own_w[...], preferred_element_type=jnp.float32)
+        mate = jnp.dot(mate_ref[...], mate_w[...], preferred_element_type=jnp.float32)
+        own, mate = (p.astype(jnp.bfloat16).astype(jnp.float32) for p in (own, mate))
+        pieces.append((own + mate).astype(jnp.bfloat16))
     straight = jnp.concatenate(pieces, axis=1)
-    return jnp.where(flip == 0, straight, jnp.concatenate(pieces[::-1], axis=1))
-
-
-def near_kernel(place_ref, own_ref, mate_ref, *refs, sides):
-    weights, (first_ref, second_ref) = refs[:sides], refs[sides : sides + 2]
-    rows = own_ref.shape[0]
-    left = jnp.concatenate([own_ref[...], mate_ref[...]], axis=0)
-    result = columns(left, weights, place_ref[0])
-    own, mate = result[:rows], result[rows:]
-    first_ref[...] = jnp.where(place_ref[1] == 0, own, mate)
-    second_ref[...] = jnp.where(place_ref[1] == 0, mate, own)
-
-
-def away_kernel(place_ref, near_ref, far_ref, *refs, sides):
-    weights, (keep_ref, send_ref) = refs[:sides], refs[sides : sides + 2]
-    result = columns(far_ref[...], weights, place_ref[0])
-    keep_ref[...] = jnp.where(place_ref[2] == 0, near_ref[...], result)
-    send_ref[...] = jnp.where(place_ref[2] == 0, result, near_ref[...])
-
-
-def project(kernel, place, left, weights):
-    rows, width = left[0].shape[0], sum(w.shape[1] for w in weights)
+    if half > 1:
+        flip = lax.rem(lax.axis_index("tok"), inner)
+        straight = jnp.where(flip == 0, straight, jnp.concatenate(pieces[::-1], axis=1))
+    out_ref[...] = straight
+
+
+def project(inner, own, mate, own_weights, mate_weights):
     vmem = pl.BlockSpec(memory_space=pltpu.VMEM)
-    outs = [pltpu.VMEM((rows, width), jnp.bfloat16)] * 2
-    outs += [pltpu.VMEM(w.shape, w.dtype) for w in weights]
-    begin = 1 + len(left)
-    first, second, *weights = pl.pallas_call(
-        partial(kernel, sides=len(weights)),
-        out_shape=tuple(outs),
-        in_specs=[pl.BlockSpec(memory_space=pltpu.SMEM)] + [vmem] * (len(left) + len(weights)),
-        out_specs=(vmem,) * len(outs),
-        input_output_aliases={begin + n: 2 + n for n in range(len(weights))},
+    operands = on_chip(own, mate, *own_weights, *mate_weights)
+    return pl.pallas_call(
+        partial(project_kernel, inner=inner),
+        out_shape=pltpu.VMEM((own.shape[0], sum(w.shape[1] for w in own_weights)), jnp.bfloat16),
+        in_specs=[vmem] * len(operands),
+        out_specs=vmem,
         compiler_params=pltpu.CompilerParams(vmem_limit_bytes=KERNEL_BYTES),
-    )(place, *on_chip(*left, *weights))
-    return first, second, weights
+    )(*operands)
 
 
 def solution(mesh):
@@ -286,15 +293,12 @@
 
     def shards(queries, keys, values, out_weight, doc_lengths):
         rows = queries.shape[0]
-        me, feat = lax.axis_index("tok"), lax.axis_index("feat")
-        x = me % inner
         longest = n_tok * rows * LONGEST[0] // LONGEST[1]
         reach = min(n_tok - 1, -(-(longest - 1) // rows))
         if reach <= FAR_BLOCKS:
-            attended, own, seen = attend_near(queries, keys, values, doc_lengths, reach, n_tok)
+            attended = attend_near(queries, keys, values, doc_lengths, reach, n_tok)
         else:
-            attended, own, seen = attend_far(queries, keys, values, doc_lengths)
-        out_weight, _ = lax.optimization_barrier((out_weight, seen))
+            attended = attend_far(queries, keys, values, doc_lengths)
         if inner == 2:
             weights = [out_weight, permute(out_weight, lambda z, x, j: (z, 1 - x, j))]
         else:
@@ -304,20 +308,22 @@
                     out_weight, "tok", axis=1, tiled=True, axis_index_groups=groups
                 )
             ]
-        mate = permute(attended, lambda z, x, j: (z ^ 1, x, j))
-        away = []
-        for k in range(2):
-            away.append(
-                permute(attended, lambda z, x, j: (z ^ (2 | ((j >> 1) ^ k)), x, j))
-            )
-        place = jnp.stack([x, feat >> 1, feat & 1]).astype(jnp.int32)
-        *near, weights = project(near_kernel, place, [own, mate], weights)
+        mate_weights = []
+        for w in weights:
+            mate_weights.append(permute(w, lambda z, x, j: (z, x, j ^ 1)))
+
+        def deliver(k, cross):
+            def move(z, x, j):
+                core = (j & 1) ^ cross
+                return (z ^ (core * 2 | ((j >> 1) ^ k)), x, (j & 2) | core)
+
+            return permute(attended, move)
+
         home = []
         for k in range(2):
-            keep, send, weights = project(away_kernel, place, [near[k], away[k]], weights)
-            other = permute(send, lambda z, x, j: (z, x, j ^ 1))
-            both = (keep.astype(jnp.float32) + other.astype(jnp.float32)).astype(jnp.bfloat16)
-            home.append(permute(both, lambda z, x, j: (z ^ ((j & 1) * 2 + ((j >> 1) ^ k)), x, z)))
+            own, mate = deliver(k, 0), deliver(k, 1)
+            mixed = project(inner, own, mate, weights, mate_weights)
+            home.append(permute(mixed, lambda z, x, j: (z ^ ((j & 1) * 2 + ((j >> 1) ^ k)), x, z)))
         return (home[0].astype(jnp.float32) + home[1].astype(jnp.float32)).astype(jnp.bfloat16)
 
     in_specs = (P("tok", "feat"), P("tok", "feat"), P("tok", "feat"), P("feat", "tok"), P())

time: 79.4 us -> 96 us (1.21)
  the two profiles are of different devices: /device:TPU:1 before, /device:TPU:7 now
where the time goes in v3:
time: 96 us; the launch traced here: 95.6 us
  waiting for transfers between devices  50.5 us (53%)
  starting transfers between devices  36.8 us (38%)
  Pallas kernels  5.54 us (6%)
  local copies, waits for them, and re-layouts  1.82 us (2%)
    ppermute x9, waiting for transfers between devices, permute(): return lax.ppermute(array, ('tok', 'feat'), everyone(move))  49.5 us
    ppermute x9, starting transfers between devices, permute(): return lax.ppermute(array, ('tok', 'feat'), everyone(move))  21.7 us
    ppermute x5, starting transfers between devices, attend_near(): lax.ppermute(both, 'tok', [(i, i + d) for i in range(n_tok - d)])  15.1 us
    pallas_call x1, Pallas kernels, attend_near(): pl.pallas_call(partial(attention_kernel, reach=reach), out_shape=whole, i...  2.62 us
  transfers between devices with their start and end apart: 14, of which 7 were waited for; matrix products, arithmetic and copies ran while one was open for 1% of the time, Pallas kernels for 6%

profile of v3, /device:TPU:7, one launch (start us, length us, event | category | flops | bytes accessed | tf_op | source)
XLA Modules:
  0.0 95.6 jit_solution(9446437683309608117)
XLA Ops:
  0.0 0.3 collective-permute-start.7
  0.3 1.0 collective-permute-start.8
  1.2 23.0 %collective-permute-done.7.refs_1_ = bf16[1024,512]{1,0:T(8,128)(2,1)S(1)} collective-permute-done((bf16[1024,512]{1,0:T(8,128)(2,1)}, bf16[1024,512]{1,0:T(8,128)(2,1)S(1)}, u32[]{:S(2)}, u32[]{:S(2)}) %collective-permute-start.7) | collective-permute-done | bytes 1048608 | tf_op jit(solution)/shard_map/ppermute | solution.py:292
  24.3 1.5 %collective-permute-start.9 = (bf16[1024,512]{1,0:T(8,128)(2,1)S(1)}, bf16[1024,512]{1,0:T(8,128)(2,1)S(1)}, u32[]{:S(2)}, u32[]{:S(2)}) collective-permute-start(bf16[1024,512]{1,0:T(8,128)(2,1)S(1)} %collective-permute-done.7.refs_1_), channel_id=1, source_target_pairs={{0,1},{1,0},{2,3},{3,2},{4,5},{5,4},{6,7},{7,6},{8,9},{9,8},{10,11... | collective-permute-start | bytes 3145736 | tf_op jit(solution)/shard_map/ppermute | solution.py:292
  25.8 0.8 constant_dynamic-update-slice_fusion.1
  26.6 0.0 copy-start.4
  26.7 0.0 copy-start.5
  26.7 3.3 %collective-permute-start = (bf16[128,512]{1,0:T(8,128)(2,1)S(1)}, bf16[128,512]{1,0:T(8,128)(2,1)S(1)}, u32[]{:S(2)}, u32[]{:S(2)}) collective-permute-start(bf16[128,512]{1,0:T(8,128)(2,1)S(1)} %constant_dynamic-update-slice_fusion), channel_id=1, source_target_pairs={{0,4},{4,8},{8,12},{12,16},{16,20},{20,24},{24,28},{1,5},{5,9},{9,... | collective-permute-start | bytes 393224 | tf_op jit(solution)/shard_map/ppermute | solution.py:151
  30.0 3.2 %collective-permute-start.1 = (bf16[128,512]{1,0:T(8,128)(2,1)S(1)}, bf16[128,512]{1,0:T(8,128)(2,1)S(1)}, u32[]{:S(2)}, u32[]{:S(2)}) collective-permute-start(bf16[128,512]{1,0:T(8,128)(2,1)S(1)} %constant_dynamic-update-slice_fusion), channel_id=1, source_target_pairs={{0,8},{4,12},{8,16},{12,20},{16,24},{20,28},{1,9},{5,13},{9,17},{1... | collective-permute-start | bytes 393224 | tf_op jit(solution)/shard_map/ppermute | solution.py:151
  33.2 4.1 %collective-permute-start.2 = (bf16[128,512]{1,0:T(8,128)(2,1)S(1)}, bf16[128,512]{1,0:T(8,128)(2,1)S(1)}, u32[]{:S(2)}, u32[]{:S(2)}) collective-permute-start(bf16[128,512]{1,0:T(8,128)(2,1)S(1)} %constant_dynamic-update-slice_fusion), channel_id=1, source_target_pairs={{0,12},{4,16},{8,20},{12,24},{16,28},{1,13},{5,17},{9,21},{13,25},... | collective-permute-start | bytes 393224 | tf_op jit(solution)/shard_map/ppermute | solution.py:151
  37.4 1.3 %collective-permute-start.3 = (bf16[128,512]{1,0:T(8,128)(2,1)S(1)}, bf16[128,512]{1,0:T(8,128)(2,1)S(1)}, u32[]{:S(2)}, u32[]{:S(2)}) collective-permute-start(bf16[128,512]{1,0:T(8,128)(2,1)S(1)} %constant_dynamic-update-slice_fusion), channel_id=1, source_target_pairs={{0,16},{4,20},{8,24},{12,28},{1,17},{5,21},{9,25},{13,29},{2,18},{... | collective-permute-start | bytes 393224 | tf_op jit(solution)/shard_map/ppermute | solution.py:151
  38.7 3.1 %collective-permute-start.4 = (bf16[128,512]{1,0:T(8,128)(2,1)S(1)}, bf16[128,512]{1,0:T(8,128)(2,1)S(1)}, u32[]{:S(2)}, u32[]{:S(2)}) collective-permute-start(bf16[128,512]{1,0:T(8,128)(2,1)S(1)} %constant_dynamic-update-slice_fusion), channel_id=1, source_target_pairs={{0,20},{4,24},{8,28},{1,21},{5,25},{9,29},{2,22},{6,26},{10,30},{3... | collective-permute-start | bytes 393224 | tf_op jit(solution)/shard_map/ppermute | solution.py:151
  41.8 0.0 copy-start.1
  41.8 0.9 copy-done.1
  42.8 1.4 %prepare.1 = (f32[640,128]{1,0:T(8,128)S(1)}, f32[640,128]{1,0:T(8,128)S(1)}, bf16[128,1024]{1,0:T(8,128)(2,1)S(1)}, bf16[128,256]{1,0:T(8,128)(2,1)S(1)}) custom-call(s32[6]{0:T(128)S(1)} %copy-done.4, f32[1,128]{1,0:T(1,128)S(1)} %copy-done.5, bf16[128,1024]{1,0:T(8,128)(2,1)S(1)} %copy-done.1, bf16[128,256]{1,0:T(8,128)(2,1)S(1)} %copy-done.2), custom_call_target="tpu_custom_call" | custom-call | tf_op jit(solution)/shard_map/prepare/pallas_call | solution.py:159
  44.2 0.0 copy-start
  44.2 0.9 collective-permute-done.4.refs_4_
  45.2 2.6 %attention.1 = bf16[128,1024]{1,0:T(8,128)(2,1)S(1)} custom-call(s32[6]{0:T(128)S(1)} %copy-done.4, f32[640,128]{1,0:T(8,128)S(1)} %get-tuple-element.9.cos_ref, f32[640,128]{1,0:T(8,128)S(1)} %get-tuple-element.10.sin_ref, bf16[128,1024]{1,0:T(8,128)(2,1)S(1)} %get-tuple-element.11.q_ref, bf16[128,256]{1,0:T(8,128)(2,1)S(1)} %get-tuple-element.12.k_ref, ...), custom_call_target="tpu_custom_call" | custom-call | tf_op jit(solution)/shard_map/attention/pallas_call | solution.py:172
  47.8 10.8 %collective-permute-start.5 = (bf16[128,1024]{1,0:T(8,128)(2,1)S(1)}, bf16[128,1024]{1,0:T(8,128)(2,1)S(1)}, u32[]{:S(2)}, u32[]{:S(2)}) collective-permute-start(bf16[128,1024]{1,0:T(8,128)(2,1)S(1)} %attention.1), channel_id=1, source_target_pairs={{0,0},{1,17},{2,10},{3,27},{4,4},{5,21},{6,14},{7,31},{8,8},{9,25}... | collective-permute-start | bytes 786440 | tf_op jit(solution)/shard_map/ppermute | solution.py:292
  58.6 0.1 collective-permute-start.6
  58.7 3.1 %collective-permute-start.11 = (bf16[128,1024]{1,0:T(8,128)(2,1)S(1)}, bf16[128,1024]{1,0:T(8,128)(2,1)S(1)}, u32[]{:S(2)}, u32[]{:S(2)}) collective-permute-start(bf16[128,1024]{1,0:T(8,128)(2,1)S(1)} %attention.1), channel_id=1, source_target_pairs={{0,8},{1,25},{2,2},{3,19},{4,12},{5,29},{6,6},{7,23},{8,0},{9,17},... | collective-permute-start | bytes 786440 | tf_op jit(solution)/shard_map/ppermute | solution.py:292
  61.8 3.0 %collective-permute-done.5.own_ref = bf16[128,1024]{1,0:T(8,128)(2,1)S(1)} collective-permute-done((bf16[128,1024]{1,0:T(8,128)(2,1)S(1)}, bf16[128,1024]{1,0:T(8,128)(2,1)S(1)}, u32[]{:S(2)}, u32[]{:S(2)}) %collective-permute-start.5) | collective-permute-done | bytes 262176 | tf_op jit(solution)/shard_map/ppermute | solution.py:292
  64.8 1.2 %collective-permute-start.12 = (bf16[128,1024]{1,0:T(8,128)(2,1)S(1)}, bf16[128,1024]{1,0:T(8,128)(2,1)S(1)}, u32[]{:S(2)}, u32[]{:S(2)}) collective-permute-start(bf16[128,1024]{1,0:T(8,128)(2,1)S(1)} %attention.1), channel_id=1, source_target_pairs={{0,25},{1,8},{2,19},{3,2},{4,29},{5,12},{6,23},{7,6},{8,17},{9,0},... | collective-permute-start | bytes 786440 | tf_op jit(solution)/shard_map/ppermute | solution.py:292
  66.0 6.1 %collective-permute-done.6.mate_ref = bf16[128,1024]{1,0:T(8,128)(2,1)S(1)} collective-permute-done((bf16[128,1024]{1,0:T(8,128)(2,1)S(1)}, bf16[128,1024]{1,0:T(8,128)(2,1)S(1)}, u32[]{:S(2)}, u32[]{:S(2)}) %collective-permute-start.6) | collective-permute-done | bytes 262176 | tf_op jit(solution)/shard_map/ppermute | solution.py:292
  72.1 0.8 shard_map.64
  72.8 1.9 %collective-permute-start.10 = (bf16[128,1024]{1,0:T(8,128)(2,1)S(1)}, bf16[128,1024]{1,0:T(8,128)(2,1)S(1)}, u32[]{:S(2)}, u32[]{:S(2)}) collective-permute-start(bf16[128,1024]{1,0:T(8,128)(2,1)S(1)} %shard_map.64), channel_id=1, source_target_pairs={{0,0},{1,16},{2,8},{3,24},{4,4},{5,20},{6,12},{7,28},{8,9},{9,25},... | collective-permute-start | bytes 786440 | tf_op jit(solution)/shard_map/ppermute | solution.py:292
  74.8 0.4 collective-permute-done.11.own_ref
  75.2 9.0 %collective-permute-done.12.mate_ref = bf16[128,1024]{1,0:T(8,128)(2,1)S(1)} collective-permute-done((bf16[128,1024]{1,0:T(8,128)(2,1)S(1)}, bf16[128,1024]{1,0:T(8,128)(2,1)S(1)}, u32[]{:S(2)}, u32[]{:S(2)}) %collective-permute-start.12) | collective-permute-done | bytes 262176 | tf_op jit(solution)/shard_map/ppermute | solution.py:292
  84.2 0.7 shard_map.65
  84.9 1.9 %collective-permute-start.13 = (bf16[128,1024]{1,0:T(8,128)(2,1)S(1)}, bf16[128,1024]{1,0:T(8,128)(2,1)S(1)}, u32[]{:S(2)}, u32[]{:S(2)}) collective-permute-start(bf16[128,1024]{1,0:T(8,128)(2,1)S(1)} %shard_map.65), channel_id=1, source_target_pairs={{0,8},{1,24},{2,0},{3,16},{4,12},{5,28},{6,4},{7,20},{8,1},{9,17},... | collective-permute-start | bytes 786440 | tf_op jit(solution)/shard_map/ppermute | solution.py:292
  86.9 8.0 %collective-permute-done.13 = bf16[128,1024]{1,0:T(8,128)(2,1)S(1)} collective-permute-done((bf16[128,1024]{1,0:T(8,128)(2,1)S(1)}, bf16[128,1024]{1,0:T(8,128)(2,1)S(1)}, u32[]{:S(2)}, u32[]{:S(2)}) %collective-permute-start.13) | collective-permute-done | bytes 262176 | tf_op jit(solution)/shard_map/ppermute | solution.py:292
  94.8 0.8 add_convert_fusion
  (15 shorter events, 0.0 us)
Async XLA Ops:
  0.0 26.6 %copy-start.3 = (bf16[128,256]{1,0:T(8,128)(2,1)S(1)}, bf16[128,256]{1,0:T(8,128)(2,1)}, u32[]{:S(2)}) copy-start(bf16[128,256]{1,0:T(8,128)(2,1)} %v_ref.1) | copy-start | bytes 196612
  0.0 24.3 %collective-permute-start.7 = (bf16[1024,512]{1,0:T(8,128)(2,1)}, bf16[1024,512]{1,0:T(8,128)(2,1)S(1)}, u32[]{:S(2)}, u32[]{:S(2)}) collective-permute-start(bf16[1024,512]{1,0:T(8,128)(2,1)} %refs_0_.3), channel_id=1, source_target_pairs={{0,4},{1,5},{2,6},{3,7},{4,0},{5,1},{6,2},{7,3},{8,12},{9,13},{10,... | collective-permute-start | bytes 3145736 | tf_op jit(solution)/shard_map/ppermute | solution.py:292
  0.3 71.8 %collective-permute-start.8 = (bf16[1024,512]{1,0:T(8,128)(2,1)}, bf16[1024,512]{1,0:T(8,128)(2,1)S(1)}, u32[]{:S(2)}, u32[]{:S(2)}) collective-permute-start(bf16[1024,512]{1,0:T(8,128)(2,1)} %refs_0_.3), channel_id=1, source_target_pairs={{0,1},{1,0},{2,3},{3,2},{4,5},{5,4},{6,7},{7,6},{8,9},{9,8},{10,11... | collective-permute-start | bytes 3145736 | tf_op jit(solution)/shard_map/ppermute | solution.py:292
  24.3 47.8 %collective-permute-start.9 = (bf16[1024,512]{1,0:T(8,128)(2,1)S(1)}, bf16[1024,512]{1,0:T(8,128)(2,1)S(1)}, u32[]{:S(2)}, u32[]{:S(2)}) collective-permute-start(bf16[1024,512]{1,0:T(8,128)(2,1)S(1)} %collective-permute-done.7.refs_1_), channel_id=1, source_target_pairs={{0,1},{1,0},{2,3},{3,2},{4,5},{5,4},{6,7},{7,6},{8,9},{9,8},{10,11... | collective-permute-start | bytes 3145736 | tf_op jit(solution)/shard_map/ppermute | solution.py:292
  26.6 15.2 %copy-start.2 = (bf16[128,256]{1,0:T(8,128)(2,1)S(1)}, bf16[128,256]{1,0:T(8,128)(2,1)}, u32[]{:S(2)}) copy-start(bf16[128,256]{1,0:T(8,128)(2,1)} %k_ref.1) | copy-start | bytes 196612
  26.6 15.2 %copy-start.4 = (s32[6]{0:T(128)S(1)}, s32[6]{0:T(128)}, u32[]{:S(2)}) copy-start(s32[6]{0:T(128)} %lengths_ref.3) | copy-start | bytes 76
  26.7 15.2 %copy-start.5 = (f32[1,128]{1,0:T(1,128)S(1)}, f32[1,128]{1,0:T(1,128)}, u32[]{:S(2)}) copy-start(f32[1,128]{1,0:T(1,128)} %constant.2.clone.freq_ref) | copy-start | bytes 1540
  26.7 10.7 %collective-permute-start = (bf16[128,512]{1,0:T(8,128)(2,1)S(1)}, bf16[128,512]{1,0:T(8,128)(2,1)S(1)}, u32[]{:S(2)}, u32[]{:S(2)}) collective-permute-start(bf16[128,512]{1,0:T(8,128)(2,1)S(1)} %constant_dynamic-update-slice_fusion), channel_id=1, source_target_pairs={{0,4},{4,8},{8,12},{12,16},{16,20},{20,24},{24,28},{1,5},{5,9},{9,... | collective-permute-start | bytes 393224 | tf_op jit(solution)/shard_map/ppermute | solution.py:151
  30.0 8.7 %collective-permute-start.1 = (bf16[128,512]{1,0:T(8,128)(2,1)S(1)}, bf16[128,512]{1,0:T(8,128)(2,1)S(1)}, u32[]{:S(2)}, u32[]{:S(2)}) collective-permute-start(bf16[128,512]{1,0:T(8,128)(2,1)S(1)} %constant_dynamic-update-slice_fusion), channel_id=1, source_target_pairs={{0,8},{4,12},{8,16},{12,20},{16,24},{20,28},{1,9},{5,13},{9,17},{1... | collective-permute-start | bytes 393224 | tf_op jit(solution)/shard_map/ppermute | solution.py:151
  33.2 11.0 %collective-permute-start.2 = (bf16[128,512]{1,0:T(8,128)(2,1)S(1)}, bf16[128,512]{1,0:T(8,128)(2,1)S(1)}, u32[]{:S(2)}, u32[]{:S(2)}) collective-permute-start(bf16[128,512]{1,0:T(8,128)(2,1)S(1)} %constant_dynamic-update-slice_fusion), channel_id=1, source_target_pairs={{0,12},{4,16},{8,20},{12,24},{16,28},{1,13},{5,17},{9,21},{13,25},... | collective-permute-start | bytes 393224 | tf_op jit(solution)/shard_map/ppermute | solution.py:151
  37.4 6.9 %collective-permute-start.3 = (bf16[128,512]{1,0:T(8,128)(2,1)S(1)}, bf16[128,512]{1,0:T(8,128)(2,1)S(1)}, u32[]{:S(2)}, u32[]{:S(2)}) collective-permute-start(bf16[128,512]{1,0:T(8,128)(2,1)S(1)} %constant_dynamic-update-slice_fusion), channel_id=1, source_target_pairs={{0,16},{4,20},{8,24},{12,28},{1,17},{5,21},{9,25},{13,29},{2,18},{... | collective-permute-start | bytes 393224 | tf_op jit(solution)/shard_map/ppermute | solution.py:151
  38.7 6.5 %collective-permute-start.4 = (bf16[128,512]{1,0:T(8,128)(2,1)S(1)}, bf16[128,512]{1,0:T(8,128)(2,1)S(1)}, u32[]{:S(2)}, u32[]{:S(2)}) collective-permute-start(bf16[128,512]{1,0:T(8,128)(2,1)S(1)} %constant_dynamic-update-slice_fusion), channel_id=1, source_target_pairs={{0,20},{4,24},{8,28},{1,21},{5,25},{9,29},{2,22},{6,26},{10,30},{3... | collective-permute-start | bytes 393224 | tf_op jit(solution)/shard_map/ppermute | solution.py:151
  41.8 1.0 copy-start.1
  44.2 27.9 %copy-start = (bf16[1024,512]{1,0:T(8,128)(2,1)S(1)}, bf16[1024,512]{1,0:T(8,128)(2,1)}, u32[]{:S(2)}) copy-start(bf16[1024,512]{1,0:T(8,128)(2,1)} %refs_0_.3) | copy-start | bytes 3145732
  47.8 17.0 %collective-permute-start.5 = (bf16[128,1024]{1,0:T(8,128)(2,1)S(1)}, bf16[128,1024]{1,0:T(8,128)(2,1)S(1)}, u32[]{:S(2)}, u32[]{:S(2)}) collective-permute-start(bf16[128,1024]{1,0:T(8,128)(2,1)S(1)} %attention.1), channel_id=1, source_target_pairs={{0,0},{1,17},{2,10},{3,27},{4,4},{5,21},{6,14},{7,31},{8,8},{9,25}... | collective-permute-start | bytes 786440 | tf_op jit(solution)/shard_map/ppermute | solution.py:292
  58.6 13.4 %collective-permute-start.6 = (bf16[128,1024]{1,0:T(8,128)(2,1)S(1)}, bf16[128,1024]{1,0:T(8,128)(2,1)S(1)}, u32[]{:S(2)}, u32[]{:S(2)}) collective-permute-start(bf16[128,1024]{1,0:T(8,128)(2,1)S(1)} %attention.1), channel_id=1, source_target_pairs={{0,17},{1,0},{2,27},{3,10},{4,21},{5,4},{6,31},{7,14},{8,25},{9,8}... | collective-permute-start | bytes 786440 | tf_op jit(solution)/shard_map/ppermute | solution.py:292
  58.7 16.5 %collective-permute-start.11 = (bf16[128,1024]{1,0:T(8,128)(2,1)S(1)}, bf16[128,1024]{1,0:T(8,128)(2,1)S(1)}, u32[]{:S(2)}, u32[]{:S(2)}) collective-permute-start(bf16[128,1024]{1,0:T(8,128)(2,1)S(1)} %attention.1), channel_id=1, source_target_pairs={{0,8},{1,25},{2,2},{3,19},{4,12},{5,29},{6,6},{7,23},{8,0},{9,17},... | collective-permute-start | bytes 786440 | tf_op jit(solution)/shard_map/ppermute | solution.py:292
  64.8 19.4 %collective-permute-start.12 = (bf16[128,1024]{1,0:T(8,128)(2,1)S(1)}, bf16[128,1024]{1,0:T(8,128)(2,1)S(1)}, u32[]{:S(2)}, u32[]{:S(2)}) collective-permute-start(bf16[128,1024]{1,0:T(8,128)(2,1)S(1)} %attention.1), channel_id=1, source_target_pairs={{0,25},{1,8},{2,19},{3,2},{4,29},{5,12},{6,23},{7,6},{8,17},{9,0},... | collective-permute-start | bytes 786440 | tf_op jit(solution)/shard_map/ppermute | solution.py:292
  72.8 14.0 %collective-permute-start.10 = (bf16[128,1024]{1,0:T(8,128)(2,1)S(1)}, bf16[128,1024]{1,0:T(8,128)(2,1)S(1)}, u32[]{:S(2)}, u32[]{:S(2)}) collective-permute-start(bf16[128,1024]{1,0:T(8,128)(2,1)S(1)} %shard_map.64), channel_id=1, source_target_pairs={{0,0},{1,16},{2,8},{3,24},{4,4},{5,20},{6,12},{7,28},{8,9},{9,25},... | collective-permute-start | bytes 786440 | tf_op jit(solution)/shard_map/ppermute | solution.py:292
  84.9 9.9 %collective-permute-start.13 = (bf16[128,1024]{1,0:T(8,128)(2,1)S(1)}, bf16[128,1024]{1,0:T(8,128)(2,1)S(1)}, u32[]{:S(2)}, u32[]{:S(2)}) collective-permute-start(bf16[128,1024]{1,0:T(8,128)(2,1)S(1)} %shard_map.65), channel_id=1, source_target_pairs={{0,8},{1,24},{2,0},{3,16},{4,12},{5,28},{6,4},{7,20},{8,1},{9,17},... | collective-permute-start | bytes 786440 | tf_op jit(solution)/shard_map/ppermute | solution.py:292

commit v4 on v3

--- a/solution.py
+++ b/solution.py
@@ -242,27 +242,28 @@
     return output.reshape(rows, heads * HD).astype(jnp.bfloat16)
 
 
-def project_kernel(own_ref, mate_ref, *refs, inner):
-    half = (len(refs) - 1) // 2
-    out_ref = refs[-1]
+def project_kernel(own_ref, mate_ref, *refs, inner, sides, added):
+    weights, (*before, out_ref) = refs[: 2 * sides], refs[2 * sides :]
     pieces = []
-    for own_w, mate_w in zip(refs[:half], refs[half:-1]):
+    for own_w, mate_w in zip(weights[:sides], weights[sides:]):
         own = jnp.dot(own_ref[...], own_w[...], preferred_element_type=jnp.float32)
         mate = jnp.dot(mate_ref[...], mate_w[...], preferred_element_type=jnp.float32)
         own, mate = (p.astype(jnp.bfloat16).astype(jnp.float32) for p in (own, mate))
-        pieces.append((own + mate).astype(jnp.bfloat16))
+        pieces.append(own + mate)
     straight = jnp.concatenate(pieces, axis=1)
-    if half > 1:
+    if sides > 1:
         flip = lax.rem(lax.axis_index("tok"), inner)
         straight = jnp.where(flip == 0, straight, jnp.concatenate(pieces[::-1], axis=1))
-    out_ref[...] = straight
-
-
-def project(inner, own, mate, own_weights, mate_weights):
+    if added:
+        straight = straight + before[0][...].astype(jnp.float32)
+    out_ref[...] = straight.astype(jnp.bfloat16)
+
+
+def project(inner, own, mate, own_weights, mate_weights, before):
     vmem = pl.BlockSpec(memory_space=pltpu.VMEM)
-    operands = on_chip(own, mate, *own_weights, *mate_weights)
+    operands = on_chip(own, mate, *own_weights, *mate_weights, *before)
     return pl.pallas_call(
-        partial(project_kernel, inner=inner),
+        partial(project_kernel, inner=inner, sides=len(own_weights), added=len(before)),
         out_shape=pltpu.VMEM((own.shape[0], sum(w.shape[1] for w in own_weights)), jnp.bfloat16),
         in_specs=[vmem] * len(operands),
         out_specs=vmem,
@@ -319,12 +320,10 @@
 
             return permute(attended, move)
 
-        home = []
-        for k in range(2):
-            own, mate = deliver(k, 0), deliver(k, 1)
-            mixed = project(inner, own, mate, weights, mate_weights)
-            home.append(permute(mixed, lambda z, x, j: (z ^ ((j & 1) * 2 + ((j >> 1) ^ k)), x, z)))
-        return (home[0].astype(jnp.float32) + home[1].astype(jnp.float32)).astype(jnp.bfloat16)
+        lent = project(inner, deliver(1, 0), deliver(1, 1), weights, mate_weights, [])
+        lent = permute(lent, lambda z, x, j: (z, x, j ^ 2))
+        mixed = project(inner, deliver(0, 0), deliver(0, 1), weights, mate_weights, [lent])
+        return permute(mixed, lambda z, x, j: (z ^ ((j & 1) * 2 | (j >> 1)), x, z))
 
     in_specs = (P("tok", "feat"), P("tok", "feat"), P("tok", "feat"), P("feat", "tok"), P())
     return jax.shard_map(

time: 96 us -> 94.7 us (0.986)
  the two profiles are of different devices: /device:TPU:7 before, /device:TPU:1 now
where the time goes in v4:
time: 94.7 us; the launch traced here: 93.6 us
  starting transfers between devices  43.1 us (46%)
  waiting for transfers between devices  42.2 us (45%)
  Pallas kernels  5.59 us (6%)
  local copies, waits for them, and re-layouts  2.53 us (3%)
    ppermute x9, waiting for transfers between devices, permute(): return lax.ppermute(array, ('tok', 'feat'), everyone(move))  41.1 us
    ppermute x9, starting transfers between devices, permute(): return lax.ppermute(array, ('tok', 'feat'), everyone(move))  27.8 us
    ppermute x5, starting transfers between devices, attend_near(): lax.ppermute(both, 'tok', [(i, i + d) for i in range(n_tok - d)])  15.3 us
    pallas_call x1, Pallas kernels, attend_near(): pl.pallas_call(partial(attention_kernel, reach=reach), out_shape=whole, i...  2.62 us
    unnamed x14, local copies, waits for them, and re-layouts  2.52 us
  transfers between devices with their start and end apart: 14, of which 7 were waited for; matrix products, arithmetic and copies ran while one was open for 1% of the time, Pallas kernels for 5%

profile of v4, /device:TPU:1, one launch (start us, length us, event | category | flops | bytes accessed | tf_op | source)
XLA Modules:
  0.0 93.6 jit_solution(12911234193796883558)
XLA Ops:
  0.0 2.0 %collective-permute-start.7 = (bf16[1024,512]{1,0:T(8,128)(2,1)}, bf16[1024,512]{1,0:T(8,128)(2,1)S(1)}, u32[]{:S(2)}, u32[]{:S(2)}) collective-permute-start(bf16[1024,512]{1,0:T(8,128)(2,1)} %refs_0_.3), channel_id=1, source_target_pairs={{0,4},{1,5},{2,6},{3,7},{4,0},{5,1},{6,2},{7,3},{8,12},{9,13},{10,... | collective-permute-start | bytes 3145736 | tf_op jit(solution)/shard_map/ppermute | solution.py:293
  2.0 1.0 %collective-permute-start.8 = (bf16[1024,512]{1,0:T(8,128)(2,1)}, bf16[1024,512]{1,0:T(8,128)(2,1)S(1)}, u32[]{:S(2)}, u32[]{:S(2)}) collective-permute-start(bf16[1024,512]{1,0:T(8,128)(2,1)} %refs_0_.3), channel_id=1, source_target_pairs={{0,1},{1,0},{2,3},{3,2},{4,5},{5,4},{6,7},{7,6},{8,9},{9,8},{10,11... | collective-permute-start | bytes 3145736 | tf_op jit(solution)/shard_map/ppermute | solution.py:293
  3.0 22.1 %collective-permute-done.7.refs_1_ = bf16[1024,512]{1,0:T(8,128)(2,1)S(1)} collective-permute-done((bf16[1024,512]{1,0:T(8,128)(2,1)}, bf16[1024,512]{1,0:T(8,128)(2,1)S(1)}, u32[]{:S(2)}, u32[]{:S(2)}) %collective-permute-start.7) | collective-permute-done | bytes 1048608 | tf_op jit(solution)/shard_map/ppermute | solution.py:293
  25.1 1.3 %collective-permute-start.9 = (bf16[1024,512]{1,0:T(8,128)(2,1)S(1)}, bf16[1024,512]{1,0:T(8,128)(2,1)S(1)}, u32[]{:S(2)}, u32[]{:S(2)}) collective-permute-start(bf16[1024,512]{1,0:T(8,128)(2,1)S(1)} %collective-permute-done.7.refs_1_), channel_id=1, source_target_pairs={{0,1},{1,0},{2,3},{3,2},{4,5},{5,4},{6,7},{7,6},{8,9},{9,8},{10,11... | collective-permute-start | bytes 3145736 | tf_op jit(solution)/shard_map/ppermute | solution.py:293
  26.4 0.8 constant_dynamic-update-slice_fusion.1
  27.2 0.0 copy-start.4
  27.2 0.0 copy-start.5
  27.2 3.5 %collective-permute-start = (bf16[128,512]{1,0:T(8,128)(2,1)S(1)}, bf16[128,512]{1,0:T(8,128)(2,1)S(1)}, u32[]{:S(2)}, u32[]{:S(2)}) collective-permute-start(bf16[128,512]{1,0:T(8,128)(2,1)S(1)} %constant_dynamic-update-slice_fusion), channel_id=1, source_target_pairs={{0,4},{4,8},{8,12},{12,16},{16,20},{20,24},{24,28},{1,5},{5,9},{9,... | collective-permute-start | bytes 393224 | tf_op jit(solution)/shard_map/ppermute | solution.py:151
  30.8 3.2 %collective-permute-start.1 = (bf16[128,512]{1,0:T(8,128)(2,1)S(1)}, bf16[128,512]{1,0:T(8,128)(2,1)S(1)}, u32[]{:S(2)}, u32[]{:S(2)}) collective-permute-start(bf16[128,512]{1,0:T(8,128)(2,1)S(1)} %constant_dynamic-update-slice_fusion), channel_id=1, source_target_pairs={{0,8},{4,12},{8,16},{12,20},{16,24},{20,28},{1,9},{5,13},{9,17},{1... | collective-permute-start | bytes 393224 | tf_op jit(solution)/shard_map/ppermute | solution.py:151
  34.0 4.2 %collective-permute-start.2 = (bf16[128,512]{1,0:T(8,128)(2,1)S(1)}, bf16[128,512]{1,0:T(8,128)(2,1)S(1)}, u32[]{:S(2)}, u32[]{:S(2)}) collective-permute-start(bf16[128,512]{1,0:T(8,128)(2,1)S(1)} %constant_dynamic-update-slice_fusion), channel_id=1, source_target_pairs={{0,12},{4,16},{8,20},{12,24},{16,28},{1,13},{5,17},{9,21},{13,25},... | collective-permute-start | bytes 393224 | tf_op jit(solution)/shard_map/ppermute | solution.py:151
  38.2 1.9 %collective-permute-start.3 = (bf16[128,512]{1,0:T(8,128)(2,1)S(1)}, bf16[128,512]{1,0:T(8,128)(2,1)S(1)}, u32[]{:S(2)}, u32[]{:S(2)}) collective-permute-start(bf16[128,512]{1,0:T(8,128)(2,1)S(1)} %constant_dynamic-update-slice_fusion), channel_id=1, source_target_pairs={{0,16},{4,20},{8,24},{12,28},{1,17},{5,21},{9,25},{13,29},{2,18},{... | collective-permute-start | bytes 393224 | tf_op jit(solution)/shard_map/ppermute | solution.py:151
  40.1 2.5 %collective-permute-start.4 = (bf16[128,512]{1,0:T(8,128)(2,1)S(1)}, bf16[128,512]{1,0:T(8,128)(2,1)S(1)}, u32[]{:S(2)}, u32[]{:S(2)}) collective-permute-start(bf16[128,512]{1,0:T(8,128)(2,1)S(1)} %constant_dynamic-update-slice_fusion), channel_id=1, source_target_pairs={{0,20},{4,24},{8,28},{1,21},{5,25},{9,29},{2,22},{6,26},{10,30},{3... | collective-permute-start | bytes 393224 | tf_op jit(solution)/shard_map/ppermute | solution.py:151
  42.7 0.0 copy-start.1
  42.7 0.9 %copy-done.1 = bf16[128,1024]{1,0:T(8,128)(2,1)S(1)} copy-done((bf16[128,1024]{1,0:T(8,128)(2,1)S(1)}, bf16[128,1024]{1,0:T(8,128)(2,1)}, u32[]{:S(2)}) %copy-start.1) | copy-done | bytes 262168
  43.6 1.4 %prepare.1 = (f32[640,128]{1,0:T(8,128)S(1)}, f32[640,128]{1,0:T(8,128)S(1)}, bf16[128,1024]{1,0:T(8,128)(2,1)S(1)}, bf16[128,256]{1,0:T(8,128)(2,1)S(1)}) custom-call(s32[6]{0:T(128)S(1)} %copy-done.4, f32[1,128]{1,0:T(1,128)S(1)} %copy-done.5, bf16[128,1024]{1,0:T(8,128)(2,1)S(1)} %copy-done.1, bf16[128,256]{1,0:T(8,128)(2,1)S(1)} %copy-done.2), custom_call_target="tpu_custom_call" | custom-call | tf_op jit(solution)/shard_map/prepare/pallas_call | solution.py:159
  45.0 0.0 copy-start
  45.1 1.1 %collective-permute-done.4.refs_4_ = bf16[128,512]{1,0:T(8,128)(2,1)S(1)} collective-permute-done((bf16[128,512]{1,0:T(8,128)(2,1)S(1)}, bf16[128,512]{1,0:T(8,128)(2,1)S(1)}, u32[]{:S(2)}, u32[]{:S(2)}) %collective-permute-start.4) | collective-permute-done | bytes 131104 | tf_op jit(solution)/shard_map/ppermute | solution.py:151
  46.2 2.6 %attention.1 = bf16[128,1024]{1,0:T(8,128)(2,1)S(1)} custom-call(s32[6]{0:T(128)S(1)} %copy-done.4, f32[640,128]{1,0:T(8,128)S(1)} %get-tuple-element.9.cos_ref, f32[640,128]{1,0:T(8,128)S(1)} %get-tuple-element.10.sin_ref, bf16[128,1024]{1,0:T(8,128)(2,1)S(1)} %get-tuple-element.11.q_ref, bf16[128,256]{1,0:T(8,128)(2,1)S(1)} %get-tuple-element.12.k_ref, ...), custom_call_target="tpu_custom_call" | custom-call | tf_op jit(solution)/shard_map/attention/pallas_call | solution.py:172
  48.8 8.8 %collective-permute-start.10 = (bf16[128,1024]{1,0:T(8,128)(2,1)S(1)}, bf16[128,1024]{1,0:T(8,128)(2,1)S(1)}, u32[]{:S(2)}, u32[]{:S(2)}) collective-permute-start(bf16[128,1024]{1,0:T(8,128)(2,1)S(1)} %attention.1), channel_id=1, source_target_pairs={{0,8},{1,25},{2,2},{3,19},{4,12},{5,29},{6,6},{7,23},{8,0},{9,17},... | collective-permute-start | bytes 786440 | tf_op jit(solution)/shard_map/ppermute | solution.py:293
  57.6 0.1 collective-permute-start.11
  57.6 3.6 %collective-permute-start.5 = (bf16[128,1024]{1,0:T(8,128)(2,1)S(1)}, bf16[128,1024]{1,0:T(8,128)(2,1)S(1)}, u32[]{:S(2)}, u32[]{:S(2)}) collective-permute-start(bf16[128,1024]{1,0:T(8,128)(2,1)S(1)} %attention.1), channel_id=1, source_target_pairs={{0,0},{1,17},{2,10},{3,27},{4,4},{5,21},{6,14},{7,31},{8,8},{9,25}... | collective-permute-start | bytes 786440 | tf_op jit(solution)/shard_map/ppermute | solution.py:293
  61.3 1.9 %collective-permute-done.10.own_ref = bf16[128,1024]{1,0:T(8,128)(2,1)S(1)} collective-permute-done((bf16[128,1024]{1,0:T(8,128)(2,1)S(1)}, bf16[128,1024]{1,0:T(8,128)(2,1)S(1)}, u32[]{:S(2)}, u32[]{:S(2)}) %collective-permute-start.10) | collective-permute-done | bytes 262176 | tf_op jit(solution)/shard_map/ppermute | solution.py:293
  63.1 6.4 %collective-permute-start.6 = (bf16[128,1024]{1,0:T(8,128)(2,1)S(1)}, bf16[128,1024]{1,0:T(8,128)(2,1)S(1)}, u32[]{:S(2)}, u32[]{:S(2)}) collective-permute-start(bf16[128,1024]{1,0:T(8,128)(2,1)S(1)} %attention.1), channel_id=1, source_target_pairs={{0,17},{1,0},{2,27},{3,10},{4,21},{5,4},{6,31},{7,14},{8,25},{9,8}... | collective-permute-start | bytes 786440 | tf_op jit(solution)/shard_map/ppermute | solution.py:293
  69.5 2.0 %collective-permute-done.11.mate_ref = bf16[128,1024]{1,0:T(8,128)(2,1)S(1)} collective-permute-done((bf16[128,1024]{1,0:T(8,128)(2,1)S(1)}, bf16[128,1024]{1,0:T(8,128)(2,1)S(1)}, u32[]{:S(2)}, u32[]{:S(2)}) %collective-permute-start.11) | collective-permute-done | bytes 262176 | tf_op jit(solution)/shard_map/ppermute | solution.py:293
  71.6 0.8 shard_map.64
  72.3 0.1 collective-permute-start.12
  72.4 2.7 %collective-permute-done.5.own_ref = bf16[128,1024]{1,0:T(8,128)(2,1)S(1)} collective-permute-done((bf16[128,1024]{1,0:T(8,128)(2,1)S(1)}, bf16[128,1024]{1,0:T(8,128)(2,1)S(1)}, u32[]{:S(2)}, u32[]{:S(2)}) %collective-permute-start.5) | collective-permute-done | bytes 262176 | tf_op jit(solution)/shard_map/ppermute | solution.py:293
  75.2 5.7 %collective-permute-done.6.mate_ref = bf16[128,1024]{1,0:T(8,128)(2,1)S(1)} collective-permute-done((bf16[128,1024]{1,0:T(8,128)(2,1)S(1)}, bf16[128,1024]{1,0:T(8,128)(2,1)S(1)}, u32[]{:S(2)}, u32[]{:S(2)}) %collective-permute-start.6) | collective-permute-done | bytes 262176 | tf_op jit(solution)/shard_map/ppermute | solution.py:293
  80.9 0.8 shard_map.65
  81.7 4.6 %collective-permute-start.13 = (bf16[128,1024]{1,0:T(8,128)(2,1)S(1)}, bf16[128,1024]{1,0:T(8,128)(2,1)S(1)}, u32[]{:S(2)}, u32[]{:S(2)}) collective-permute-start(bf16[128,1024]{1,0:T(8,128)(2,1)S(1)} %shard_map.65), channel_id=1, source_target_pairs={{0,0},{1,16},{2,8},{3,24},{4,4},{5,20},{6,12},{7,28},{8,9},{9,25},... | collective-permute-start | bytes 786440 | tf_op jit(solution)/shard_map/ppermute | solution.py:293
  86.3 6.6 %collective-permute-done.13 = bf16[128,1024]{1,0:T(8,128)(2,1)S(1)} collective-permute-done((bf16[128,1024]{1,0:T(8,128)(2,1)S(1)}, bf16[128,1024]{1,0:T(8,128)(2,1)S(1)}, u32[]{:S(2)}, u32[]{:S(2)}) %collective-permute-start.13) | collective-permute-done | bytes 262176 | tf_op jit(solution)/shard_map/ppermute | solution.py:293
  92.9 0.7 copy.9
  (15 shorter events, 0.0 us)
Async XLA Ops:
  0.0 27.2 %copy-start.3 = (bf16[128,256]{1,0:T(8,128)(2,1)S(1)}, bf16[128,256]{1,0:T(8,128)(2,1)}, u32[]{:S(2)}) copy-start(bf16[128,256]{1,0:T(8,128)(2,1)} %v_ref.1) | copy-start | bytes 196612
  0.0 25.1 %collective-permute-start.7 = (bf16[1024,512]{1,0:T(8,128)(2,1)}, bf16[1024,512]{1,0:T(8,128)(2,1)S(1)}, u32[]{:S(2)}, u32[]{:S(2)}) collective-permute-start(bf16[1024,512]{1,0:T(8,128)(2,1)} %refs_0_.3), channel_id=1, source_target_pairs={{0,4},{1,5},{2,6},{3,7},{4,0},{5,1},{6,2},{7,3},{8,12},{9,13},{10,... | collective-permute-start | bytes 3145736 | tf_op jit(solution)/shard_map/ppermute | solution.py:293
  2.0 69.5 %collective-permute-start.8 = (bf16[1024,512]{1,0:T(8,128)(2,1)}, bf16[1024,512]{1,0:T(8,128)(2,1)S(1)}, u32[]{:S(2)}, u32[]{:S(2)}) collective-permute-start(bf16[1024,512]{1,0:T(8,128)(2,1)} %refs_0_.3), channel_id=1, source_target_pairs={{0,1},{1,0},{2,3},{3,2},{4,5},{5,4},{6,7},{7,6},{8,9},{9,8},{10,11... | collective-permute-start | bytes 3145736 | tf_op jit(solution)/shard_map/ppermute | solution.py:293
  25.1 46.5 %collective-permute-start.9 = (bf16[1024,512]{1,0:T(8,128)(2,1)S(1)}, bf16[1024,512]{1,0:T(8,128)(2,1)S(1)}, u32[]{:S(2)}, u32[]{:S(2)}) collective-permute-start(bf16[1024,512]{1,0:T(8,128)(2,1)S(1)} %collective-permute-done.7.refs_1_), channel_id=1, source_target_pairs={{0,1},{1,0},{2,3},{3,2},{4,5},{5,4},{6,7},{7,6},{8,9},{9,8},{10,11... | collective-permute-start | bytes 3145736 | tf_op jit(solution)/shard_map/ppermute | solution.py:293
  27.2 15.4 %copy-start.2 = (bf16[128,256]{1,0:T(8,128)(2,1)S(1)}, bf16[128,256]{1,0:T(8,128)(2,1)}, u32[]{:S(2)}) copy-start(bf16[128,256]{1,0:T(8,128)(2,1)} %k_ref.1) | copy-start | bytes 196612
  27.2 15.4 %copy-start.4 = (s32[6]{0:T(128)S(1)}, s32[6]{0:T(128)}, u32[]{:S(2)}) copy-start(s32[6]{0:T(128)} %lengths_ref.3) | copy-start | bytes 76
  27.2 15.4 %copy-start.5 = (f32[1,128]{1,0:T(1,128)S(1)}, f32[1,128]{1,0:T(1,128)}, u32[]{:S(2)}) copy-start(f32[1,128]{1,0:T(1,128)} %constant.2.clone.freq_ref) | copy-start | bytes 1540
  27.2 10.9 %collective-permute-start = (bf16[128,512]{1,0:T(8,128)(2,1)S(1)}, bf16[128,512]{1,0:T(8,128)(2,1)S(1)}, u32[]{:S(2)}, u32[]{:S(2)}) collective-permute-start(bf16[128,512]{1,0:T(8,128)(2,1)S(1)} %constant_dynamic-update-slice_fusion), channel_id=1, source_target_pairs={{0,4},{4,8},{8,12},{12,16},{16,20},{20,24},{24,28},{1,5},{5,9},{9,... | collective-permute-start | bytes 393224 | tf_op jit(solution)/shard_map/ppermute | solution.py:151
  30.8 9.4 %collective-permute-start.1 = (bf16[128,512]{1,0:T(8,128)(2,1)S(1)}, bf16[128,512]{1,0:T(8,128)(2,1)S(1)}, u32[]{:S(2)}, u32[]{:S(2)}) collective-permute-start(bf16[128,512]{1,0:T(8,128)(2,1)S(1)} %constant_dynamic-update-slice_fusion), channel_id=1, source_target_pairs={{0,8},{4,12},{8,16},{12,20},{16,24},{20,28},{1,9},{5,13},{9,17},{1... | collective-permute-start | bytes 393224 | tf_op jit(solution)/shard_map/ppermute | solution.py:151
  34.0 11.1 %collective-permute-start.2 = (bf16[128,512]{1,0:T(8,128)(2,1)S(1)}, bf16[128,512]{1,0:T(8,128)(2,1)S(1)}, u32[]{:S(2)}, u32[]{:S(2)}) collective-permute-start(bf16[128,512]{1,0:T(8,128)(2,1)S(1)} %constant_dynamic-update-slice_fusion), channel_id=1, source_target_pairs={{0,12},{4,16},{8,20},{12,24},{16,28},{1,13},{5,17},{9,21},{13,25},... | collective-permute-start | bytes 393224 | tf_op jit(solution)/shard_map/ppermute | solution.py:151
  38.2 6.9 %collective-permute-start.3 = (bf16[128,512]{1,0:T(8,128)(2,1)S(1)}, bf16[128,512]{1,0:T(8,128)(2,1)S(1)}, u32[]{:S(2)}, u32[]{:S(2)}) collective-permute-start(bf16[128,512]{1,0:T(8,128)(2,1)S(1)} %constant_dynamic-update-slice_fusion), channel_id=1, source_target_pairs={{0,16},{4,20},{8,24},{12,28},{1,17},{5,21},{9,25},{13,29},{2,18},{... | collective-permute-start | bytes 393224 | tf_op jit(solution)/shard_map/ppermute | solution.py:151
  40.1 6.0 %collective-permute-start.4 = (bf16[128,512]{1,0:T(8,128)(2,1)S(1)}, bf16[128,512]{1,0:T(8,128)(2,1)S(1)}, u32[]{:S(2)}, u32[]{:S(2)}) collective-permute-start(bf16[128,512]{1,0:T(8,128)(2,1)S(1)} %constant_dynamic-update-slice_fusion), channel_id=1, source_target_pairs={{0,20},{4,24},{8,28},{1,21},{5,25},{9,29},{2,22},{6,26},{10,30},{3... | collective-permute-start | bytes 393224 | tf_op jit(solution)/shard_map/ppermute | solution.py:151
  42.7 1.0 %copy-start.1 = (bf16[128,1024]{1,0:T(8,128)(2,1)S(1)}, bf16[128,1024]{1,0:T(8,128)(2,1)}, u32[]{:S(2)}) copy-start(bf16[128,1024]{1,0:T(8,128)(2,1)} %q_ref.1) | copy-start | bytes 786436
  45.0 26.5 %copy-start = (bf16[1024,512]{1,0:T(8,128)(2,1)S(1)}, bf16[1024,512]{1,0:T(8,128)(2,1)}, u32[]{:S(2)}) copy-start(bf16[1024,512]{1,0:T(8,128)(2,1)} %refs_0_.3) | copy-start | bytes 3145732
  48.8 14.3 %collective-permute-start.10 = (bf16[128,1024]{1,0:T(8,128)(2,1)S(1)}, bf16[128,1024]{1,0:T(8,128)(2,1)S(1)}, u32[]{:S(2)}, u32[]{:S(2)}) collective-permute-start(bf16[128,1024]{1,0:T(8,128)(2,1)S(1)} %attention.1), channel_id=1, source_target_pairs={{0,8},{1,25},{2,2},{3,19},{4,12},{5,29},{6,6},{7,23},{8,0},{9,17},... | collective-permute-start | bytes 786440 | tf_op jit(solution)/shard_map/ppermute | solution.py:293
  57.6 14.0 %collective-permute-start.11 = (bf16[128,1024]{1,0:T(8,128)(2,1)S(1)}, bf16[128,1024]{1,0:T(8,128)(2,1)S(1)}, u32[]{:S(2)}, u32[]{:S(2)}) collective-permute-start(bf16[128,1024]{1,0:T(8,128)(2,1)S(1)} %attention.1), channel_id=1, source_target_pairs={{0,25},{1,8},{2,19},{3,2},{4,29},{5,12},{6,23},{7,6},{8,17},{9,0},... | collective-permute-start | bytes 786440 | tf_op jit(solution)/shard_map/ppermute | solution.py:293
  57.6 17.5 %collective-permute-start.5 = (bf16[128,1024]{1,0:T(8,128)(2,1)S(1)}, bf16[128,1024]{1,0:T(8,128)(2,1)S(1)}, u32[]{:S(2)}, u32[]{:S(2)}) collective-permute-start(bf16[128,1024]{1,0:T(8,128)(2,1)S(1)} %attention.1), channel_id=1, source_target_pairs={{0,0},{1,17},{2,10},{3,27},{4,4},{5,21},{6,14},{7,31},{8,8},{9,25}... | collective-permute-start | bytes 786440 | tf_op jit(solution)/shard_map/ppermute | solution.py:293
  63.1 17.8 %collective-permute-start.6 = (bf16[128,1024]{1,0:T(8,128)(2,1)S(1)}, bf16[128,1024]{1,0:T(8,128)(2,1)S(1)}, u32[]{:S(2)}, u32[]{:S(2)}) collective-permute-start(bf16[128,1024]{1,0:T(8,128)(2,1)S(1)} %attention.1), channel_id=1, source_target_pairs={{0,17},{1,0},{2,27},{3,10},{4,21},{5,4},{6,31},{7,14},{8,25},{9,8}... | collective-permute-start | bytes 786440 | tf_op jit(solution)/shard_map/ppermute | solution.py:293
  72.3 8.5 %collective-permute-start.12 = (bf16[128,1024]{1,0:T(8,128)(2,1)S(1)}, bf16[128,1024]{1,0:T(8,128)(2,1)S(1)}, u32[]{:S(2)}, u32[]{:S(2)}) collective-permute-start(bf16[128,1024]{1,0:T(8,128)(2,1)S(1)} %shard_map.64), channel_id=1, source_target_pairs={{0,2},{1,3},{2,0},{3,1},{4,6},{5,7},{6,4},{7,5},{8,10},{9,11},{10,... | collective-permute-start | bytes 786440 | tf_op jit(solution)/shard_map/ppermute | solution.py:293
  81.7 11.2 %collective-permute-start.13 = (bf16[128,1024]{1,0:T(8,128)(2,1)S(1)}, bf16[128,1024]{1,0:T(8,128)(2,1)S(1)}, u32[]{:S(2)}, u32[]{:S(2)}) collective-permute-start(bf16[128,1024]{1,0:T(8,128)(2,1)S(1)} %shard_map.65), channel_id=1, source_target_pairs={{0,0},{1,16},{2,8},{3,24},{4,4},{5,20},{6,12},{7,28},{8,9},{9,25},... | collective-permute-start | bytes 786440 | tf_op jit(solution)/shard_map/ppermute | solution.py:293

commit v5 on v4

--- a/solution.py
+++ b/solution.py
@@ -320,9 +320,11 @@
 
             return permute(attended, move)
 
-        lent = project(inner, deliver(1, 0), deliver(1, 1), weights, mate_weights, [])
+        own, mate = deliver(1, 0), deliver(1, 1)
+        lent = project(inner, own, mate, weights, mate_weights, [])
+        passed = permute(mate, lambda z, x, j: (z ^ 1, x, j))
         lent = permute(lent, lambda z, x, j: (z, x, j ^ 2))
-        mixed = project(inner, deliver(0, 0), deliver(0, 1), weights, mate_weights, [lent])
+        mixed = project(inner, deliver(0, 0), passed, weights, mate_weights, [lent])
         return permute(mixed, lambda z, x, j: (z ^ ((j & 1) * 2 | (j >> 1)), x, z))
 
     in_specs = (P("tok", "feat"), P("tok", "feat"), P("tok", "feat"), P("feat", "tok"), P())

time: 94.7 us -> 92.4 us (0.976)
  the two profiles are of different devices: /device:TPU:1 before, /device:TPU:10 now
where the time goes in v5:
time: 92.4 us; the launch traced here: 92 us
  waiting for transfers between devices  57.8 us (63%)
  starting transfers between devices  25.9 us (28%)
  Pallas kernels  5.59 us (6%)
  local copies, waits for them, and re-layouts  2.53 us (3%)
    ppermute x9, waiting for transfers between devices, permute(): return lax.ppermute(array, ('tok', 'feat'), everyone(move))  49.1 us
    ppermute x5, starting transfers between devices, attend_near(): lax.ppermute(both, 'tok', [(i, i + d) for i in range(n_tok - d)])  13.1 us
    ppermute x9, starting transfers between devices, permute(): return lax.ppermute(array, ('tok', 'feat'), everyone(move))  12.8 us
    ppermute x5, waiting for transfers between devices, attend_near(): lax.ppermute(both, 'tok', [(i, i + d) for i in range(n_tok - d)])  8.73 us
    pallas_call x1, Pallas kernels, attend_near(): pl.pallas_call(partial(attention_kernel, reach=reach), out_shape=whole, i...  2.62 us
    unnamed x14, local copies, waits for them, and re-layouts  2.52 us
  transfers between devices with their start and end apart: 14, of which 7 were waited for; matrix products, arithmetic and copies ran while one was open for 1% of the time, Pallas kernels for 5%

profile of v5, /device:TPU:10, one launch (start us, length us, event | category | flops | bytes accessed | tf_op | source)
XLA Modules:
  0.0 92.0 jit_solution(1254683282869299167)
XLA Ops:
  0.0 0.5 collective-permute-start.8
  0.5 0.0 collective-permute-start.9
  0.5 24.6 %collective-permute-done.8.refs_1_ = bf16[1024,512]{1,0:T(8,128)(2,1)S(1)} collective-permute-done((bf16[1024,512]{1,0:T(8,128)(2,1)}, bf16[1024,512]{1,0:T(8,128)(2,1)S(1)}, u32[]{:S(2)}, u32[]{:S(2)}) %collective-permute-start.8) | collective-permute-done | bytes 1048608 | tf_op jit(solution)/shard_map/ppermute | solution.py:293
  25.1 0.8 constant_dynamic-update-slice_fusion.1
  26.0 0.0 copy-start.4
  26.0 0.0 copy-start.5
  26.0 3.6 %collective-permute-start = (bf16[128,512]{1,0:T(8,128)(2,1)S(1)}, bf16[128,512]{1,0:T(8,128)(2,1)S(1)}, u32[]{:S(2)}, u32[]{:S(2)}) collective-permute-start(bf16[128,512]{1,0:T(8,128)(2,1)S(1)} %constant_dynamic-update-slice_fusion), channel_id=1, source_target_pairs={{0,4},{4,8},{8,12},{12,16},{16,20},{20,24},{24,28},{1,5},{5,9},{9,... | collective-permute-start | bytes 393224 | tf_op jit(solution)/shard_map/ppermute | solution.py:151
  29.6 3.5 %collective-permute-start.1 = (bf16[128,512]{1,0:T(8,128)(2,1)S(1)}, bf16[128,512]{1,0:T(8,128)(2,1)S(1)}, u32[]{:S(2)}, u32[]{:S(2)}) collective-permute-start(bf16[128,512]{1,0:T(8,128)(2,1)S(1)} %constant_dynamic-update-slice_fusion), channel_id=1, source_target_pairs={{0,8},{4,12},{8,16},{12,20},{16,24},{20,28},{1,9},{5,13},{9,17},{1... | collective-permute-start | bytes 393224 | tf_op jit(solution)/shard_map/ppermute | solution.py:151
  33.1 2.2 %collective-permute-start.2 = (bf16[128,512]{1,0:T(8,128)(2,1)S(1)}, bf16[128,512]{1,0:T(8,128)(2,1)S(1)}, u32[]{:S(2)}, u32[]{:S(2)}) collective-permute-start(bf16[128,512]{1,0:T(8,128)(2,1)S(1)} %constant_dynamic-update-slice_fusion), channel_id=1, source_target_pairs={{0,12},{4,16},{8,20},{12,24},{16,28},{1,13},{5,17},{9,21},{13,25},... | collective-permute-start | bytes 393224 | tf_op jit(solution)/shard_map/ppermute | solution.py:151
  35.3 0.0 collective-permute-done.refs_0_
  35.3 3.1 %collective-permute-start.3 = (bf16[128,512]{1,0:T(8,128)(2,1)S(1)}, bf16[128,512]{1,0:T(8,128)(2,1)S(1)}, u32[]{:S(2)}, u32[]{:S(2)}) collective-permute-start(bf16[128,512]{1,0:T(8,128)(2,1)S(1)} %constant_dynamic-update-slice_fusion), channel_id=1, source_target_pairs={{0,16},{4,20},{8,24},{12,28},{1,17},{5,21},{9,25},{13,29},{2,18},{... | collective-permute-start | bytes 393224 | tf_op jit(solution)/shard_map/ppermute | solution.py:151
  38.4 0.7 collective-permute-start.4
  39.2 0.0 copy-start.1
  39.2 0.9 %copy-done.1 = bf16[128,1024]{1,0:T(8,128)(2,1)S(1)} copy-done((bf16[128,1024]{1,0:T(8,128)(2,1)S(1)}, bf16[128,1024]{1,0:T(8,128)(2,1)}, u32[]{:S(2)}) %copy-start.1) | copy-done | bytes 262168
  40.1 1.4 %prepare.1 = (f32[640,128]{1,0:T(8,128)S(1)}, f32[640,128]{1,0:T(8,128)S(1)}, bf16[128,1024]{1,0:T(8,128)(2,1)S(1)}, bf16[128,256]{1,0:T(8,128)(2,1)S(1)}) custom-call(s32[6]{0:T(128)S(1)} %copy-done.4, f32[1,128]{1,0:T(1,128)S(1)} %copy-done.5, bf16[128,1024]{1,0:T(8,128)(2,1)S(1)} %copy-done.1, bf16[128,256]{1,0:T(8,128)(2,1)S(1)} %copy-done.2), custom_call_target="tpu_custom_call" | custom-call | tf_op jit(solution)/shard_map/prepare/pallas_call | solution.py:159
  41.5 0.0 copy-start
  41.5 6.5 %collective-permute-done.2.refs_2_ = bf16[128,512]{1,0:T(8,128)(2,1)S(1)} collective-permute-done((bf16[128,512]{1,0:T(8,128)(2,1)S(1)}, bf16[128,512]{1,0:T(8,128)(2,1)S(1)}, u32[]{:S(2)}, u32[]{:S(2)}) %collective-permute-start.2) | collective-permute-done | bytes 131104 | tf_op jit(solution)/shard_map/ppermute | solution.py:151
  48.0 2.2 %collective-permute-done.3.refs_3_ = bf16[128,512]{1,0:T(8,128)(2,1)S(1)} collective-permute-done((bf16[128,512]{1,0:T(8,128)(2,1)S(1)}, bf16[128,512]{1,0:T(8,128)(2,1)S(1)}, u32[]{:S(2)}, u32[]{:S(2)}) %collective-permute-start.3) | collective-permute-done | bytes 131104 | tf_op jit(solution)/shard_map/ppermute | solution.py:151
  50.3 2.6 %attention.1 = bf16[128,1024]{1,0:T(8,128)(2,1)S(1)} custom-call(s32[6]{0:T(128)S(1)} %copy-done.4, f32[640,128]{1,0:T(8,128)S(1)} %get-tuple-element.9.cos_ref, f32[640,128]{1,0:T(8,128)S(1)} %get-tuple-element.10.sin_ref, bf16[128,1024]{1,0:T(8,128)(2,1)S(1)} %get-tuple-element.11.q_ref, bf16[128,256]{1,0:T(8,128)(2,1)S(1)} %get-tuple-element.12.k_ref, ...), custom_call_target="tpu_custom_call" | custom-call | tf_op jit(solution)/shard_map/attention/pallas_call | solution.py:172
  52.9 0.1 collective-permute-start.6
  53.0 5.9 %collective-permute-start.11 = (bf16[128,1024]{1,0:T(8,128)(2,1)S(1)}, bf16[128,1024]{1,0:T(8,128)(2,1)S(1)}, u32[]{:S(2)}, u32[]{:S(2)}) collective-permute-start(bf16[128,1024]{1,0:T(8,128)(2,1)S(1)} %attention.1), channel_id=1, source_target_pairs={{0,8},{1,25},{2,2},{3,19},{4,12},{5,29},{6,6},{7,23},{8,0},{9,17},... | collective-permute-start | bytes 786440 | tf_op jit(solution)/shard_map/ppermute | solution.py:293
  58.8 0.7 collective-permute-start.5
  59.5 3.4 %collective-permute-start.7 = (bf16[128,1024]{1,0:T(8,128)(2,1)S(1)}, bf16[128,1024]{1,0:T(8,128)(2,1)S(1)}, u32[]{:S(2)}, u32[]{:S(2)}) collective-permute-start(bf16[128,1024]{1,0:T(8,128)(2,1)S(1)} %collective-permute-done.6.mate_ref), channel_id=1, source_target_pairs={{0,8},{1,9},{2,10},{3,11},{4,12},{5,13},{6,14},{7,15},{8,0},{9,1},... | collective-permute-start | bytes 786440 | tf_op jit(solution)/shard_map/ppermute | solution.py:293
  62.9 6.1 %collective-permute-done.11.own_ref = bf16[128,1024]{1,0:T(8,128)(2,1)S(1)} collective-permute-done((bf16[128,1024]{1,0:T(8,128)(2,1)S(1)}, bf16[128,1024]{1,0:T(8,128)(2,1)S(1)}, u32[]{:S(2)}, u32[]{:S(2)}) %collective-permute-start.11) | collective-permute-done | bytes 262176 | tf_op jit(solution)/shard_map/ppermute | solution.py:293
  69.0 0.8 shard_map.64
  69.8 0.1 collective-permute-start.12
  69.9 5.3 %collective-permute-done.7.mate_ref = bf16[128,1024]{1,0:T(8,128)(2,1)S(1)} collective-permute-done((bf16[128,1024]{1,0:T(8,128)(2,1)S(1)}, bf16[128,1024]{1,0:T(8,128)(2,1)S(1)}, u32[]{:S(2)}, u32[]{:S(2)}) %collective-permute-start.7) | collective-permute-done | bytes 262176 | tf_op jit(solution)/shard_map/ppermute | solution.py:293
  75.2 3.4 %collective-permute-done.12.refs_4_ = bf16[128,1024]{1,0:T(8,128)(2,1)S(1)} collective-permute-done((bf16[128,1024]{1,0:T(8,128)(2,1)S(1)}, bf16[128,1024]{1,0:T(8,128)(2,1)S(1)}, u32[]{:S(2)}, u32[]{:S(2)}) %collective-permute-start.12) | collective-permute-done | bytes 262176 | tf_op jit(solution)/shard_map/ppermute | solution.py:293
  78.6 0.8 shard_map.65
  79.4 2.2 %collective-permute-start.13 = (bf16[128,1024]{1,0:T(8,128)(2,1)S(1)}, bf16[128,1024]{1,0:T(8,128)(2,1)S(1)}, u32[]{:S(2)}, u32[]{:S(2)}) collective-permute-start(bf16[128,1024]{1,0:T(8,128)(2,1)S(1)} %shard_map.65), channel_id=1, source_target_pairs={{0,0},{1,16},{2,8},{3,24},{4,4},{5,20},{6,12},{7,28},{8,9},{9,25},... | collective-permute-start | bytes 786440 | tf_op jit(solution)/shard_map/ppermute | solution.py:293
  81.6 9.7 %collective-permute-done.13 = bf16[128,1024]{1,0:T(8,128)(2,1)S(1)} collective-permute-done((bf16[128,1024]{1,0:T(8,128)(2,1)S(1)}, bf16[128,1024]{1,0:T(8,128)(2,1)S(1)}, u32[]{:S(2)}, u32[]{:S(2)}) %collective-permute-start.13) | collective-permute-done | bytes 262176 | tf_op jit(solution)/shard_map/ppermute | solution.py:293
  91.3 0.7 copy.9
  (15 shorter events, 0.0 us)
Async XLA Ops:
  0.0 26.0 %copy-start.3 = (bf16[128,256]{1,0:T(8,128)(2,1)S(1)}, bf16[128,256]{1,0:T(8,128)(2,1)}, u32[]{:S(2)}) copy-start(bf16[128,256]{1,0:T(8,128)(2,1)} %v_ref.1) | copy-start | bytes 196612
  0.0 25.1 %collective-permute-start.8 = (bf16[1024,512]{1,0:T(8,128)(2,1)}, bf16[1024,512]{1,0:T(8,128)(2,1)S(1)}, u32[]{:S(2)}, u32[]{:S(2)}) collective-permute-start(bf16[1024,512]{1,0:T(8,128)(2,1)} %refs_0_.3), channel_id=1, source_target_pairs={{0,4},{1,5},{2,6},{3,7},{4,0},{5,1},{6,2},{7,3},{8,12},{9,13},{10,... | collective-permute-start | bytes 3145736 | tf_op jit(solution)/shard_map/ppermute | solution.py:293
  0.5 68.5 %collective-permute-start.9 = (bf16[1024,512]{1,0:T(8,128)(2,1)}, bf16[1024,512]{1,0:T(8,128)(2,1)S(1)}, u32[]{:S(2)}, u32[]{:S(2)}) collective-permute-start(bf16[1024,512]{1,0:T(8,128)(2,1)} %refs_0_.3), channel_id=1, source_target_pairs={{0,1},{1,0},{2,3},{3,2},{4,5},{5,4},{6,7},{7,6},{8,9},{9,8},{10,11... | collective-permute-start | bytes 3145736 | tf_op jit(solution)/shard_map/ppermute | solution.py:293
  25.1 43.9 %collective-permute-start.10 = (bf16[1024,512]{1,0:T(8,128)(2,1)S(1)}, bf16[1024,512]{1,0:T(8,128)(2,1)S(1)}, u32[]{:S(2)}, u32[]{:S(2)}) collective-permute-start(bf16[1024,512]{1,0:T(8,128)(2,1)S(1)} %collective-permute-done.8.refs_1_), channel_id=1, source_target_pairs={{0,1},{1,0},{2,3},{3,2},{4,5},{5,4},{6,7},{7,6},{8,9},{9,8},{10,11... | collective-permute-start | bytes 3145736 | tf_op jit(solution)/shard_map/ppermute | solution.py:293
  26.0 13.2 %copy-start.2 = (bf16[128,256]{1,0:T(8,128)(2,1)S(1)}, bf16[128,256]{1,0:T(8,128)(2,1)}, u32[]{:S(2)}) copy-start(bf16[128,256]{1,0:T(8,128)(2,1)} %k_ref.1) | copy-start | bytes 196612
  26.0 13.2 %copy-start.4 = (s32[6]{0:T(128)S(1)}, s32[6]{0:T(128)}, u32[]{:S(2)}) copy-start(s32[6]{0:T(128)} %lengths_ref.3) | copy-start | bytes 76
  26.0 13.2 %copy-start.5 = (f32[1,128]{1,0:T(1,128)S(1)}, f32[1,128]{1,0:T(1,128)}, u32[]{:S(2)}) copy-start(f32[1,128]{1,0:T(1,128)} %constant.2.clone.freq_ref) | copy-start | bytes 1540
  26.0 9.3 %collective-permute-start = (bf16[128,512]{1,0:T(8,128)(2,1)S(1)}, bf16[128,512]{1,0:T(8,128)(2,1)S(1)}, u32[]{:S(2)}, u32[]{:S(2)}) collective-permute-start(bf16[128,512]{1,0:T(8,128)(2,1)S(1)} %constant_dynamic-update-slice_fusion), channel_id=1, source_target_pairs={{0,4},{4,8},{8,12},{12,16},{16,20},{20,24},{24,28},{1,5},{5,9},{9,... | collective-permute-start | bytes 393224 | tf_op jit(solution)/shard_map/ppermute | solution.py:151
  29.6 8.8 %collective-permute-start.1 = (bf16[128,512]{1,0:T(8,128)(2,1)S(1)}, bf16[128,512]{1,0:T(8,128)(2,1)S(1)}, u32[]{:S(2)}, u32[]{:S(2)}) collective-permute-start(bf16[128,512]{1,0:T(8,128)(2,1)S(1)} %constant_dynamic-update-slice_fusion), channel_id=1, source_target_pairs={{0,8},{4,12},{8,16},{12,20},{16,24},{20,28},{1,9},{5,13},{9,17},{1... | collective-permute-start | bytes 393224 | tf_op jit(solution)/shard_map/ppermute | solution.py:151
  33.1 14.9 %collective-permute-start.2 = (bf16[128,512]{1,0:T(8,128)(2,1)S(1)}, bf16[128,512]{1,0:T(8,128)(2,1)S(1)}, u32[]{:S(2)}, u32[]{:S(2)}) collective-permute-start(bf16[128,512]{1,0:T(8,128)(2,1)S(1)} %constant_dynamic-update-slice_fusion), channel_id=1, source_target_pairs={{0,12},{4,16},{8,20},{12,24},{16,28},{1,13},{5,17},{9,21},{13,25},... | collective-permute-start | bytes 393224 | tf_op jit(solution)/shard_map/ppermute | solution.py:151
  35.3 14.9 %collective-permute-start.3 = (bf16[128,512]{1,0:T(8,128)(2,1)S(1)}, bf16[128,512]{1,0:T(8,128)(2,1)S(1)}, u32[]{:S(2)}, u32[]{:S(2)}) collective-permute-start(bf16[128,512]{1,0:T(8,128)(2,1)S(1)} %constant_dynamic-update-slice_fusion), channel_id=1, source_target_pairs={{0,16},{4,20},{8,24},{12,28},{1,17},{5,21},{9,25},{13,29},{2,18},{... | collective-permute-start | bytes 393224 | tf_op jit(solution)/shard_map/ppermute | solution.py:151
  38.4 11.8 %collective-permute-start.4 = (bf16[128,512]{1,0:T(8,128)(2,1)S(1)}, bf16[128,512]{1,0:T(8,128)(2,1)S(1)}, u32[]{:S(2)}, u32[]{:S(2)}) collective-permute-start(bf16[128,512]{1,0:T(8,128)(2,1)S(1)} %constant_dynamic-update-slice_fusion), channel_id=1, source_target_pairs={{0,20},{4,24},{8,28},{1,21},{5,25},{9,29},{2,22},{6,26},{10,30},{3... | collective-permute-start | bytes 393224 | tf_op jit(solution)/shard_map/ppermute | solution.py:151
  39.2 1.0 %copy-start.1 = (bf16[128,1024]{1,0:T(8,128)(2,1)S(1)}, bf16[128,1024]{1,0:T(8,128)(2,1)}, u32[]{:S(2)}) copy-start(bf16[128,1024]{1,0:T(8,128)(2,1)} %q_ref.1) | copy-start | bytes 786436
  41.5 27.5 %copy-start = (bf16[1024,512]{1,0:T(8,128)(2,1)S(1)}, bf16[1024,512]{1,0:T(8,128)(2,1)}, u32[]{:S(2)}) copy-start(bf16[1024,512]{1,0:T(8,128)(2,1)} %refs_0_.3) | copy-start | bytes 3145732
  52.9 6.6 %collective-permute-start.6 = (bf16[128,1024]{1,0:T(8,128)(2,1)S(1)}, bf16[128,1024]{1,0:T(8,128)(2,1)S(1)}, u32[]{:S(2)}, u32[]{:S(2)}) collective-permute-start(bf16[128,1024]{1,0:T(8,128)(2,1)S(1)} %attention.1), channel_id=1, source_target_pairs={{0,25},{1,8},{2,19},{3,2},{4,29},{5,12},{6,23},{7,6},{8,17},{9,0},... | collective-permute-start | bytes 786440 | tf_op jit(solution)/shard_map/ppermute | solution.py:293
  53.0 16.1 %collective-permute-start.11 = (bf16[128,1024]{1,0:T(8,128)(2,1)S(1)}, bf16[128,1024]{1,0:T(8,128)(2,1)S(1)}, u32[]{:S(2)}, u32[]{:S(2)}) collective-permute-start(bf16[128,1024]{1,0:T(8,128)(2,1)S(1)} %attention.1), channel_id=1, source_target_pairs={{0,8},{1,25},{2,2},{3,19},{4,12},{5,29},{6,6},{7,23},{8,0},{9,17},... | collective-permute-start | bytes 786440 | tf_op jit(solution)/shard_map/ppermute | solution.py:293
  58.8 11.0 %collective-permute-start.5 = (bf16[128,1024]{1,0:T(8,128)(2,1)S(1)}, bf16[128,1024]{1,0:T(8,128)(2,1)S(1)}, u32[]{:S(2)}, u32[]{:S(2)}) collective-permute-start(bf16[128,1024]{1,0:T(8,128)(2,1)S(1)} %attention.1), channel_id=1, source_target_pairs={{0,0},{1,17},{2,10},{3,27},{4,4},{5,21},{6,14},{7,31},{8,8},{9,25}... | collective-permute-start | bytes 786440 | tf_op jit(solution)/shard_map/ppermute | solution.py:293
  59.5 15.7 %collective-permute-start.7 = (bf16[128,1024]{1,0:T(8,128)(2,1)S(1)}, bf16[128,1024]{1,0:T(8,128)(2,1)S(1)}, u32[]{:S(2)}, u32[]{:S(2)}) collective-permute-start(bf16[128,1024]{1,0:T(8,128)(2,1)S(1)} %collective-permute-done.6.mate_ref), channel_id=1, source_target_pairs={{0,8},{1,9},{2,10},{3,11},{4,12},{5,13},{6,14},{7,15},{8,0},{9,1},... | collective-permute-start | bytes 786440 | tf_op jit(solution)/shard_map/ppermute | solution.py:293
  69.8 8.8 %collective-permute-start.12 = (bf16[128,1024]{1,0:T(8,128)(2,1)S(1)}, bf16[128,1024]{1,0:T(8,128)(2,1)S(1)}, u32[]{:S(2)}, u32[]{:S(2)}) collective-permute-start(bf16[128,1024]{1,0:T(8,128)(2,1)S(1)} %shard_map.64), channel_id=1, source_target_pairs={{0,2},{1,3},{2,0},{3,1},{4,6},{5,7},{6,4},{7,5},{8,10},{9,11},{10,... | collective-permute-start | bytes 786440 | tf_op jit(solution)/shard_map/ppermute | solution.py:293
  79.4 11.9 %collective-permute-start.13 = (bf16[128,1024]{1,0:T(8,128)(2,1)S(1)}, bf16[128,1024]{1,0:T(8,128)(2,1)S(1)}, u32[]{:S(2)}, u32[]{:S(2)}) collective-permute-start(bf16[128,1024]{1,0:T(8,128)(2,1)S(1)} %shard_map.65), channel_id=1, source_target_pairs={{0,0},{1,16},{2,8},{3,24},{4,4},{5,20},{6,12},{7,28},{8,9},{9,25},... | collective-permute-start | bytes 786440 | tf_op jit(solution)/shard_map/ppermute | solution.py:293

commit v6 on v5

--- a/solution.py
+++ b/solution.py
@@ -87,8 +87,16 @@
             target[:, at] = turn(source[:, at], cosine, sine)
 
 
-def attention_kernel(lengths_ref, cos_ref, sin_ref, q_ref, k_ref, v_ref, *refs, reach):
-    far, (out_ref, score_ref, weight_ref) = refs[:reach], refs[reach:]
+def attention_kernel(lengths_ref, cos_ref, sin_ref, q_ref, k_ref, v_ref, *refs, reach, mixed):
+    out_ref, score_ref, weight_ref = refs[-3:]
+    far, taken = [], 0
+    base = lax.axis_size("tok") // 2
+    for d in range(1, reach + 1):
+        far.append(refs[taken][...])
+        if mixed[d - 1]:
+            inside = lax.rem(lax.axis_index("tok"), base) >= d
+            far[-1] = jnp.where(inside, refs[taken + 1][...], far[-1])
+        taken += 2 if mixed[d - 1] else 1
     rows = k_ref.shape[0]
     kv_heads = k_ref.shape[1] // HD
     group = q_ref.shape[1] // k_ref.shape[1]
@@ -141,14 +149,32 @@
             out_ref[:, head * HD : (head + 1) * HD] = piece.astype(jnp.bfloat16)
 
 
-def attend_near(queries, keys, values, doc_lengths, reach, n_tok):
+def attend_near(queries, keys, values, doc_lengths, reach, n_tok, inner):
     rows = queries.shape[0]
     kv_heads = keys.shape[1] // HD
     group = queries.shape[1] // keys.shape[1]
     both = jnp.concatenate([keys, values], axis=1)
     far = []
+    base = n_tok // 2
+
+    def shift(array, d, pairs):
+        return lax.ppermute(array, "tok", [(i, i + d) for i in pairs])
+
+    held = shift(both, base, range(n_tok - base))
     for d in range(1, reach + 1):
-        far.append(lax.ppermute(both, "tok", [(i, i + d) for i in range(n_tok - d)]))
+        if d == base:
+            far.append(held)
+        elif (d - base) % inner:
+            far.append(shift(both, d, range(n_tok - d)))
+        else:
+            inside = [i for i in range(n_tok - d) if i // base == (i + d) // base]
+            onward = [
+                i for i in range(base, n_tok) if base <= i + d - base < n_tok and i - base < n_tok - d
+            ]
+            relayed = shift(held, d - base, onward)
+            far.append((relayed, shift(both, d, inside)) if inside else relayed)
+    mixed = [isinstance(f, tuple) for f in far]
+    far = [a for f in far for a in (f if isinstance(f, tuple) else (f,))]
     half = np.arange(HD, dtype=np.float32) % (HD // 2)
     freq = jnp.asarray((ROPE_BASE ** (-(half * 2.0 / HD))).astype(np.float32).reshape(1, HD))
     vmem = pl.BlockSpec(memory_space=pltpu.VMEM)
@@ -170,9 +196,9 @@
         name="prepare",
     )(doc_lengths, freq, *on_chip(queries, keys))
     return pl.pallas_call(
-        partial(attention_kernel, reach=reach),
+        partial(attention_kernel, reach=reach, mixed=mixed),
         out_shape=whole,
-        in_specs=[smem] + [vmem] * (5 + reach),
+        in_specs=[smem] + [vmem] * (5 + len(far)),
         out_specs=vmem,
         scratch_shapes=[
             pltpu.VMEM((kv_heads, group * rows, span), jnp.float32),
@@ -297,7 +323,7 @@
         longest = n_tok * rows * LONGEST[0] // LONGEST[1]
         reach = min(n_tok - 1, -(-(longest - 1) // rows))
         if reach <= FAR_BLOCKS:
-            attended = attend_near(queries, keys, values, doc_lengths, reach, n_tok)
+            attended = attend_near(queries, keys, values, doc_lengths, reach, n_tok, inner)
         else:
             attended = attend_far(queries, keys, values, doc_lengths)
         if inner == 2:

time: 92.4 us -> 93 us (level)
  the two profiles are of different devices: /device:TPU:10 before, /device:TPU:1 now
where the time goes in v6:
time: 93 us; the launch traced here: 91.9 us
  waiting for transfers between devices  42.3 us (45%)
  starting transfers between devices  41.3 us (44%)
  Pallas kernels  5.56 us (6%)
  local copies, waits for them, and re-layouts  2.52 us (3%)
    ppermute x9, waiting for transfers between devices, permute(): return lax.ppermute(array, ('tok', 'feat'), everyone(move))  41.6 us
    ppermute x9, starting transfers between devices, permute(): return lax.ppermute(array, ('tok', 'feat'), everyone(move))  24.6 us
    ppermute x6, starting transfers between devices, shift(): return lax.ppermute(array, 'tok', [(i, i + d) for i in pairs])  16.7 us
    pallas_call x1, Pallas kernels, attend_near(): pl.pallas_call(partial(attention_kernel, reach=reach, mixed=mixed), out_s...  2.62 us
    unnamed x14, local copies, waits for them, and re-layouts  2.52 us
  transfers between devices with their start and end apart: 15, of which 8 were waited for; matrix products, arithmetic and copies ran while one was open for 1% of the time, Pallas kernels for 5%

profile of v6, /device:TPU:1, one launch (start us, length us, event | category | flops | bytes accessed | tf_op | source)
XLA Modules:
  0.0 91.9 jit_solution(9506987372927223319)
XLA Ops:
  0.0 2.0 %collective-permute-start.9 = (bf16[1024,512]{1,0:T(8,128)(2,1)}, bf16[1024,512]{1,0:T(8,128)(2,1)S(1)}, u32[]{:S(2)}, u32[]{:S(2)}) collective-permute-start(bf16[1024,512]{1,0:T(8,128)(2,1)} %refs_0_.3), channel_id=1, source_target_pairs={{0,4},{1,5},{2,6},{3,7},{4,0},{5,1},{6,2},{7,3},{8,12},{9,13},{10,... | collective-permute-start | bytes 3145736 | tf_op jit(solution)/shard_map/ppermute | solution.py:319
  2.0 1.0 %collective-permute-start.10 = (bf16[1024,512]{1,0:T(8,128)(2,1)}, bf16[1024,512]{1,0:T(8,128)(2,1)S(1)}, u32[]{:S(2)}, u32[]{:S(2)}) collective-permute-start(bf16[1024,512]{1,0:T(8,128)(2,1)} %refs_0_.3), channel_id=1, source_target_pairs={{0,1},{1,0},{2,3},{3,2},{4,5},{5,4},{6,7},{7,6},{8,9},{9,8},{10,11... | collective-permute-start | bytes 3145736 | tf_op jit(solution)/shard_map/ppermute | solution.py:319
  3.0 22.1 %collective-permute-done.9.refs_1_ = bf16[1024,512]{1,0:T(8,128)(2,1)S(1)} collective-permute-done((bf16[1024,512]{1,0:T(8,128)(2,1)}, bf16[1024,512]{1,0:T(8,128)(2,1)S(1)}, u32[]{:S(2)}, u32[]{:S(2)}) %collective-permute-start.9) | collective-permute-done | bytes 1048608 | tf_op jit(solution)/shard_map/ppermute | solution.py:319
  25.1 1.3 %collective-permute-start.11 = (bf16[1024,512]{1,0:T(8,128)(2,1)S(1)}, bf16[1024,512]{1,0:T(8,128)(2,1)S(1)}, u32[]{:S(2)}, u32[]{:S(2)}) collective-permute-start(bf16[1024,512]{1,0:T(8,128)(2,1)S(1)} %collective-permute-done.9.refs_1_), channel_id=1, source_target_pairs={{0,1},{1,0},{2,3},{3,2},{4,5},{5,4},{6,7},{7,6},{8,9},{9,8},{10,11... | collective-permute-start | bytes 3145736 | tf_op jit(solution)/shard_map/ppermute | solution.py:319
  26.4 0.8 constant_dynamic-update-slice_fusion.1
  27.2 0.0 copy-start.4
  27.2 0.0 copy-start.5
  27.2 4.6 %collective-permute-start.1 = (bf16[128,512]{1,0:T(8,128)(2,1)S(1)}, bf16[128,512]{1,0:T(8,128)(2,1)S(1)}, u32[]{:S(2)}, u32[]{:S(2)}) collective-permute-start(bf16[128,512]{1,0:T(8,128)(2,1)S(1)} %constant_dynamic-update-slice_fusion), channel_id=1, source_target_pairs={{0,16},{4,20},{8,24},{12,28},{1,17},{5,21},{9,25},{13,29},{2,18},{... | collective-permute-start | bytes 393224 | tf_op jit(solution)/shard_map/ppermute | solution.py:161
  31.9 3.1 %collective-permute-start = (bf16[128,512]{1,0:T(8,128)(2,1)S(1)}, bf16[128,512]{1,0:T(8,128)(2,1)S(1)}, u32[]{:S(2)}, u32[]{:S(2)}) collective-permute-start(bf16[128,512]{1,0:T(8,128)(2,1)S(1)} %constant_dynamic-update-slice_fusion), channel_id=1, source_target_pairs={{0,4},{4,8},{8,12},{12,16},{16,20},{20,24},{24,28},{1,5},{5,9},{9,... | collective-permute-start | bytes 393224 | tf_op jit(solution)/shard_map/ppermute | solution.py:161
  35.0 3.2 %collective-permute-start.3 = (bf16[128,512]{1,0:T(8,128)(2,1)S(1)}, bf16[128,512]{1,0:T(8,128)(2,1)S(1)}, u32[]{:S(2)}, u32[]{:S(2)}) collective-permute-start(bf16[128,512]{1,0:T(8,128)(2,1)S(1)} %constant_dynamic-update-slice_fusion), channel_id=1, source_target_pairs={{0,8},{4,12},{16,24},{20,28},{1,9},{5,13},{17,25},{21,29},{2,10},{... | collective-permute-start | bytes 393224 | tf_op jit(solution)/shard_map/ppermute | solution.py:161
  38.2 3.8 %collective-permute-start.4 = (bf16[128,512]{1,0:T(8,128)(2,1)S(1)}, bf16[128,512]{1,0:T(8,128)(2,1)S(1)}, u32[]{:S(2)}, u32[]{:S(2)}) collective-permute-start(bf16[128,512]{1,0:T(8,128)(2,1)S(1)} %constant_dynamic-update-slice_fusion), channel_id=1, source_target_pairs={{0,12},{4,16},{8,20},{12,24},{16,28},{1,13},{5,17},{9,21},{13,25},... | collective-permute-start | bytes 393224 | tf_op jit(solution)/shard_map/ppermute | solution.py:161
  42.0 1.3 %collective-permute-start.5 = (bf16[128,512]{1,0:T(8,128)(2,1)S(1)}, bf16[128,512]{1,0:T(8,128)(2,1)S(1)}, u32[]{:S(2)}, u32[]{:S(2)}) collective-permute-start(bf16[128,512]{1,0:T(8,128)(2,1)S(1)} %constant_dynamic-update-slice_fusion), channel_id=1, source_target_pairs={{0,20},{4,24},{8,28},{1,21},{5,25},{9,29},{2,22},{6,26},{10,30},{3... | collective-permute-start | bytes 393224 | tf_op jit(solution)/shard_map/ppermute | solution.py:161
  43.3 0.7 collective-permute-start.2
  44.0 0.0 copy-start.1
  44.0 0.9 %copy-done.1 = bf16[128,1024]{1,0:T(8,128)(2,1)S(1)} copy-done((bf16[128,1024]{1,0:T(8,128)(2,1)S(1)}, bf16[128,1024]{1,0:T(8,128)(2,1)}, u32[]{:S(2)}) %copy-start.1) | copy-done | bytes 262168
  45.0 1.4 %prepare.1 = (f32[640,128]{1,0:T(8,128)S(1)}, f32[640,128]{1,0:T(8,128)S(1)}, bf16[128,1024]{1,0:T(8,128)(2,1)S(1)}, bf16[128,256]{1,0:T(8,128)(2,1)S(1)}) custom-call(s32[6]{0:T(128)S(1)} %copy-done.4, f32[1,128]{1,0:T(1,128)S(1)} %copy-done.5, bf16[128,1024]{1,0:T(8,128)(2,1)S(1)} %copy-done.1, bf16[128,256]{1,0:T(8,128)(2,1)S(1)} %copy-done.2), custom_call_target="tpu_custom_call" | custom-call | tf_op jit(solution)/shard_map/prepare/pallas_call | solution.py:185
  46.4 0.7 collective-permute-done.5.refs_5_
  47.1 2.6 %attention.1 = bf16[128,1024]{1,0:T(8,128)(2,1)S(1)} custom-call(s32[6]{0:T(128)S(1)} %copy-done.4, f32[640,128]{1,0:T(8,128)S(1)} %get-tuple-element.9.cos_ref, f32[640,128]{1,0:T(8,128)S(1)} %get-tuple-element.10.sin_ref, bf16[128,1024]{1,0:T(8,128)(2,1)S(1)} %get-tuple-element.11.q_ref, bf16[128,256]{1,0:T(8,128)(2,1)S(1)} %get-tuple-element.12.k_ref, ...), custom_call_target="tpu_custom_call" | custom-call | tf_op jit(solution)/shard_map/attention/pallas_call | solution.py:198
  49.8 5.0 %collective-permute-start.7 = (bf16[128,1024]{1,0:T(8,128)(2,1)S(1)}, bf16[128,1024]{1,0:T(8,128)(2,1)S(1)}, u32[]{:S(2)}, u32[]{:S(2)}) collective-permute-start(bf16[128,1024]{1,0:T(8,128)(2,1)S(1)} %attention.1), channel_id=1, source_target_pairs={{0,25},{1,8},{2,19},{3,2},{4,29},{5,12},{6,23},{7,6},{8,17},{9,0},... | collective-permute-start | bytes 786440 | tf_op jit(solution)/shard_map/ppermute | solution.py:319
  54.8 4.5 %collective-permute-start.12 = (bf16[128,1024]{1,0:T(8,128)(2,1)S(1)}, bf16[128,1024]{1,0:T(8,128)(2,1)S(1)}, u32[]{:S(2)}, u32[]{:S(2)}) collective-permute-start(bf16[128,1024]{1,0:T(8,128)(2,1)S(1)} %attention.1), channel_id=1, source_target_pairs={{0,8},{1,25},{2,2},{3,19},{4,12},{5,29},{6,6},{7,23},{8,0},{9,17},... | collective-permute-start | bytes 786440 | tf_op jit(solution)/shard_map/ppermute | solution.py:319
  59.3 2.3 %collective-permute-start.6 = (bf16[128,1024]{1,0:T(8,128)(2,1)S(1)}, bf16[128,1024]{1,0:T(8,128)(2,1)S(1)}, u32[]{:S(2)}, u32[]{:S(2)}) collective-permute-start(bf16[128,1024]{1,0:T(8,128)(2,1)S(1)} %attention.1), channel_id=1, source_target_pairs={{0,0},{1,17},{2,10},{3,27},{4,4},{5,21},{6,14},{7,31},{8,8},{9,25}... | collective-permute-start | bytes 786440 | tf_op jit(solution)/shard_map/ppermute | solution.py:319
  61.6 2.8 %collective-permute-done.7.mate_ref = bf16[128,1024]{1,0:T(8,128)(2,1)S(1)} collective-permute-done((bf16[128,1024]{1,0:T(8,128)(2,1)S(1)}, bf16[128,1024]{1,0:T(8,128)(2,1)S(1)}, u32[]{:S(2)}, u32[]{:S(2)}) %collective-permute-start.7) | collective-permute-done | bytes 262176 | tf_op jit(solution)/shard_map/ppermute | solution.py:319
  64.4 4.8 %collective-permute-done.12.own_ref = bf16[128,1024]{1,0:T(8,128)(2,1)S(1)} collective-permute-done((bf16[128,1024]{1,0:T(8,128)(2,1)S(1)}, bf16[128,1024]{1,0:T(8,128)(2,1)S(1)}, u32[]{:S(2)}, u32[]{:S(2)}) %collective-permute-start.12) | collective-permute-done | bytes 262176 | tf_op jit(solution)/shard_map/ppermute | solution.py:319
  69.2 0.7 shard_map.64
  70.0 3.6 %collective-permute-start.13 = (bf16[128,1024]{1,0:T(8,128)(2,1)S(1)}, bf16[128,1024]{1,0:T(8,128)(2,1)S(1)}, u32[]{:S(2)}, u32[]{:S(2)}) collective-permute-start(bf16[128,1024]{1,0:T(8,128)(2,1)S(1)} %shard_map.64), channel_id=1, source_target_pairs={{0,2},{1,3},{2,0},{3,1},{4,6},{5,7},{6,4},{7,5},{8,10},{9,11},{10,... | collective-permute-start | bytes 786440 | tf_op jit(solution)/shard_map/ppermute | solution.py:319
  73.6 0.8 collective-permute-done.6.own_ref
  74.4 2.3 %collective-permute-done.8.mate_ref = bf16[128,1024]{1,0:T(8,128)(2,1)S(1)} collective-permute-done((bf16[128,1024]{1,0:T(8,128)(2,1)S(1)}, bf16[128,1024]{1,0:T(8,128)(2,1)S(1)}, u32[]{:S(2)}, u32[]{:S(2)}) %collective-permute-start.8) | collective-permute-done | bytes 262176 | tf_op jit(solution)/shard_map/ppermute | solution.py:319
  76.7 3.3 %collective-permute-done.13.refs_4_ = bf16[128,1024]{1,0:T(8,128)(2,1)S(1)} collective-permute-done((bf16[128,1024]{1,0:T(8,128)(2,1)S(1)}, bf16[128,1024]{1,0:T(8,128)(2,1)S(1)}, u32[]{:S(2)}, u32[]{:S(2)}) %collective-permute-start.13) | collective-permute-done | bytes 262176 | tf_op jit(solution)/shard_map/ppermute | solution.py:319
  80.1 0.8 shard_map.65
  80.8 4.9 %collective-permute-start.14 = (bf16[128,1024]{1,0:T(8,128)(2,1)S(1)}, bf16[128,1024]{1,0:T(8,128)(2,1)S(1)}, u32[]{:S(2)}, u32[]{:S(2)}) collective-permute-start(bf16[128,1024]{1,0:T(8,128)(2,1)S(1)} %shard_map.65), channel_id=1, source_target_pairs={{0,0},{1,16},{2,8},{3,24},{4,4},{5,20},{6,12},{7,28},{8,9},{9,25},... | collective-permute-start | bytes 786440 | tf_op jit(solution)/shard_map/ppermute | solution.py:319
  85.8 5.4 %collective-permute-done.14 = bf16[128,1024]{1,0:T(8,128)(2,1)S(1)} collective-permute-done((bf16[128,1024]{1,0:T(8,128)(2,1)S(1)}, bf16[128,1024]{1,0:T(8,128)(2,1)S(1)}, u32[]{:S(2)}, u32[]{:S(2)}) %collective-permute-start.14) | collective-permute-done | bytes 262176 | tf_op jit(solution)/shard_map/ppermute | solution.py:319
  91.2 0.7 copy.9
  (17 shorter events, 0.0 us)
Async XLA Ops:
  0.0 27.2 %copy-start.3 = (bf16[128,256]{1,0:T(8,128)(2,1)S(1)}, bf16[128,256]{1,0:T(8,128)(2,1)}, u32[]{:S(2)}) copy-start(bf16[128,256]{1,0:T(8,128)(2,1)} %v_ref.1) | copy-start | bytes 196612
  0.0 25.1 %collective-permute-start.9 = (bf16[1024,512]{1,0:T(8,128)(2,1)}, bf16[1024,512]{1,0:T(8,128)(2,1)S(1)}, u32[]{:S(2)}, u32[]{:S(2)}) collective-permute-start(bf16[1024,512]{1,0:T(8,128)(2,1)} %refs_0_.3), channel_id=1, source_target_pairs={{0,4},{1,5},{2,6},{3,7},{4,0},{5,1},{6,2},{7,3},{8,12},{9,13},{10,... | collective-permute-start | bytes 3145736 | tf_op jit(solution)/shard_map/ppermute | solution.py:319
  2.0 67.2 %collective-permute-start.10 = (bf16[1024,512]{1,0:T(8,128)(2,1)}, bf16[1024,512]{1,0:T(8,128)(2,1)S(1)}, u32[]{:S(2)}, u32[]{:S(2)}) collective-permute-start(bf16[1024,512]{1,0:T(8,128)(2,1)} %refs_0_.3), channel_id=1, source_target_pairs={{0,1},{1,0},{2,3},{3,2},{4,5},{5,4},{6,7},{7,6},{8,9},{9,8},{10,11... | collective-permute-start | bytes 3145736 | tf_op jit(solution)/shard_map/ppermute | solution.py:319
  25.1 44.1 %collective-permute-start.11 = (bf16[1024,512]{1,0:T(8,128)(2,1)S(1)}, bf16[1024,512]{1,0:T(8,128)(2,1)S(1)}, u32[]{:S(2)}, u32[]{:S(2)}) collective-permute-start(bf16[1024,512]{1,0:T(8,128)(2,1)S(1)} %collective-permute-done.9.refs_1_), channel_id=1, source_target_pairs={{0,1},{1,0},{2,3},{3,2},{4,5},{5,4},{6,7},{7,6},{8,9},{9,8},{10,11... | collective-permute-start | bytes 3145736 | tf_op jit(solution)/shard_map/ppermute | solution.py:319
  27.2 16.8 %copy-start.2 = (bf16[128,256]{1,0:T(8,128)(2,1)S(1)}, bf16[128,256]{1,0:T(8,128)(2,1)}, u32[]{:S(2)}) copy-start(bf16[128,256]{1,0:T(8,128)(2,1)} %k_ref.1) | copy-start | bytes 196612
  27.2 16.8 %copy-start.4 = (s32[6]{0:T(128)S(1)}, s32[6]{0:T(128)}, u32[]{:S(2)}) copy-start(s32[6]{0:T(128)} %lengths_ref.3) | copy-start | bytes 76
  27.2 16.8 %copy-start.5 = (f32[1,128]{1,0:T(1,128)S(1)}, f32[1,128]{1,0:T(1,128)}, u32[]{:S(2)}) copy-start(f32[1,128]{1,0:T(1,128)} %constant.2.clone.freq_ref) | copy-start | bytes 1540
  27.2 11.0 %collective-permute-start.1 = (bf16[128,512]{1,0:T(8,128)(2,1)S(1)}, bf16[128,512]{1,0:T(8,128)(2,1)S(1)}, u32[]{:S(2)}, u32[]{:S(2)}) collective-permute-start(bf16[128,512]{1,0:T(8,128)(2,1)S(1)} %constant_dynamic-update-slice_fusion), channel_id=1, source_target_pairs={{0,16},{4,20},{8,24},{12,28},{1,17},{5,21},{9,25},{13,29},{2,18},{... | collective-permute-start | bytes 393224 | tf_op jit(solution)/shard_map/ppermute | solution.py:161
  31.9 10.1 %collective-permute-start = (bf16[128,512]{1,0:T(8,128)(2,1)S(1)}, bf16[128,512]{1,0:T(8,128)(2,1)S(1)}, u32[]{:S(2)}, u32[]{:S(2)}) collective-permute-start(bf16[128,512]{1,0:T(8,128)(2,1)S(1)} %constant_dynamic-update-slice_fusion), channel_id=1, source_target_pairs={{0,4},{4,8},{8,12},{12,16},{16,20},{20,24},{24,28},{1,5},{5,9},{9,... | collective-permute-start | bytes 393224 | tf_op jit(solution)/shard_map/ppermute | solution.py:161
  35.0 8.3 %collective-permute-start.3 = (bf16[128,512]{1,0:T(8,128)(2,1)S(1)}, bf16[128,512]{1,0:T(8,128)(2,1)S(1)}, u32[]{:S(2)}, u32[]{:S(2)}) collective-permute-start(bf16[128,512]{1,0:T(8,128)(2,1)S(1)} %constant_dynamic-update-slice_fusion), channel_id=1, source_target_pairs={{0,8},{4,12},{16,24},{20,28},{1,9},{5,13},{17,25},{21,29},{2,10},{... | collective-permute-start | bytes 393224 | tf_op jit(solution)/shard_map/ppermute | solution.py:161
  38.2 8.2 %collective-permute-start.4 = (bf16[128,512]{1,0:T(8,128)(2,1)S(1)}, bf16[128,512]{1,0:T(8,128)(2,1)S(1)}, u32[]{:S(2)}, u32[]{:S(2)}) collective-permute-start(bf16[128,512]{1,0:T(8,128)(2,1)S(1)} %constant_dynamic-update-slice_fusion), channel_id=1, source_target_pairs={{0,12},{4,16},{8,20},{12,24},{16,28},{1,13},{5,17},{9,21},{13,25},... | collective-permute-start | bytes 393224 | tf_op jit(solution)/shard_map/ppermute | solution.py:161
  42.0 5.2 %collective-permute-start.5 = (bf16[128,512]{1,0:T(8,128)(2,1)S(1)}, bf16[128,512]{1,0:T(8,128)(2,1)S(1)}, u32[]{:S(2)}, u32[]{:S(2)}) collective-permute-start(bf16[128,512]{1,0:T(8,128)(2,1)S(1)} %constant_dynamic-update-slice_fusion), channel_id=1, source_target_pairs={{0,20},{4,24},{8,28},{1,21},{5,25},{9,29},{2,22},{6,26},{10,30},{3... | collective-permute-start | bytes 393224 | tf_op jit(solution)/shard_map/ppermute | solution.py:161
  43.3 3.8 %collective-permute-start.2 = (bf16[128,512]{1,0:T(8,128)(2,1)S(1)}, bf16[128,512]{1,0:T(8,128)(2,1)S(1)}, u32[]{:S(2)}, u32[]{:S(2)}) collective-permute-start(bf16[128,512]{1,0:T(8,128)(2,1)S(1)} %collective-permute-done.1.refs_4_), channel_id=1, source_target_pairs={{24,16},{28,20},{25,17},{29,21},{26,18},{30,22},{27,19},{31,23}} | collective-permute-start | bytes 393224 | tf_op jit(solution)/shard_map/ppermute | solution.py:161
  44.0 1.0 %copy-start.1 = (bf16[128,1024]{1,0:T(8,128)(2,1)S(1)}, bf16[128,1024]{1,0:T(8,128)(2,1)}, u32[]{:S(2)}) copy-start(bf16[128,1024]{1,0:T(8,128)(2,1)} %q_ref.1) | copy-start | bytes 786436
  47.1 22.1 %copy-start = (bf16[1024,512]{1,0:T(8,128)(2,1)S(1)}, bf16[1024,512]{1,0:T(8,128)(2,1)}, u32[]{:S(2)}) copy-start(bf16[1024,512]{1,0:T(8,128)(2,1)} %refs_0_.3) | copy-start | bytes 3145732
  49.8 14.7 %collective-permute-start.7 = (bf16[128,1024]{1,0:T(8,128)(2,1)S(1)}, bf16[128,1024]{1,0:T(8,128)(2,1)S(1)}, u32[]{:S(2)}, u32[]{:S(2)}) collective-permute-start(bf16[128,1024]{1,0:T(8,128)(2,1)S(1)} %attention.1), channel_id=1, source_target_pairs={{0,25},{1,8},{2,19},{3,2},{4,29},{5,12},{6,23},{7,6},{8,17},{9,0},... | collective-permute-start | bytes 786440 | tf_op jit(solution)/shard_map/ppermute | solution.py:319
  54.8 14.4 %collective-permute-start.12 = (bf16[128,1024]{1,0:T(8,128)(2,1)S(1)}, bf16[128,1024]{1,0:T(8,128)(2,1)S(1)}, u32[]{:S(2)}, u32[]{:S(2)}) collective-permute-start(bf16[128,1024]{1,0:T(8,128)(2,1)S(1)} %attention.1), channel_id=1, source_target_pairs={{0,8},{1,25},{2,2},{3,19},{4,12},{5,29},{6,6},{7,23},{8,0},{9,17},... | collective-permute-start | bytes 786440 | tf_op jit(solution)/shard_map/ppermute | solution.py:319
  59.3 15.1 %collective-permute-start.6 = (bf16[128,1024]{1,0:T(8,128)(2,1)S(1)}, bf16[128,1024]{1,0:T(8,128)(2,1)S(1)}, u32[]{:S(2)}, u32[]{:S(2)}) collective-permute-start(bf16[128,1024]{1,0:T(8,128)(2,1)S(1)} %attention.1), channel_id=1, source_target_pairs={{0,0},{1,17},{2,10},{3,27},{4,4},{5,21},{6,14},{7,31},{8,8},{9,25}... | collective-permute-start | bytes 786440 | tf_op jit(solution)/shard_map/ppermute | solution.py:319
  64.4 12.3 %collective-permute-start.8 = (bf16[128,1024]{1,0:T(8,128)(2,1)S(1)}, bf16[128,1024]{1,0:T(8,128)(2,1)S(1)}, u32[]{:S(2)}, u32[]{:S(2)}) collective-permute-start(bf16[128,1024]{1,0:T(8,128)(2,1)S(1)} %collective-permute-done.7.mate_ref), channel_id=1, source_target_pairs={{0,8},{1,9},{2,10},{3,11},{4,12},{5,13},{6,14},{7,15},{8,0},{9,1},... | collective-permute-start | bytes 786440 | tf_op jit(solution)/shard_map/ppermute | solution.py:319
  70.0 10.1 %collective-permute-start.13 = (bf16[128,1024]{1,0:T(8,128)(2,1)S(1)}, bf16[128,1024]{1,0:T(8,128)(2,1)S(1)}, u32[]{:S(2)}, u32[]{:S(2)}) collective-permute-start(bf16[128,1024]{1,0:T(8,128)(2,1)S(1)} %shard_map.64), channel_id=1, source_target_pairs={{0,2},{1,3},{2,0},{3,1},{4,6},{5,7},{6,4},{7,5},{8,10},{9,11},{10,... | collective-permute-start | bytes 786440 | tf_op jit(solution)/shard_map/ppermute | solution.py:319
  80.8 10.3 %collective-permute-start.14 = (bf16[128,1024]{1,0:T(8,128)(2,1)S(1)}, bf16[128,1024]{1,0:T(8,128)(2,1)S(1)}, u32[]{:S(2)}, u32[]{:S(2)}) collective-permute-start(bf16[128,1024]{1,0:T(8,128)(2,1)S(1)} %shard_map.65), channel_id=1, source_target_pairs={{0,0},{1,16},{2,8},{3,24},{4,4},{5,20},{6,12},{7,28},{8,9},{9,25},... | collective-permute-start | bytes 786440 | tf_op jit(solution)/shard_map/ppermute | solution.py:319
